TPU v7x, 8 devices: a whole 2x2x1 slice. The times are simulated.
8 devices in a mesh: dp: 1 (over z), tp: 8 (over y, x, core).
Axes of the slice: x: 2, y: 2, z: 1, core: 2. Of those that a mesh axis runs over, the one named last changes fastest.
Arguments:
- hidden: bfloat16 [16, 64, 5120], P('dp')
- tree_mask: int32 [16, 64, 64], P('dp')
- depth: int32 [16, 64], P('dp')
- ctx_len: int32 [16], P('dp')
- block_table: int32 [16, 32], P('dp')
- score_id: int32 [16, 64], P('dp')
- k_cache: bfloat16 [512, 16, 40, 128], P('dp', None, 'tp')
- v_cache: bfloat16 [512, 16, 40, 128], P('dp', None, 'tp')
- attn_norm: bfloat16 [5120], replicated
- w_q: bfloat16 [5120, 5120], P(None, 'tp')
- w_k: bfloat16 [5120, 5120], P(None, 'tp')
- w_v: bfloat16 [5120, 5120], P(None, 'tp')
- w_o: bfloat16 [5120, 5120], P('tp')
- mlp_norm: bfloat16 [5120], replicated
- w_gate: bfloat16 [5120, 13824], P(None, 'tp')
- w_up: bfloat16 [5120, 13824], P(None, 'tp')
- w_down: bfloat16 [13824, 5120], P('tp')
- final_norm: bfloat16 [5120], replicated
- w_lm: bfloat16 [5120, 32000], P(None, 'tp')
Outputs:
- output 1: float32 [16, 64], P('dp')
- output 2: float32 [16, 64], P('dp')
- output 3: bfloat16 [512, 16, 40, 128], P('dp', None, 'tp')
- output 4: bfloat16 [512, 16, 40, 128], P('dp', None, 'tp')
All inputs are finite; a program needn't handle non-finite values.
Results may differ from a plain program's by a relative error of at most 0.00355428.
Values are sent between devices in bfloat16 or wider.
A program may use at most 1 GiB of HBM per device.

v0:
```python
import jax
import jax.numpy as jnp
from jax import lax
from jax.sharding import PartitionSpec as P

RMS_EPS = 1e-5
ROPE_THETA = 500000


def rms_norm(values, gain):
    widened = values.astype(jnp.float32)
    scale = lax.rsqrt(jnp.mean(widened * widened, axis=-1, keepdims=True) + RMS_EPS)
    return (widened * scale * gain.astype(jnp.float32)).astype(jnp.bfloat16)


def rotate(values, positions):
    head_dim = values.shape[-1]
    half = head_dim // 2
    inv_freq = 1.0 / (ROPE_THETA ** (jnp.arange(half, dtype=jnp.float32) * (2.0 / head_dim)))
    angles = positions.astype(jnp.float32)[..., None] * inv_freq
    cosine = jnp.cos(angles)[..., None, :]
    sine = jnp.sin(angles)[..., None, :]
    first = values[..., :half]
    second = values[..., half:]
    return jnp.concatenate([first * cosine - second * sine, second * cosine + first * sine], axis=-1)


def tree_attention(query, key_new, val_new, key_old, val_old, tree_mask, ctx_len):
    scale = query.shape[-1] ** -0.5
    span = key_old.shape[1]
    score_old = jnp.einsum("btkgh,bskh->btkgs", query, key_old, preferred_element_type=jnp.float32) * scale
    seen_old = jnp.arange(span)[None, :] < ctx_len[:, None]
    score_old = jnp.where(seen_old[:, None, None, None, :], score_old, -jnp.inf)
    score_new = jnp.einsum("btkgh,bjkh->btkgj", query, key_new, preferred_element_type=jnp.float32) * scale
    score_new = jnp.where((tree_mask > 0)[:, :, None, None, :], score_new, -jnp.inf)
    top = jnp.maximum(jnp.max(score_old, axis=-1), jnp.max(score_new, axis=-1))[..., None]
    prob_old = jnp.exp(score_old - top)
    prob_new = jnp.exp(score_new - top)
    total = jnp.sum(prob_old, axis=-1) + jnp.sum(prob_new, axis=-1)
    mixed = jnp.einsum("btkgs,bskh->btkgh", prob_old.astype(jnp.bfloat16), val_old, preferred_element_type=jnp.float32)
    mixed = mixed + jnp.einsum("btkgj,bjkh->btkgh", prob_new.astype(jnp.bfloat16), val_new, preferred_element_type=jnp.float32)
    return (mixed / total[..., None]).astype(jnp.bfloat16)


def write_cache(cache, table, ctx_len, new_rows):
    page_size = cache.shape[1]
    slots = ctx_len[:, None] + jnp.arange(new_rows.shape[1])[None, :]
    slot_blocks = jnp.take_along_axis(table, slots // page_size, axis=1)
    return cache.at[slot_blocks, slots % page_size].set(new_rows)


def layer_and_logits(hidden, tree_mask, depth, ctx_len, block_table, k_cache, v_cache, attn_norm, w_q, w_k, w_v, w_o, mlp_norm, w_gate, w_up, w_down, final_norm, w_lm):
    requests = hidden.shape[0]
    nodes = hidden.shape[1]
    page_size = k_cache.shape[1]
    kv_local = k_cache.shape[2]
    head_dim = k_cache.shape[3]
    span = block_table.shape[1] * page_size
    heads_local = w_q.shape[1] // head_dim
    normed = rms_norm(hidden, attn_norm)
    positions = ctx_len[:, None] + depth
    query = jnp.dot(normed, w_q, preferred_element_type=jnp.float32).reshape(requests, nodes, heads_local, head_dim)
    query = rotate(query, positions).astype(jnp.bfloat16).reshape(requests, nodes, kv_local, heads_local // kv_local, head_dim)
    key_new = jnp.dot(normed, w_k, preferred_element_type=jnp.float32).reshape(requests, nodes, kv_local, head_dim)
    key_new = rotate(key_new, positions).astype(jnp.bfloat16)
    val_new = jnp.dot(normed, w_v, preferred_element_type=jnp.float32).astype(jnp.bfloat16).reshape(requests, nodes, kv_local, head_dim)
    key_old = k_cache[block_table].reshape(requests, span, kv_local, head_dim)
    val_old = v_cache[block_table].reshape(requests, span, kv_local, head_dim)
    attended = tree_attention(query, key_new, val_new, key_old, val_old, tree_mask, ctx_len).reshape(requests, nodes, heads_local * head_dim)
    attn_sum = lax.psum(jnp.dot(attended, w_o, preferred_element_type=jnp.float32).astype(jnp.bfloat16), "tp")
    residual = (hidden.astype(jnp.float32) + attn_sum.astype(jnp.float32)).astype(jnp.bfloat16)
    normed_mlp = rms_norm(residual, mlp_norm)
    gate = jnp.dot(normed_mlp, w_gate, preferred_element_type=jnp.float32)
    upper = jnp.dot(normed_mlp, w_up, preferred_element_type=jnp.float32)
    product = (jax.nn.silu(gate) * upper).astype(jnp.bfloat16)
    mlp_sum = lax.psum(jnp.dot(product, w_down, preferred_element_type=jnp.float32).astype(jnp.bfloat16), "tp")
    layer_out = (residual.astype(jnp.float32) + mlp_sum.astype(jnp.float32)).astype(jnp.bfloat16)
    logits = jnp.dot(rms_norm(layer_out, final_norm), w_lm, preferred_element_type=jnp.float32)
    return logits, key_new, val_new


def solution(mesh):
    def group_step(hidden, tree_mask, depth, ctx_len, block_table, score_id, k_cache, v_cache, attn_norm, w_q, w_k, w_v, w_o, mlp_norm, w_gate, w_up, w_down, final_norm, w_lm):
        logits, key_new, val_new = layer_and_logits(hidden, tree_mask, depth, ctx_len, block_table, k_cache, v_cache, attn_norm, w_q, w_k, w_v, w_o, mlp_norm, w_gate, w_up, w_down, final_norm, w_lm)
        vocab_local = logits.shape[-1]
        global_top = lax.pmax(jnp.max(logits, axis=-1), "tp")
        part_sum = jnp.sum(jnp.exp(logits - global_top[..., None]), axis=-1)
        local_id = score_id - lax.axis_index("tp") * vocab_local
        inside = (local_id >= 0) & (local_id < vocab_local)
        picked = jnp.take_along_axis(logits, jnp.clip(local_id, 0, vocab_local - 1)[..., None], axis=-1)[..., 0]
        summed = lax.psum(jnp.stack([part_sum, jnp.where(inside, picked, 0.0)]), "tp")
        log_norm = global_top + jnp.log(summed[0])
        log_prob = summed[1] - log_norm
        return log_norm, log_prob, write_cache(k_cache, block_table, ctx_len, key_new), write_cache(v_cache, block_table, ctx_len, val_new)

    request_spec = P("dp", None, None)
    node_spec = P("dp", None)
    cache_spec = P("dp", None, "tp", None)
    shared_spec = P(None)
    column_spec = P(None, "tp")
    row_spec = P("tp", None)
    in_specs = (request_spec, request_spec, node_spec, P("dp"), node_spec, node_spec, cache_spec, cache_spec, shared_spec, column_spec, column_spec, column_spec, row_spec, shared_spec, column_spec, column_spec, row_spec, shared_spec, column_spec)
    out_specs = (node_spec, node_spec, cache_spec, cache_spec)
    return jax.shard_map(group_step, mesh=mesh, in_specs=in_specs, out_specs=out_specs, check_vma=False)
```

profile of v0, /device:TPU:0, one launch (start us, length us, event | category | flops | bytes accessed | tf_op | source)
XLA Modules:
  0.0 851.3 jit_solution(4571157928766276386)
XLA Ops:
  7.2 0.7 iota_compare_fusion
  8.0 1.4 bitcast_or_fusion
  9.4 0.7 compare_select_fusion.4
  10.1 0.1 reshape.271
  10.2 6.1 fusion.5
  16.3 0.1 reshape.320
  16.4 7.6 gather_fusion.3
  24.0 0.1 reshape.323
  24.1 0.1 broadcast_compare_fusion
  24.2 0.3 copy.49
  24.5 14.1 %fusion.59 = bf16[16,64,640]{2,1,0:T(8,128)(2,1)} fusion(bf16[5120,640]{1,0:T(8,128)(2,1)} %param.32, bf16[16,64,5120]{2,1,0:T(8,128)(2,1)} %param.21, f32[5120]{0:T(1024)S(1)} %convert_element_type.72, f32[16,64]{1,0:T(8,128)S(1)} %add_rsqrt_fusion.2), kind=kOutput, calls=%fused_computation.72 | convolution fusion | flops 6732513280 | bytes 18374656 | tf_op jit(solution)/shard_map/dot_general | solution.py:66
  38.5 11.4 %fusion.37 = f32[16,64,640]{2,1,0:T(8,128)} fusion(bf16[5120,640]{1,0:T(8,128)(2,1)} %param.31, bf16[16,64,5120]{2,1,0:T(8,128)(2,1)S(1)} %bitcast.131, f32[5120]{0:T(1024)S(1)} %convert_element_type.72, f32[16,64]{1,0:T(8,128)S(1)} %add_rsqrt_fusion.2), kind=kOutput, calls=%fused_computation.52 | convolution fusion | flops 6731857920 | bytes 19685376 | tf_op jit(solution)/shard_map/dot_general | solution.py:64
  49.9 4.4 reshape.249
  54.3 13.1 %fusion.39 = f32[16,64,640]{2,1,0:T(8,128)S(1)} fusion(bf16[5120,640]{1,0:T(8,128)(2,1)} %param.30, bf16[16,64,5120]{2,1,0:T(8,128)(2,1)} %param.21, f32[5120]{0:T(1024)S(1)} %convert_element_type.72, f32[16,64]{1,0:T(8,128)S(1)} %add_rsqrt_fusion.2), kind=kOutput, calls=%fused_computation.54 | convolution fusion | flops 6731857920 | bytes 19685376 | tf_op jit(solution)/shard_map/dot_general | solution.py:62
  67.4 2.2 reshape.248
  69.6 18.9 %gather_fusion = bf16[512,16,5,128]{3,1,2,0:T(8,128)(2,1)} fusion(bf16[512,16,5,128]{3,1,2,0:T(8,128)(2,1)} %param.28, s32[1024]{0:T(1024)S(1)} %pad_clamp_fusion), kind=kCustom, calls=%fused_computation.1 | custom fusion | bytes 20973568 | tf_op jit(solution)/shard_map/gather | solution.py:68
  88.5 9.9 %copy.44 = bf16[512,16,5,128]{3,1,0,2:T(8,128)(2,1)} copy(bf16[512,16,5,128]{3,1,2,0:T(8,128)(2,1)} %gather_fusion) | data formatting | bytes 20971520 | tf_op jit(solution)/shard_map/gather | solution.py:68
  98.4 18.9 %gather_fusion.1 = bf16[512,16,5,128]{3,1,2,0:T(8,128)(2,1)} fusion(bf16[512,16,5,128]{3,1,2,0:T(8,128)(2,1)} %param.27, s32[1024]{0:T(1024)S(1)} %pad_clamp_fusion), kind=kCustom, calls=%fused_computation.2 | custom fusion | bytes 20973568 | tf_op jit(solution)/shard_map/gather | solution.py:67
  117.3 9.8 %copy.45 = bf16[512,16,5,128]{3,1,0,2:T(8,128)(2,1)} copy(bf16[512,16,5,128]{3,1,2,0:T(8,128)(2,1)} %gather_fusion.1) | data formatting | bytes 20971520 | tf_op jit(solution)/shard_map/gather | solution.py:67
  127.0 0.7 fusion.75
  127.7 1.9 multiply_cosine_fusion
  129.6 8.8 %fusion.98 = (f32[16,64,5,64]{3,2,1,0:T(8,128)S(1)}, f32[16,64,5,64]{3,2,1,0:T(8,128)S(1)}, f32[16,64,5,64]{3,2,1,0:T(8,128)S(1)}, f32[16,64,5,64]{3,2,1,0:T(8,128)S(1)}) fusion(f32[16,64,5,128]{3,2,1,0:T(8,128)} %reshape.249, f32[16,64,5,128]{3,2,1,0:T(8,128)} %reshape.248), kind=kLoop, calls=%fused_computation.143 | loop fusion | bytes 10485760 | tf_op jit(solution)/shard_map/slice | solution.py:23
  138.4 2.7 subtract_convert_fusion
  141.1 0.7 pad_maximum_fusion.1
  141.8 1.2 copy-done.2
  143.0 1.4 fusion.58
  144.4 12.7 %bitcast_reduce_fusion = (f32[16,64,5]{1,2,0:T(8,128)S(1)}, f32[16,5,512,64]{2,3,1,0:T(8,128)}) fusion(pred[16,512]{1,0:T(8,128)(4,1)S(1)} %iota_compare_fusion, bf16[16,64,5,64]{3,1,2,0:T(8,128)(2,1)} %copy-done.4, bf16[16,64,5,64]{3,1,2,0:T(8,128)(2,1)} %copy-done.5, bf16[16,512,5,128]{3,1,0,2:T(8,128)(2,1)} %bitcast.135), kind=kOutput, calls=%fused_computation.35 | convolution fusion | flops 681569280 | bytes 22310912 | tf_op jit(solution)/shard_map/btkgh,bskh->btkgs/dot_general | solution.py:31
  157.2 5.8 fusion.30
  163.0 10.8 %fusion.21 = f32[16,5,128,64]{2,3,1,0:T(8,128)} fusion(bf16[16,512,5,128]{3,1,0,2:T(8,128)(2,1)} %bitcast.134, f32[16,5,512,64]{2,3,1,0:T(8,128)} %get-tuple-element.34, f32[16,64,5]{1,2,0:T(8,128)S(1)} %max.15, pred[16,512]{1,0:T(8,128)(4,1)S(1)} %iota_compare_fusion), kind=kOutput, calls=%fused_computation.38 | convolution fusion | flops 681574400 | bytes 23621632 | tf_op jit(solution)/shard_map/btkgs,bskh->btkgh/dot_general | solution.py:40
  173.8 0.8 fusion.56
  174.7 3.6 fusion.55
  178.2 1.1 copy.55
  179.3 1.6 reshape.253
  180.9 13.8 %convolution_convert_fusion = bf16[16,64,5120]{2,1,0:T(8,128)(2,1)} fusion(bf16[16,64,640]{2,1,0:T(8,128)(2,1)S(1)} %reshape.253, bf16[640,5120]{1,0:T(8,128)(2,1)} %param.33), kind=kOutput, calls=%fused_computation.45 | convolution fusion | flops 6716129280 | bytes 18350080 | tf_op jit(solution)/shard_map/dot_general | solution.py:70
  194.8 0.6 copy-done.11
  195.4 139.8 %all-reduce.3.cloned.1.call-done = bf16[16,64,5120]{2,1,0:T(8,128)(2,1)} async-done(((bf16[16,64,5120]{2,1,0:T(8,128)(2,1)}), bf16[16,64,5120]{2,1,0:T(8,128)(2,1)}) %all-reduce.3.cloned.1.call-update) | async-done | bytes 10485776 | tf_op jit(solution)/shard_map/psum | solution.py:70
  335.2 9.5 %fusion.9 = (f32[16,64]{1,0:T(8,128)S(1)}, bf16[16,64,5120]{2,1,0:T(8,128)(2,1)S(1)}) fusion(bf16[16,64,5120]{2,1,0:T(8,128)(2,1)} %all-reduce.3.cloned.1.call-done, bf16[16,64,5120]{2,1,0:T(8,128)(2,1)} %param.21), kind=kLoop, calls=%fused_computation.23 | loop fusion | flops 36699136 | bytes 31461376 | tf_op jit(solution)/shard_map/reduce_sum | solution.py:12
  344.8 4.0 copy-done.1
  348.8 24.6 %fusion.17 = f32[16,64,1728]{2,1,0:T(8,128)} fusion(bf16[5120,1728]{0,1:T(8,128)(2,1)} %param.35, bf16[16,64,5120]{2,1,0:T(8,128)(2,1)S(1)} %get-tuple-element.16, f32[5120]{0:T(1024)S(1)} %convert_element_type.83, f32[16,64]{1,0:T(8,128)S(1)} %add_rsqrt_fusion.1), kind=kOutput, calls=%fused_computation.31 | convolution fusion | flops 18140364800 | bytes 35282944 | tf_op jit(solution)/shard_map/dot_general | solution.py:73
  373.4 30.4 %multiply_convert_fusion = bf16[16,64,1728]{2,1,0:T(8,128)(2,1)} fusion(f32[16,64,1728]{2,1,0:T(8,128)} %fusion.17, bf16[5120,1728]{0,1:T(8,128)(2,1)} %param.36, bf16[16,64,5120]{2,1,0:T(8,128)(2,1)} %copy-done.1, f32[5120]{0:T(1024)S(1)} %convert_element_type.83, f32[16,64]{1,0:T(8,128)S(1)} %add_rsqrt_fusion.1), kind=kOutput, calls=%fused_computation.48 | convolution fusion | flops 18150981632 | bytes 38821888 | tf_op jit(solution)/shard_map/dot_general | solution.py:74
  403.8 24.8 %fusion.27 = bf16[16,64,5120]{2,1,0:T(8,128)(2,1)} fusion(bf16[16,64,1728]{2,1,0:T(8,128)(2,1)} %multiply_convert_fusion, bf16[1728,5120]{1,0:T(8,128)(2,1)} %param.37), kind=kOutput, calls=%fused_computation.44 | convolution fusion | flops 18124636160 | bytes 31719424 | tf_op jit(solution)/shard_map/dot_general | solution.py:76
  428.6 3.2 reshape.301
  431.8 1.2 copy.57
  433.0 9.9 %copy.56 = bf16[512,16,5,128]{3,1,0,2:T(8,128)(2,1)} copy(bf16[512,16,5,128]{3,1,2,0:T(8,128)(2,1)} %param.27) | data formatting | bytes 20971520 | tf_op args[6]
  442.9 9.7 %copy.61 = bf16[512,16,5,128]{3,1,0,2:T(8,128)(2,1)} copy(bf16[512,16,5,128]{3,1,2,0:T(8,128)(2,1)} %param.28) | data formatting | bytes 20971520 | tf_op args[7]
  452.6 0.1 reshape.287
  452.7 0.1 multiply_reduce_fusion
  452.8 0.1 and_reduce_fusion
  452.9 0.1 reshape.293
  452.9 3.6 copy.59
  456.5 15.3 %copy.58 = bf16[8192,5,128]{2,1,0:T(8,128)(2,1)} copy(bf16[8192,5,128]{2,0,1:T(8,128)(2,1)} %bitcast.133) | data formatting | bytes 20971520
  471.8 100.0 %scatter_fusion = bf16[8192,5,128]{2,1,0:T(8,128)(2,1)} fusion(bf16[8192,5,128]{2,1,0:T(8,128)(2,1)} %copy.58, s32[1024]{0:T(1024)S(1)} %reshape.293, bf16[1024,5,128]{2,1,0:T(8,128)(2,1)} %copy.59), kind=kCustom, calls=%fused_computation.4 | custom fusion | bytes 3936256
  571.9 12.4 %copy.64 = bf16[512,16,5,128]{3,1,2,0:T(8,128)(2,1)} copy(bf16[512,16,5,128]{3,2,1,0:T(8,128)(2,1)} %bitcast.129) | data formatting | bytes 20971520
  584.3 15.5 %copy.62 = bf16[8192,5,128]{2,1,0:T(8,128)(2,1)} copy(bf16[8192,5,128]{2,0,1:T(8,128)(2,1)} %bitcast.132) | data formatting | bytes 20971520
  599.8 94.5 %scatter_fusion.1 = bf16[8192,5,128]{2,1,0:T(8,128)(2,1)} fusion(bf16[8192,5,128]{2,1,0:T(8,128)(2,1)} %copy.62, s32[1024]{0:T(1024)S(1)} %reshape.293, bf16[1024,5,128]{2,1,0:T(8,128)(2,1)S(1)} %reshape.301), kind=kCustom, calls=%fused_computation.5 | custom fusion | bytes 3936256
  694.3 12.4 %copy.65 = bf16[512,16,5,128]{3,1,2,0:T(8,128)(2,1)} copy(bf16[512,16,5,128]{3,2,1,0:T(8,128)(2,1)} %bitcast.128) | data formatting | bytes 20971520
  706.8 9.2 %fusion.2 = f32[16,64]{1,0:T(8,128)S(1)} fusion(bf16[16,64,5120]{2,1,0:T(8,128)(2,1)} %all-reduce.5.cloned.1.call-done, bf16[16,64,5120]{2,1,0:T(8,128)(2,1)} %copy-done.1), kind=kLoop, calls=%fused_computation.16 | loop fusion | flops 36699136 | bytes 20975616 | tf_op jit(solution)/shard_map/reduce_sum | solution.py:12
  716.0 55.5 %fusion.100 = (f32[16,64]{1,0:T(8,128)S(1)}, f32[16,64,4000]{2,1,0:T(8,128)}) fusion(bf16[5120,4000]{0,1:T(8,128)(2,1)} %param.39, f32[5120]{0:T(1024)S(1)} %convert_element_type.90, f32[16,64]{1,0:T(8,128)S(1)} %add_rsqrt_fusion, bf16[16,64,5120]{2,1,0:T(8,128)(2,1)} %all-reduce.5.cloned.1.call-done, bf16[16,64,5120]{2,1,0:T(8,128)(2,1)} %copy-done.1), kind=kOutput, calls=%fused_computation.145 | convolution fusion | flops 41989079040 | bytes 78344192 | tf_op jit(solution)/shard_map/dot_general | solution.py:78
  771.5 22.7 %pmax.7 = f32[16,64]{1,0:T(8,128)S(1)} all-reduce(f32[16,64]{1,0:T(8,128)S(1)} %get-tuple-element.37), channel_id=1, replica_groups=mesh['dp'=1,'tp'=8] {'tp'}, use_global_device_ids=true, to_apply=%region_10.11 | all-reduce | flops 1024 | bytes 8192 | tf_op jit(solution)/shard_map/pmax | solution.py:86
  794.2 16.5 %gather_fusion.2 = f32[1024]{0:T(1024)S(1)} fusion(f32[16,64,4000]{2,1,0:T(8,128)} %get-tuple-element.38, s32[1024]{0:T(1024)S(1)} %reshape.287), kind=kCustom, calls=%fused_computation.3 | custom fusion | bytes 20480 | tf_op jit(solution)/shard_map/jit(take_along_axis)/gather | solution.py:90
  810.7 8.1 exponential_reduce_fusion
  818.8 0.1 gather.18
  818.9 24.4 %psum.23 = f32[2,16,64]{2,1,0:T(8,128)S(1)} all-reduce(f32[2,16,64]{2,1,0:T(8,128)S(1)} %pad_maximum_fusion.4), channel_id=1, replica_groups=mesh['dp'=1,'tp'=8] {'tp'}, use_global_device_ids=true, to_apply=%region_12.13 | all-reduce | flops 2048 | bytes 16384 | tf_op jit(solution)/shard_map/psum | solution.py:91
  843.3 0.6 fusion.76
  (61 shorter events, 0.3 us)
Async XLA Ops:
  7.2 9.2 %copy-start = (s32[16,32]{1,0:T(8,128)S(1)}, s32[16,32]{1,0:T(8,128)}, u32[]{:S(2)}) copy-start(s32[16,32]{1,0:T(8,128)} %param.25) | copy-start | bytes 6148
  7.2 328.1 %all-reduce.3.cloned.1.call-start = ((), (), s32[]{:S(2)}) async-start(), calls=%async_computation | async-start | bytes 20971520 | tf_op jit(solution)/shard_map/psum | solution.py:70
  10.2 13.9 %copy-start.10 = (bf16[5120]{0:T(1024)(128)(2,1)S(1)}, bf16[5120]{0:T(1024)(128)(2,1)}, u32[]{:S(2)}) copy-start(bf16[5120]{0:T(1024)(128)(2,1)} %param.29) | copy-start | bytes 30724
  10.2 13.9 %copy-start.6 = (s32[16,64,64]{2,1,0:T(8,128)S(1)}, s32[16,64,64]{2,1,0:T(8,128)}, u32[]{:S(2)}) copy-start(s32[16,64,64]{2,1,0:T(8,128)} %param.22) | copy-start | bytes 786436
  24.1 14.5 %slice-start = ((s8[10485760]{0:T(1024)(128)(4,1)}), s8[2097152]{0:T(1024)(128)(4,1)S(1)}, s32[]{:S(2)}) async-start(s8[10485760]{0:T(1024)(128)(4,1)} %bitcast.130), calls=%async_computation.2 | async-start | bytes 4194304
  24.4 14.1 %slice-start.1 = ((s8[10485760]{0:T(1024)(128)(4,1)}), s8[4194304]{0:T(1024)(128)(4,1)S(1)}, s32[]{:S(2)}) async-start(s8[10485760]{0:T(1024)(128)(4,1)} %bitcast.130), calls=%async_computation.3 | async-start | bytes 8388608
  24.4 14.1 %slice-start.2 = ((s8[10485760]{0:T(1024)(128)(4,1)}), s8[4194304]{0:T(1024)(128)(4,1)S(1)}, s32[]{:S(2)}) async-start(s8[10485760]{0:T(1024)(128)(4,1)} %bitcast.130), calls=%async_computation.4 | async-start | bytes 8388608
  117.2 9.8 %copy-start.13 = (s32[16]{0:T(128)S(1)}, s32[16]{0:T(128)}, u32[]{:S(2)}) copy-start(s32[16]{0:T(128)} %param.24) | copy-start | bytes 196
  117.3 9.8 %copy-start.14 = (s32[16,64]{1,0:T(8,128)S(1)}, s32[16,64]{1,0:T(8,128)}, u32[]{:S(2)}) copy-start(s32[16,64]{1,0:T(8,128)} %param.23) | copy-start | bytes 12292
  141.1 3.3 copy-start.4
  141.1 3.3 copy-start.5
  141.8 1.2 copy-start.2
  194.7 0.7 copy-start.11
  194.7 512.0 %all-reduce.5.cloned.1.call-start = ((), (), s32[]{:S(2)}) async-start(), calls=%async_computation.1 | async-start | bytes 20971520 | tf_op jit(solution)/shard_map/psum | solution.py:76
  344.8 4.0 copy-start.1
  428.6 3.2 copy-start.3
  442.8 9.7 %copy-start.9 = (s32[16,64]{1,0:T(8,128)S(1)}, s32[16,64]{1,0:T(8,128)}, u32[]{:S(2)}) copy-start(s32[16,64]{1,0:T(8,128)} %param.26) | copy-start | bytes 12292
  442.9 9.8 %copy-start.7 = (s32[16,64,1]{1,0,2:T(8,128)S(1)}, s32[16,64,1]{1,0,2:T(8,128)}, u32[]{:S(2)}) copy-start(s32[16,64,1]{1,0,2:T(8,128)} %get-tuple-element.32) | copy-start | bytes 12292
  442.9 9.8 %copy-start.8 = (s32[16,64,1]{1,0,2:T(8,128)S(1)}, s32[16,64,1]{1,0,2:T(8,128)}, u32[]{:S(2)}) copy-start(s32[16,64,1]{1,0,2:T(8,128)} %get-tuple-element.29) | copy-start | bytes 12292
  442.9 9.8 %copy-start.16 = (s32[2]{0:T(128)S(1)}, s32[2]{0:T(128)}, u32[]{:S(2)}) copy-start(s32[2]{0:T(128)} %constant.97) | copy-start | bytes 28
  442.9 9.9 %copy-start.15 = (s32[2]{0:T(128)S(1)}, s32[2]{0:T(128)}, u32[]{:S(2)}) copy-start(s32[2]{0:T(128)} %constant.100) | copy-start | bytes 28
  442.9 10.1 %copy-start.12 = (bf16[5120]{0:T(1024)(128)(2,1)S(1)}, bf16[5120]{0:T(1024)(128)(2,1)}, u32[]{:S(2)}) copy-start(bf16[5120]{0:T(1024)(128)(2,1)} %param.38) | copy-start | bytes 30724
Sparse Core Ops, SparseCore 0:
  194.9 140.3 all-reduce.2
  428.7 137.6 all-reduce.4
where the time goes:
time: 862 us; the launch traced here: 851 us
  local copies, waits for them, and re-layouts  384 us (45%)
  matrix products  216 us (25%)
  waiting for transfers between devices  140 us (16%)
  other arithmetic  49.4 us (6%)
  blocking collectives  47 us (5%)
  between operations  14.9 us (2%)
    unnamed x51, local copies, waits for them, and re-layouts  276 us
    psum x1, waiting for transfers between devices, layer_and_logits(): lax.psum(jnp.dot(attended, w_o, preferred_element_type=jnp.float32).astyp...  140 us
    dot_general x1, matrix products, layer_and_logits(): jnp.dot(rms_norm(layer_out, final_norm), w_lm, preferred_element_type=jnp...  55.5 us
    dot_general x1, matrix products, layer_and_logits(): upper = jnp.dot(normed_mlp, w_up, preferred_element_type=jnp.float32)  30.4 us
    gather x2, local copies, waits for them, and re-layouts, layer_and_logits(): val_old = v_cache[block_table].reshape(requests, span, kv_local, head_dim)  28.7 us
    gather x2, local copies, waits for them, and re-layouts, layer_and_logits(): key_old = k_cache[block_table].reshape(requests, span, kv_local, head_dim)  28.6 us
    reduce_sum x3, other arithmetic, rms_norm(): jnp.mean(widened * widened, axis=-1, keepdims=True) + RMS_EPS  24.9 us
    dot_general x1, matrix products, layer_and_logits(): jnp.dot(product, w_down, preferred_element_type=jnp.float32)  24.8 us
  transfers between devices with their start and end apart: 2, of which 1 were waited for; matrix products, arithmetic and copies ran while one was open for 33% of the time, Pallas kernels for 0%

commit v1 on v0

v1 whole, which is shorter than its diff:
```python
import functools

import jax
import jax.numpy as jnp
from jax import lax
from jax.experimental import pallas as pl
from jax.experimental.pallas import tpu as pltpu
from jax.sharding import PartitionSpec as P

RMS_EPS = 1e-5
ROPE_THETA = 500000
MESH = pl.DeviceIdType.MESH
NT_DIMS = (((1,), (1,)), ((), ()))
VMEM_MAX = 67043328


def dot_nt(left, right):
    return lax.dot_general(left, right, NT_DIMS, preferred_element_type=jnp.float32)


def qkv_kernel(hid_ref, gain_ref, cos_ref, sin_ref, wq_ref, wk_ref, wv_ref, q_ref, k_ref, v_ref):
    requests, heads, nodes, head_dim = q_ref.shape
    widened = hid_ref[...].astype(jnp.float32)
    scale = lax.rsqrt(jnp.mean(widened * widened, axis=-1, keepdims=True) + RMS_EPS)
    normed = (widened * scale * gain_ref[...].astype(jnp.float32)).astype(jnp.bfloat16)
    cosine = cos_ref[...]
    sine = sin_ref[...]

    def put(out_ref, weight_ref, turned):
        product = jnp.dot(normed, weight_ref[...], preferred_element_type=jnp.float32)
        for h in range(heads):
            part = product[:, h * head_dim : (h + 1) * head_dim]
            if turned:
                part = part * cosine + pltpu.roll(part, head_dim // 2, 1) * sine
            out_ref[:, h] = part.astype(jnp.bfloat16).reshape(requests, nodes, head_dim)

    put(q_ref, wq_ref, True)
    put(k_ref, wk_ref, True)
    put(v_ref, wv_ref, False)


def project(hidden, gain, cosine, sine, w_q, w_k, w_v, requests, nodes, head_dim, group):
    rows, dim = hidden.shape
    cols = w_q.shape[1]
    heads = cols // head_dim
    block = group * nodes
    full = pl.BlockSpec((dim, cols), lambda i: (0, 0), pipeline_mode=pl.Buffered(1))
    out = pl.BlockSpec((group, heads, nodes, head_dim), lambda i: (i, 0, 0, 0))
    shape = jax.ShapeDtypeStruct((requests, heads, nodes, head_dim), jnp.bfloat16)
    return pl.pallas_call(
        qkv_kernel,
        grid=(rows // block,),
        in_specs=[
            pl.BlockSpec((block, dim), lambda i: (i, 0)),
            pl.BlockSpec((1, dim), lambda i: (0, 0)),
            pl.BlockSpec((block, head_dim), lambda i: (i, 0)),
            pl.BlockSpec((block, head_dim), lambda i: (i, 0)),
            full,
            full,
            full,
        ],
        out_specs=[out, out, out],
        out_shape=[shape, shape, shape],
        compiler_params=pltpu.CompilerParams(vmem_limit_bytes=VMEM_MAX),
        name="project",
    )(hidden, gain, cosine, sine, w_q, w_k, w_v)


def attend_kernel(table_ref, ctx_ref, q_ref, kn_ref, vn_ref, mask_ref, kc_ref, vc_ref, out_ref, ko_ref, vo_ref, kbuf, vbuf, rsem, wsem):
    b = pl.program_id(0)
    count = pl.num_programs(0)
    heads, span, head_dim = kbuf.shape[1:]
    nodes = q_ref.shape[2]
    page = kc_ref.shape[2]
    pages = span // page
    window = nodes + page

    def load(i, slot):
        def one(s, _):
            block = table_ref[i, s]
            rows = pl.ds(pl.multiple_of(s * page, page), page)
            pltpu.make_async_copy(kc_ref.at[block], kbuf.at[slot, :, rows], rsem.at[0, slot]).start()
            pltpu.make_async_copy(vc_ref.at[block], vbuf.at[slot, :, rows], rsem.at[1, slot]).start()
            return 0

        lax.fori_loop(0, pages, one, 0)

    def save(i, slot):
        def one(s, _):
            block = table_ref[i, s]
            rows = pl.ds(pl.multiple_of(s * page, page), page)
            pltpu.make_async_copy(kbuf.at[slot, :, rows], ko_ref.at[block], wsem.at[0, slot]).start()
            pltpu.make_async_copy(vbuf.at[slot, :, rows], vo_ref.at[block], wsem.at[1, slot]).start()
            return 0

        lax.fori_loop(0, pages, one, 0)

    def whole(slot, sem):
        pltpu.make_async_copy(kbuf.at[slot], kbuf.at[slot], sem.at[0, slot]).wait()
        pltpu.make_async_copy(vbuf.at[slot], vbuf.at[slot], sem.at[1, slot]).wait()

    slot = lax.rem(b, 3)
    after = lax.rem(b + 1, 3)

    @pl.when(b == 0)
    def _():
        load(0, 0)

    @pl.when(b >= 2)
    def _():
        whole(after, wsem)

    @pl.when(b + 1 < count)
    def _():
        load(b + 1, after)

    whole(slot, rsem)
    ctx = ctx_ref[b]
    base = pl.multiple_of(jnp.minimum((ctx // page) * page, span - window), page)
    row = base + lax.broadcasted_iota(jnp.int32, (window, nodes), 0)
    node = ctx + lax.broadcasted_iota(jnp.int32, (window, nodes), 1)
    place = jnp.where(row == node, 1.0, 0.0).astype(jnp.bfloat16)
    slot_id = base + lax.broadcasted_iota(jnp.int32, (window, head_dim), 0)
    fresh = (slot_id >= ctx) & (slot_id < ctx + nodes)
    for h in range(heads):
        for buf, new_ref in ((kbuf, kn_ref), (vbuf, vn_ref)):
            moved = jnp.dot(place, new_ref[0, h], preferred_element_type=jnp.float32)
            old = buf[slot, h, pl.ds(base, window), :]
            buf[slot, h, pl.ds(base, window), :] = jnp.where(fresh, moved, old.astype(jnp.float32)).astype(jnp.bfloat16)
    save(b, slot)
    spread = jnp.where(
        ctx + lax.broadcasted_iota(jnp.int32, (nodes, span), 0) == lax.broadcasted_iota(jnp.int32, (nodes, span), 1), 1.0, 0.0
    ).astype(jnp.bfloat16)
    linked = jnp.where(mask_ref[0] > 0, 1.0, 0.0).astype(jnp.bfloat16)
    seen_new = jnp.dot(linked, spread, preferred_element_type=jnp.float32) > 0.5
    seen = seen_new | (lax.broadcasted_iota(jnp.int32, (nodes, span), 1) < ctx)
    scale = head_dim**-0.5
    for h in range(heads):
        score = dot_nt(q_ref[0, h], kbuf[slot, h]) * scale
        score = jnp.where(seen, score, -jnp.inf)
        top = jnp.max(score, axis=-1, keepdims=True)
        prob = jnp.exp(score - top)
        total = jnp.sum(prob, axis=-1, keepdims=True)
        mixed = jnp.dot(prob.astype(jnp.bfloat16), vbuf[slot, h], preferred_element_type=jnp.float32)
        out_ref[:, h * head_dim : (h + 1) * head_dim] = (mixed / total).astype(jnp.bfloat16)

    @pl.when(b == count - 1)
    def _():
        whole(lax.rem(b + 2, 3), wsem)
        whole(slot, wsem)


def attend(table, ctx_len, query, key_new, val_new, tree_mask, k_cache, v_cache):
    requests, heads, nodes, head_dim = query.shape
    page = k_cache.shape[2]
    span = table.shape[1] * page
    node_spec = pl.BlockSpec((1, heads, nodes, head_dim), lambda b, *_: (b, 0, 0, 0))
    anywhere = pl.BlockSpec(memory_space=pl.ANY)
    return pl.pallas_call(
        attend_kernel,
        grid_spec=pltpu.PrefetchScalarGridSpec(
            num_scalar_prefetch=2,
            grid=(requests,),
            in_specs=[
                node_spec,
                node_spec,
                node_spec,
                pl.BlockSpec((1, nodes, nodes), lambda b, *_: (b, 0, 0)),
                anywhere,
                anywhere,
            ],
            out_specs=[pl.BlockSpec((nodes, heads * head_dim), lambda b, *_: (b, 0)), anywhere, anywhere],
            scratch_shapes=[
                pltpu.VMEM((3, heads, span, head_dim), jnp.bfloat16),
                pltpu.VMEM((3, heads, span, head_dim), jnp.bfloat16),
                pltpu.SemaphoreType.DMA((2, 3)),
                pltpu.SemaphoreType.DMA((2, 3)),
            ],
        ),
        out_shape=[
            jax.ShapeDtypeStruct((requests * nodes, heads * head_dim), jnp.bfloat16),
            jax.ShapeDtypeStruct(k_cache.shape, k_cache.dtype),
            jax.ShapeDtypeStruct(v_cache.shape, v_cache.dtype),
        ],
        name="attend",
    )(table, ctx_len, query, key_new, val_new, tree_mask, k_cache, v_cache)


def rms_norm(values, gain):
    widened = values.astype(jnp.float32)
    scale = lax.rsqrt(jnp.mean(widened * widened, axis=-1, keepdims=True) + RMS_EPS)
    return (widened * scale * gain.astype(jnp.float32)).astype(jnp.bfloat16)


def rope_tables(positions, head_dim):
    half = head_dim // 2
    inv_freq = 1.0 / (ROPE_THETA ** (jnp.arange(half, dtype=jnp.float32) * (2.0 / head_dim)))
    angles = positions.astype(jnp.float32)[:, None] * inv_freq
    cosine = jnp.cos(angles)
    sine = jnp.sin(angles)
    return jnp.concatenate([cosine, cosine], axis=-1), jnp.concatenate([-sine, sine], axis=-1)


def solution(mesh):
    def group_step(hidden, tree_mask, depth, ctx_len, block_table, score_id, k_cache, v_cache, attn_norm, w_q, w_k, w_v, w_o, mlp_norm, w_gate, w_up, w_down, final_norm, w_lm):
        requests, nodes, dim = hidden.shape
        head_dim = k_cache.shape[3]
        rows = requests * nodes
        flat = hidden.reshape(rows, dim)
        cosine, sine = rope_tables((ctx_len[:, None] + depth).reshape(rows), head_dim)
        query, key_new, val_new = project(flat, attn_norm.reshape(1, dim), cosine, sine, w_q, w_k, w_v, requests, nodes, head_dim, 4)
        attended, k_out, v_out = attend(
            block_table, ctx_len, query, key_new, val_new, tree_mask, jnp.transpose(k_cache, (0, 2, 1, 3)), jnp.transpose(v_cache, (0, 2, 1, 3))
        )
        k_out = jnp.transpose(k_out, (0, 2, 1, 3))
        v_out = jnp.transpose(v_out, (0, 2, 1, 3))

        attn_sum = lax.psum(jnp.dot(attended, w_o, preferred_element_type=jnp.float32).astype(jnp.bfloat16), "tp")
        residual = (flat.astype(jnp.float32) + attn_sum.astype(jnp.float32)).astype(jnp.bfloat16)
        normed_mlp = rms_norm(residual, mlp_norm)
        gate = jnp.dot(normed_mlp, w_gate, preferred_element_type=jnp.float32)
        upper = jnp.dot(normed_mlp, w_up, preferred_element_type=jnp.float32)
        product = (jax.nn.silu(gate) * upper).astype(jnp.bfloat16)
        mlp_sum = lax.psum(jnp.dot(product, w_down, preferred_element_type=jnp.float32).astype(jnp.bfloat16), "tp")
        layer_out = (residual.astype(jnp.float32) + mlp_sum.astype(jnp.float32)).astype(jnp.bfloat16)
        logits = jnp.dot(rms_norm(layer_out, final_norm), w_lm, preferred_element_type=jnp.float32)
        vocab_local = logits.shape[-1]
        local_id = score_id.reshape(rows, 1) - lax.axis_index("tp") * vocab_local
        top = jnp.max(logits, axis=-1)
        part = jnp.sum(jnp.exp(logits - top[:, None]), axis=-1)
        hit = lax.broadcasted_iota(jnp.int32, logits.shape, 1) == local_id
        picked = jnp.sum(jnp.where(hit, logits, 0.0), axis=-1)
        stats = lax.all_gather(jnp.stack([top, part, picked]), "tp")
        global_top = jnp.max(stats[:, 0], axis=0)
        total = jnp.sum(stats[:, 1] * jnp.exp(stats[:, 0] - global_top), axis=0)
        log_norm = global_top + jnp.log(total)
        log_prob = jnp.sum(stats[:, 2], axis=0) - log_norm
        return log_norm.reshape(requests, nodes), log_prob.reshape(requests, nodes), k_out, v_out

    request_spec = P("dp", None, None)
    node_spec = P("dp", None)
    cache_spec = P("dp", None, "tp", None)
    shared_spec = P(None)
    column_spec = P(None, "tp")
    row_spec = P("tp", None)
    in_specs = (request_spec, request_spec, node_spec, P("dp"), node_spec, node_spec, cache_spec, cache_spec, shared_spec, column_spec, column_spec, column_spec, row_spec, shared_spec, column_spec, column_spec, row_spec, shared_spec, column_spec)
    out_specs = (node_spec, node_spec, cache_spec, cache_spec)
    return jax.shard_map(group_step, mesh=mesh, in_specs=in_specs, out_specs=out_specs, check_vma=False)
```

time: 862 us -> 568 us (0.66)
  local copies, waits for them, and re-layouts: 384 us -> 2.29 us
  waiting for transfers between devices: 140 us -> 267 us
  Pallas kernels: 0 us -> 77.1 us
  matrix products: 216 us -> 145 us
  blocking collectives: 47 us -> 11.2 us
  other arithmetic: 49.4 us -> 31.3 us
  starting transfers between devices: 0.08 us -> 10.8 us
    unnamed x51 -> x10, local copies, waits for them, and re-layouts: 276 us -> 0.69 us
    psum x2, waiting for transfers between devices: 140 us -> 267 us  [the longest x1 137 us: group_step(): lax.psum(jnp.dot(product, w_down, preferred_element_type=jnp.float32).ast...]
    gather x10 -> x0, local copies, waits for them, and re-layouts: 81.8 us -> none  [the longest x2 28.7 us: layer_and_logits(): val_old = v_cache[block_table].reshape(requests, span, kv_local, head_dim)]
    pallas_call x0 -> x2, Pallas kernels: none -> 77.1 us  [the longest x1 41.5 us: attend(): pl.pallas_call(attend_kernel, grid_spec=pltpu.PrefetchScalarGridSpec(num_...]
    dot_general x12 -> x5, matrix products: 216 us -> 145 us  [the longest x1 55.2 us: group_step(): jnp.dot(rms_norm(layer_out, final_norm), w_lm, preferred_element_type=jnp...]
    psum x1 -> x0, blocking collectives: 24.4 us -> none  [group_step(): lax.psum(jnp.stack([part_sum, jnp.where(inside, picked, 0.0)]), 'tp')]
    pmax x1 -> x0, blocking collectives: 22.7 us -> none  [group_step(): global_top = lax.pmax(jnp.max(logits, axis=-1), 'tp')]
    all_gather x0 -> x1, blocking collectives: none -> 11.2 us  [group_step(): stats = lax.all_gather(jnp.stack([top, part, picked]), 'tp')]
  transfers between devices with their start and end apart: 2 -> 2, of which waited for: 1 -> 2; matrix products, arithmetic and copies ran while one was open for 33% -> 0% of each run, Pallas kernels for 0% -> 0%
where the time goes in v1:
time: 568 us; the launch traced here: 559 us
  waiting for transfers between devices  267 us (47%)
  matrix products  145 us (26%)
  Pallas kernels  77.1 us (14%)
  other arithmetic  31.3 us (6%)
  between operations  14.5 us (3%)
  blocking collectives  11.2 us (2%)
  starting transfers between devices  10.8 us (2%)
    psum x1, waiting for transfers between devices, group_step(): lax.psum(jnp.dot(product, w_down, preferred_element_type=jnp.float32).ast...  137 us
    psum x1, waiting for transfers between devices, group_step(): lax.psum(jnp.dot(attended, w_o, preferred_element_type=jnp.float32).astyp...  130 us
    dot_general x1, matrix products, group_step(): jnp.dot(rms_norm(layer_out, final_norm), w_lm, preferred_element_type=jnp...  55.2 us
    pallas_call x1, Pallas kernels, attend(): pl.pallas_call(attend_kernel, grid_spec=pltpu.PrefetchScalarGridSpec(num_...  41.5 us
    pallas_call x1, Pallas kernels, project(): pl.pallas_call(qkv_kernel, grid=(rows // block,), in_specs=[pl.BlockSpec(...  35.6 us
    dot_general x1, matrix products, group_step(): gate = jnp.dot(normed_mlp, w_gate, preferred_element_type=jnp.float32)  26.8 us
    dot_general x1, matrix products, group_step(): jnp.dot(product, w_down, preferred_element_type=jnp.float32)  25.2 us
    dot_general x1, matrix products, group_step(): upper = jnp.dot(normed_mlp, w_up, preferred_element_type=jnp.float32)  24.3 us
  transfers between devices with their start and end apart: 2, of which 2 were waited for; matrix products, arithmetic and copies ran while one was open for 0% of the time, Pallas kernels for 0%

profile of v1, /device:TPU:0, one launch (start us, length us, event | category | flops | bytes accessed | tf_op | source)
XLA Modules:
  0.0 559.5 jit_solution(9758833350298245237)
XLA Ops:
  7.2 0.0 all-reduce.3.cloned.1.call-start
  7.2 0.8 add_convert_fusion.1
  8.0 0.1 convert_element_type.55
  8.1 1.3 reshape.68.gain_ref
  9.4 1.9 fusion.15
  11.3 1.3 pad_maximum_fusion
  12.6 35.6 %project.1 = (bf16[16,5,64,128]{3,2,1,0:T(8,128)(2,1)}, bf16[16,5,64,128]{3,2,1,0:T(8,128)(2,1)}, bf16[16,5,64,128]{3,2,1,0:T(8,128)(2,1)}) custom-call(bf16[1024,5120]{1,0:T(8,128)(2,1)} %bitcast.32, bf16[1,5120]{1,0:T(2,128)(2,1)} %reshape.68.gain_ref, f32[1024,128]{1,0:T(8,128)} %get-tuple-element.31.cos_ref, f32[1024,128]{1,0:T(8,128)} %get-tuple-element.32.sin_ref, ...), custom_call_target="tpu_custom_call" | custom-call | tf_op jit(solution)/shard_map/project/pallas_call | solution.py:50
  48.2 41.5 %attend.1 = (bf16[1024,640]{1,0:T(8,128)(2,1)}, bf16[512,5,16,128]{3,2,1,0:T(8,128)(2,1)}, bf16[512,5,16,128]{3,2,1,0:T(8,128)(2,1)}) custom-call(s32[16,32]{1,0:T(8,128)} %table_ref.1, s32[16]{0:T(128)} %ctx_ref.1, bf16[16,5,64,128]{3,2,1,0:T(8,128)(2,1)} %get-tuple-element.10.q_ref, bf16[16,5,64,128]{3,2,1,0:T(8,128)(2,1)} %get-tuple-element.11.kn_ref, ...), custom_call_target="tpu_custom_call" | custom-call | tf_op jit(solution)/shard_map/attend/pallas_call | solution.py:159
  89.7 13.9 %convolution_convert_fusion.1 = bf16[1024,5120]{1,0:T(8,128)(2,1)} fusion(bf16[1024,640]{1,0:T(8,128)(2,1)} %get-tuple-element.13, bf16[640,5120]{1,0:T(8,128)(2,1)} %param.31), kind=kOutput, calls=%fused_computation.20 | convolution fusion | flops 6716129280 | bytes 18350080 | tf_op jit(solution)/shard_map/dot_general | solution.py:218
  103.7 0.0 copy-start.2
  103.7 0.0 all-reduce.3.cloned.1.call-update
  103.7 10.7 %all-reduce.5.cloned.1.call-start = ((), (), s32[]{:S(2)}) async-start(), calls=%async_computation.1 | async-start | bytes 20971520 | tf_op jit(solution)/shard_map/psum | solution.py:224
  114.4 0.0 copy-done.2
  114.4 129.8 %all-reduce.3.cloned.1.call-done = bf16[1024,5120]{1,0:T(8,128)(2,1)} async-done(((bf16[1024,5120]{1,0:T(8,128)(2,1)}), bf16[1024,5120]{1,0:T(8,128)(2,1)}) %all-reduce.3.cloned.1.call-update) | async-done | bytes 10485776 | tf_op jit(solution)/shard_map/psum | solution.py:218
  244.2 9.4 %fusion.3 = (f32[1024]{0:T(1024)S(1)}, bf16[1024,5120]{1,0:T(8,128)(2,1)S(1)}) fusion(bf16[1024,5120]{1,0:T(8,128)(2,1)} %all-reduce.3.cloned.1.call-done, bf16[16,64,5120]{2,1,0:T(8,128)(2,1)} %param.19), kind=kLoop, calls=%fused_computation.8 | loop fusion | flops 36699136 | bytes 31461376 | tf_op jit(solution)/shard_map/reduce_sum | solution.py:191
  253.6 0.0 copy-start
  253.7 26.8 %fusion.13 = f32[1024,1728]{0,1:T(8,128)} fusion(bf16[5120,1728]{0,1:T(8,128)(2,1)} %param.33, bf16[1024,5120]{1,0:T(8,128)(2,1)S(1)} %get-tuple-element.21, f32[5120]{0:T(1024)S(1)} %convert_element_type.60, f32[1024]{0:T(1024)S(1)} %add_rsqrt_fusion.1), kind=kOutput, calls=%fused_computation.22 | convolution fusion | flops 18140364800 | bytes 35282944 | tf_op jit(solution)/shard_map/dot_general | solution.py:221
  280.4 0.0 copy-done
  280.4 24.3 %multiply_convert_fusion = bf16[1024,1728]{0,1:T(8,128)(2,1)} fusion(f32[1024,1728]{0,1:T(8,128)} %fusion.13, bf16[5120,1728]{0,1:T(8,128)(2,1)} %param.34, bf16[1024,5120]{1,0:T(8,128)(2,1)S(1)} %get-tuple-element.21, f32[5120]{0:T(1024)S(1)} %convert_element_type.60, f32[1024]{0:T(1024)S(1)} %add_rsqrt_fusion.1), kind=kOutput, calls=%fused_computation.21 | convolution fusion | flops 18150981632 | bytes 38821888 | tf_op jit(solution)/shard_map/dot_general | solution.py:222
  304.7 25.2 %convolution_convert_fusion = bf16[1024,5120]{1,0:T(8,128)(2,1)} fusion(bf16[1024,1728]{0,1:T(8,128)(2,1)} %multiply_convert_fusion, bf16[1728,5120]{1,0:T(8,128)(2,1)} %param.35), kind=kOutput, calls=%fused_computation.19 | convolution fusion | flops 18124636160 | bytes 31719424 | tf_op jit(solution)/shard_map/dot_general | solution.py:224
  330.0 0.0 copy-start.3
  330.0 0.0 copy-start.4
  330.0 0.0 all-reduce.5.cloned.1.call-update
  330.0 0.7 copy-done.3
  330.7 0.0 copy-done.4
  330.7 0.1 sub.38
  330.7 137.0 %all-reduce.5.cloned.1.call-done = bf16[1024,5120]{1,0:T(8,128)(2,1)} async-done(((bf16[1024,5120]{1,0:T(8,128)(2,1)}), bf16[1024,5120]{1,0:T(8,128)(2,1)}) %all-reduce.5.cloned.1.call-update) | async-done | bytes 10485776 | tf_op jit(solution)/shard_map/psum | solution.py:224
  467.8 9.2 %fusion = f32[1024]{0:T(1024)S(1)} fusion(bf16[1024,5120]{1,0:T(8,128)(2,1)} %all-reduce.5.cloned.1.call-done, bf16[1024,5120]{1,0:T(8,128)(2,1)} %copy-done), kind=kLoop, calls=%fused_computation.5 | loop fusion | flops 36699136 | bytes 20975616 | tf_op jit(solution)/shard_map/reduce_sum | solution.py:191
  477.0 55.2 %fusion.21 = (f32[1024]{0:T(1024)S(1)}, f32[1024,4000]{0,1:T(8,128)}) fusion(bf16[5120,4000]{0,1:T(8,128)(2,1)} %param.37, f32[5120]{0:T(1024)S(1)} %convert_element_type.67, f32[1024]{0:T(1024)S(1)} %add_rsqrt_fusion, bf16[1024,5120]{1,0:T(8,128)(2,1)} %all-reduce.5.cloned.1.call-done, bf16[1024,5120]{1,0:T(8,128)(2,1)} %copy-done), kind=kOutput, calls=%fused_computation.43 | convolution fusion | flops 41989079040 | bytes 78344192 | tf_op jit(solution)/shard_map/dot_general | solution.py:226
  532.2 8.0 %exponential_reduce_fusion = (f32[1024]{0:T(1024)S(1)}, f32[1024]{0:T(1024)S(1)}) fusion(f32[1024,4000]{0,1:T(8,128)} %get-tuple-element.30, f32[1024]{0:T(1024)S(1)} %get-tuple-element.29, s32[1024]{0:T(1024)S(1)} %sub.38), kind=kLoop, calls=%fused_computation.15 | loop fusion | flops 20477952 | bytes 16400384 | tf_op jit(solution)/shard_map/reduce_sum | solution.py:230
  540.1 11.2 %all-gather.1 = f32[8,3,1024]{2,1,0:T(4,128)S(1)} all-gather(f32[1,3,1024]{2,1,0:T(4,128)S(1)} %maximum_bitcast_fusion), channel_id=2, replica_groups=mesh['dp'=1,'tp'=8] {'tp'}, dimensions={0}, use_global_device_ids=true | all-gather | bytes 110592 | tf_op jit(solution)/shard_map/all_gather | solution.py:233
  551.4 0.1 fusion.20
  551.5 0.1 add.54
  551.6 0.0 copy-start.1
  551.6 0.1 reduce_sum.62
  551.7 0.6 sub.41
  552.3 0.0 copy-done.1
  (9 shorter events, 0.1 us)
Async XLA Ops:
  7.2 237.1 %all-reduce.3.cloned.1.call-start = ((), (), s32[]{:S(2)}) async-start(), calls=%async_computation | async-start | bytes 20971520 | tf_op jit(solution)/shard_map/psum | solution.py:218
  103.7 10.8 %copy-start.2 = (bf16[5120]{0:T(1024)(128)(2,1)S(1)}, bf16[5120]{0:T(1024)(128)(2,1)}, u32[]{:S(2)}) copy-start(bf16[5120]{0:T(1024)(128)(2,1)} %param.32) | copy-start | bytes 30724
  103.7 364.1 %all-reduce.5.cloned.1.call-start = ((), (), s32[]{:S(2)}) async-start(), calls=%async_computation.1 | async-start | bytes 20971520 | tf_op jit(solution)/shard_map/psum | solution.py:224
  253.6 26.8 %copy-start = (bf16[1024,5120]{1,0:T(8,128)(2,1)}, bf16[1024,5120]{1,0:T(8,128)(2,1)S(1)}, u32[]{:S(2)}) copy-start(bf16[1024,5120]{1,0:T(8,128)(2,1)S(1)} %get-tuple-element.21) | copy-start | bytes 31457284
  330.0 0.7 copy-start.3
  330.0 0.7 copy-start.4
  551.6 0.7 copy-start.1
Sparse Core Ops, SparseCore 0:
  103.8 140.3 all-reduce.2
  330.1 137.6 all-reduce.4

commit v2 on v1

--- a/solution.py
+++ b/solution.py
@@ -186,10 +186,428 @@
     )(table, ctx_len, query, key_new, val_new, tree_mask, k_cache, v_cache)
 
 
-def rms_norm(values, gain):
-    widened = values.astype(jnp.float32)
-    scale = lax.rsqrt(jnp.mean(widened * widened, axis=-1, keepdims=True) + RMS_EPS)
-    return (widened * scale * gain.astype(jnp.float32)).astype(jnp.bfloat16)
+TILE = 512
+HALF = TILE // 2
+PAIR, X1, Y1, X2, Y2, GX, GY, GP, FX, FY, PX, PY, PD = range(13)
+
+
+def seat():
+    me = lax.axis_index("tp")
+    core = me % 2
+    x = (me // 2) % 2
+    y = me // 4
+    to_x = y * 4 + (1 - x) * 2 + core
+    to_y = (1 - y) * 4 + x * 2 + core
+    to_pair = y * 4 + x * 2 + (1 - core)
+    return me, core, x, y, to_x, to_y, to_pair
+
+
+def send(src, dst, ssem, rsem, kind, t, target):
+    pltpu.make_async_remote_copy(
+        src_ref=src, dst_ref=dst, send_sem=ssem.at[kind], recv_sem=rsem.at[kind, t], device_id={"tp": target}, device_id_type=MESH
+    ).start()
+
+
+def landed(ref, rsem, kind, t):
+    pltpu.make_async_copy(ref, ref, rsem.at[kind, t]).wait()
+
+
+def sent(ref, ssem, kind):
+    pltpu.make_async_copy(ref, ref, ssem.at[kind]).wait()
+
+
+def reduce_norm_gather(left_ref, w_hbm, wbuf, wsem, resid, resid_ready, gain_ref, h_ref, mbuf, r1, rx, ry, r2x, r2y, ssq, ssem, rsem, free, idle_work, compute):
+    me, core, x, y, to_x, to_y, to_pair = seat()
+    tiles = mbuf.shape[0]
+    rows = mbuf.shape[4]
+    depth = w_hbm.shape[0]
+
+    def fetch(t):
+        cols = pl.ds(pl.multiple_of(t * TILE, TILE), TILE)
+        return pltpu.make_async_copy(w_hbm.at[:, cols], wbuf.at[t % 2, pl.ds(0, depth)], wsem.at[t % 2])
+
+    fetch(0).start()
+    fetch(1).start()
+
+    def scatter_step(j, _):
+        @pl.when(j < tiles)
+        def _():
+            fetch(j).wait()
+            for half in range(2):
+                cols = pl.ds(half * HALF, HALF)
+                part = jnp.dot(left_ref[...], wbuf[j % 2, :, cols], preferred_element_type=jnp.float32)
+                mbuf[j, :, :, :, :, cols] = part.astype(jnp.bfloat16).reshape(2, 2, 2, rows, HALF)
+
+            @pl.when(j + 2 < tiles)
+            def _():
+                fetch(j + 2).start()
+
+            send(mbuf.at[j, :, :, 1 - core], r1.at[j], ssem, rsem, PAIR, j, to_pair)
+            idle_work(j)
+
+        @pl.when((j >= 1) & (j < tiles + 1))
+        def _():
+            t = j - 1
+            landed(r1.at[t], rsem, PAIR, t)
+            for yy in range(2):
+                for xx in range(2):
+                    mbuf[t, yy, xx, core] = mbuf[t, yy, xx, core] + r1[t, yy, xx]
+            send(mbuf.at[t, :, 1 - x, core, :, pl.ds(0, HALF)], rx.at[t], ssem, rsem, X1, t, to_x)
+            send(mbuf.at[t, 1 - y, :, core, :, pl.ds(HALF, HALF)], ry.at[t], ssem, rsem, Y1, t, to_y)
+
+        @pl.when((j >= 2) & (j < tiles + 2))
+        def _():
+            t = j - 2
+            landed(rx.at[t], rsem, X1, t)
+            for yy in range(2):
+                mbuf[t, yy, x, core, :, pl.ds(0, HALF)] = mbuf[t, yy, x, core, :, pl.ds(0, HALF)] + rx[t, yy]
+            send(mbuf.at[t, 1 - y, x, core, :, pl.ds(0, HALF)], r2y.at[t], ssem, rsem, Y2, t, to_y)
+            landed(ry.at[t], rsem, Y1, t)
+            for xx in range(2):
+                mbuf[t, y, xx, core, :, pl.ds(HALF, HALF)] = mbuf[t, y, xx, core, :, pl.ds(HALF, HALF)] + ry[t, xx]
+            send(mbuf.at[t, y, 1 - x, core, :, pl.ds(HALF, HALF)], r2x.at[t], ssem, rsem, X2, t, to_x)
+
+        @pl.when(j == 3)
+        def _():
+            resid_ready()
+            ssq[...] = jnp.zeros_like(ssq)
+
+        @pl.when(j >= 3)
+        def _():
+            t = j - 3
+            landed(r2y.at[t], rsem, Y2, t)
+            landed(r2x.at[t], rsem, X2, t)
+            for half, other in ((0, r2y), (1, r2x)):
+                cols = pl.ds(half * HALF, HALF)
+                total = (mbuf[t, y, x, core, :, cols] + other[t]).astype(jnp.float32)
+                new = (resid[t, :, cols].astype(jnp.float32) + total).astype(jnp.bfloat16)
+                h_ref[t, :, cols] = new
+                wide = new.astype(jnp.float32)
+                wide = wide * wide
+                for lane in range(0, HALF, 128):
+                    ssq[...] += wide[:, lane : lane + 128]
+
+        return 0
+
+    lax.fori_loop(0, tiles + 3, scatter_step, 0)
+    sent(r1, ssem, PAIR)
+    sent(rx, ssem, X1)
+    sent(ry, ssem, Y1)
+    sent(r2x, ssem, X2)
+    sent(r2y, ssem, Y2)
+    for target in (to_x, to_y, to_pair):
+        pl.semaphore_signal(free, inc=1, device_id={"tp": target}, device_id_type=MESH)
+    scale = lax.rsqrt(jnp.sum(ssq[...], axis=-1, keepdims=True) * (1.0 / (tiles * TILE)) + RMS_EPS)
+
+    def norm_step(t, _):
+        mbuf[t, y, x, core] = (h_ref[t].astype(jnp.float32) * scale * gain_ref[t].astype(jnp.float32)).astype(jnp.bfloat16)
+        return 0
+
+    lax.fori_loop(0, tiles, norm_step, 0)
+    pl.semaphore_wait(free, 3)
+
+    def own(t):
+        mine = mbuf.at[t, y, x, core]
+        send(mine, mine, ssem, rsem, GX, t, to_x)
+        send(mine, mine, ssem, rsem, GY, t, to_y)
+        send(mine, mine, ssem, rsem, GP, t, to_pair)
+
+    own(0)
+    own(1)
+
+    def gather_step(j, _):
+        @pl.when(j + 2 < tiles)
+        def _():
+            own(j + 2)
+
+        @pl.when(j < tiles)
+        def _():
+            from_x = mbuf.at[j, y, 1 - x, core]
+            from_y = mbuf.at[j, 1 - y, x, core]
+            landed(from_x, rsem, GX, j)
+            upper = from_x.at[pl.ds(0, rows // 2)]
+            send(upper, upper, ssem, rsem, FY, j, to_y)
+            send(from_x, from_x, ssem, rsem, PX, j, to_pair)
+            landed(from_y, rsem, GY, j)
+            lower = from_y.at[pl.ds(rows // 2, rows // 2)]
+            send(lower, lower, ssem, rsem, FX, j, to_x)
+            send(from_y, from_y, ssem, rsem, PY, j, to_pair)
+
+        @pl.when((j >= 1) & (j < tiles + 1))
+        def _():
+            t = j - 1
+            far = mbuf.at[t, 1 - y, 1 - x, core]
+            landed(far.at[pl.ds(0, rows // 2)], rsem, FY, t)
+            landed(far.at[pl.ds(rows // 2, rows // 2)], rsem, FX, t)
+            send(far, far, ssem, rsem, PD, t, to_pair)
+
+        @pl.when(j >= 2)
+        def _():
+            t = j - 2
+            landed(mbuf.at[t, y, x, 1 - core], rsem, GP, t)
+            landed(mbuf.at[t, y, 1 - x, 1 - core], rsem, PX, t)
+            landed(mbuf.at[t, 1 - y, x, 1 - core], rsem, PY, t)
+            landed(mbuf.at[t, 1 - y, 1 - x, 1 - core], rsem, PD, t)
+            compute(t)
+
+        return 0
+
+    lax.fori_loop(0, tiles + 2, gather_step, 0)
+    for kind in (GX, GY, GP, PX, PY, PD):
+        sent(h_ref, ssem, kind)
+    for kind in (FX, FY):
+        sent(h_ref.at[pl.ds(0, tiles // 2)], ssem, kind)
+
+
+def greet(targets):
+    barrier = pltpu.get_barrier_semaphore()
+    for target in targets:
+        pl.semaphore_signal(barrier, inc=1, device_id={"tp": target}, device_id_type=MESH)
+    pl.semaphore_wait(barrier, len(targets))
+
+
+def mlp_kernel(att_ref, gain_ref, hid_hbm, wo_hbm, wg_hbm, wu_hbm, prod_ref, h_ref, mbuf, r1, rx, ry, r2x, r2y, ssq, wo_buf, resid, wg_buf, wu_buf, acc_g, acc_u, ssem, rsem, wsem, gsem, hsem, free):
+    me, core, x, y, to_x, to_y, to_pair = seat()
+    tiles = mbuf.shape[0]
+    rows = mbuf.shape[4]
+    width = wg_hbm.shape[0]
+    blocks = acc_g.shape[0]
+    padded = wg_buf.shape[1]
+
+    def fetch(t):
+        cols = pl.ds(pl.multiple_of(t * TILE, TILE), TILE)
+        slot = t % 2
+        return (
+            pltpu.make_async_copy(wg_hbm.at[:, cols], wg_buf.at[slot, pl.ds(0, width)], gsem.at[0, slot]),
+            pltpu.make_async_copy(wu_hbm.at[:, cols], wu_buf.at[slot, pl.ds(0, width)], gsem.at[1, slot]),
+        )
+
+    greet((to_x, to_y, to_pair))
+    if padded > width:
+        for slot in range(2):
+            wg_buf[slot, pl.ds(width, padded - width)] = jnp.zeros((padded - width, TILE), jnp.bfloat16)
+            wu_buf[slot, pl.ds(width, padded - width)] = jnp.zeros((padded - width, TILE), jnp.bfloat16)
+    for t in range(2):
+        for copy in fetch(t):
+            copy.start()
+
+    def hidden_copy(t):
+        cols = pl.ds(t * TILE, TILE)
+        return pltpu.make_async_copy(hid_hbm.at[pl.ds(pl.multiple_of(me * rows, rows), rows), cols], resid.at[t], hsem)
+
+    for t in range(tiles):
+        hidden_copy(t).start()
+
+    def resid_ready():
+        pltpu.make_async_copy(resid, resid, hsem).wait()
+
+    def idle_work(j):
+        @pl.when(j < blocks)
+        def _():
+            acc_g[j] = jnp.zeros(acc_g.shape[1:], jnp.float32)
+            acc_u[j] = jnp.zeros(acc_u.shape[1:], jnp.float32)
+
+    def compute(t):
+        slot = t % 2
+        for copy in fetch(t):
+            copy.wait()
+
+        def one(n, _):
+            cols = pl.ds(pl.multiple_of(n * 256, 256), 256)
+            left = mbuf[t].reshape(8 * rows, TILE)
+            acc_g[n] += dot_nt(left, wg_buf[slot, cols])
+            acc_u[n] += dot_nt(left, wu_buf[slot, cols])
+            return 0
+
+        lax.fori_loop(0, blocks, one, 0)
+
+        @pl.when(t + 2 < tiles)
+        def _():
+            for copy in fetch(t + 2):
+                copy.start()
+
+    reduce_norm_gather(att_ref, wo_hbm, wo_buf, wsem, resid, resid_ready, gain_ref, h_ref, mbuf, r1, rx, ry, r2x, r2y, ssq, ssem, rsem, free, idle_work, compute)
+
+    def finish(n, _):
+        cols = pl.ds(pl.multiple_of(n * 256, 256), 256)
+        prod_ref[:, cols] = (jax.nn.silu(acc_g[n]) * acc_u[n]).astype(jnp.bfloat16)
+        return 0
+
+    lax.fori_loop(0, blocks, finish, 0)
+
+
+def head_kernel(prod_ref, gain_ref, res_ref, id_ref, wd_hbm, wl_hbm, out_ref, h_ref, mbuf, r1, rx, ry, r2x, r2y, ssq, wd_buf, wl_buf, acc, stats, ssem, rsem, wsem, lsem, tsem, usem, free):
+    me, core, x, y, to_x, to_y, to_pair = seat()
+    tiles = mbuf.shape[0]
+    rows = mbuf.shape[4]
+    depth = wd_hbm.shape[0]
+    padded = wd_buf.shape[1]
+    blocks, block = acc.shape[0], acc.shape[1]
+    vocab = wl_hbm.shape[0]
+    others = [(me + i) % 8 for i in range(1, 8)]
+
+    def fetch(t):
+        cols = pl.ds(pl.multiple_of(t * TILE, TILE), TILE)
+        return pltpu.make_async_copy(wl_hbm.at[:, cols], wl_buf.at[t % 2], lsem.at[t % 2])
+
+    greet(others)
+    if padded > depth:
+        for slot in range(2):
+            wd_buf[slot, pl.ds(depth, padded - depth)] = jnp.zeros((padded - depth, TILE), jnp.bfloat16)
+    fetch(0).start()
+    fetch(1).start()
+
+    def resid_ready():
+        pass
+
+    def idle_work(j):
+        @pl.when(j < blocks)
+        def _():
+            acc[j] = jnp.zeros(acc.shape[1:], jnp.float32)
+
+    def compute(t):
+        fetch(t).wait()
+
+        def one(n, _):
+            part = pl.ds(pl.multiple_of(n * block, block), block)
+            acc[n] += dot_nt(wl_buf[t % 2, part], mbuf[t].reshape(8 * rows, TILE))
+            return 0
+
+        lax.fori_loop(0, blocks, one, 0)
+
+        @pl.when(t + 2 < tiles)
+        def _():
+            fetch(t + 2).start()
+
+    reduce_norm_gather(prod_ref, wd_hbm, wd_buf, wsem, res_ref, resid_ready, gain_ref, h_ref, mbuf, r1, rx, ry, r2x, r2y, ssq, ssem, rsem, free, idle_work, compute)
+
+    count = 8 * rows
+
+    def top_step(n, best):
+        return jnp.maximum(best, jnp.max(acc[n].reshape(block // 8, 8, count), axis=0))
+
+    best = lax.fori_loop(0, blocks, top_step, jnp.full((8, count), -jnp.inf, jnp.float32))
+    best = jnp.max(best, axis=0, keepdims=True)
+    local_id = id_ref[...] - me * vocab
+
+    def sum_step(n, carry):
+        total, picked = carry
+        value = acc[n]
+        hit = lax.broadcasted_iota(jnp.int32, (block, count), 0) + n * block == local_id
+        total = total + jnp.sum(jnp.exp(value - best).reshape(block // 8, 8, count), axis=0)
+        picked = picked + jnp.sum(jnp.where(hit, value, 0.0).reshape(block // 8, 8, count), axis=0)
+        return total, picked
+
+    zero = jnp.zeros((8, count), jnp.float32)
+    total, picked = lax.fori_loop(0, blocks, sum_step, (zero, zero))
+
+    def pack(values):
+        return jnp.concatenate([values[:, i * 128 : (i + 1) * 128] for i in range(8)], axis=0)
+
+    stats[me, 0] = pack(best)
+    stats[me, 1] = pack(jnp.sum(total, axis=0, keepdims=True))
+    stats[me, 2] = pack(jnp.sum(picked, axis=0, keepdims=True))
+    copies = []
+    for i, other in enumerate(others):
+        copy = pltpu.make_async_remote_copy(
+            src_ref=stats.at[me], dst_ref=stats.at[me], send_sem=tsem.at[i], recv_sem=usem.at[i], device_id={"tp": other}, device_id_type=MESH
+        )
+        copy.start()
+        copies.append(copy)
+    for copy in copies:
+        copy.wait()
+    top = stats[0, 0]
+    for d in range(1, 8):
+        top = jnp.maximum(top, stats[d, 0])
+    whole = jnp.zeros_like(top)
+    score = jnp.zeros_like(top)
+    for d in range(8):
+        whole = whole + stats[d, 1] * jnp.exp(stats[d, 0] - top)
+        score = score + stats[d, 2]
+    norm = top + jnp.log(whole)
+    out_ref[0] = norm
+    out_ref[1] = score - norm
+
+
+def exchange_scratch(tiles, rows):
+    bf16 = jnp.bfloat16
+    return [
+        pltpu.VMEM((tiles, 2, 2, 2, rows, TILE), bf16),
+        pltpu.VMEM((tiles, 2, 2, rows, TILE), bf16),
+        pltpu.VMEM((tiles, 2, rows, HALF), bf16),
+        pltpu.VMEM((tiles, 2, rows, HALF), bf16),
+        pltpu.VMEM((tiles, rows, HALF), bf16),
+        pltpu.VMEM((tiles, rows, HALF), bf16),
+        pltpu.VMEM((rows, 128), jnp.float32),
+    ]
+
+
+def mlp_stage(attended, gain, hidden, w_o, gate_t, up_t):
+    count, dim = hidden.shape
+    tiles = dim // TILE
+    rows = count // 8
+    width = gate_t.shape[0]
+    blocks = pl.cdiv(width, 256)
+    padded = blocks * 256
+    vmem = pl.BlockSpec(memory_space=pltpu.VMEM)
+    anywhere = pl.BlockSpec(memory_space=pl.ANY)
+    bf16 = jnp.bfloat16
+    return pl.pallas_call(
+        mlp_kernel,
+        in_specs=[vmem, vmem, anywhere, anywhere, anywhere, anywhere],
+        out_specs=[vmem, vmem],
+        out_shape=[jax.ShapeDtypeStruct((count, padded), bf16), jax.ShapeDtypeStruct((tiles, rows, TILE), bf16)],
+        scratch_shapes=exchange_scratch(tiles, rows)
+        + [
+            pltpu.VMEM((2, w_o.shape[0], TILE), bf16),
+            pltpu.VMEM((tiles, rows, TILE), bf16),
+            pltpu.VMEM((2, padded, TILE), bf16),
+            pltpu.VMEM((2, padded, TILE), bf16),
+            pltpu.VMEM((blocks, count, 256), jnp.float32),
+            pltpu.VMEM((blocks, count, 256), jnp.float32),
+            pltpu.SemaphoreType.DMA((13,)),
+            pltpu.SemaphoreType.DMA((13, tiles)),
+            pltpu.SemaphoreType.DMA((2,)),
+            pltpu.SemaphoreType.DMA((2, 2)),
+            pltpu.SemaphoreType.DMA,
+            pltpu.SemaphoreType.REGULAR,
+        ],
+        compiler_params=pltpu.CompilerParams(collective_id=1, has_side_effects=True, vmem_limit_bytes=VMEM_MAX),
+        name="mlp_stage",
+    )(attended, gain, hidden, w_o, gate_t, up_t)
+
+
+def head_stage(product, gain, residual, score_id, w_down, head_t):
+    count, padded = product.shape
+    tiles, rows, _ = residual.shape
+    vocab = head_t.shape[0]
+    block = vocab // 5
+    vmem = pl.BlockSpec(memory_space=pltpu.VMEM)
+    anywhere = pl.BlockSpec(memory_space=pl.ANY)
+    bf16 = jnp.bfloat16
+    return pl.pallas_call(
+        head_kernel,
+        in_specs=[vmem, vmem, vmem, vmem, anywhere, anywhere],
+        out_specs=vmem,
+        out_shape=jax.ShapeDtypeStruct((2, 8, count // 8), jnp.float32),
+        scratch_shapes=[pltpu.VMEM((tiles, rows, TILE), bf16)]
+        + exchange_scratch(tiles, rows)
+        + [
+            pltpu.VMEM((2, padded, TILE), bf16),
+            pltpu.VMEM((2, vocab, TILE), bf16),
+            pltpu.VMEM((5, block, count), jnp.float32),
+            pltpu.VMEM((8, 3, 8, count // 8), jnp.float32),
+            pltpu.SemaphoreType.DMA((13,)),
+            pltpu.SemaphoreType.DMA((13, tiles)),
+            pltpu.SemaphoreType.DMA((2,)),
+            pltpu.SemaphoreType.DMA((2,)),
+            pltpu.SemaphoreType.DMA((7,)),
+            pltpu.SemaphoreType.DMA((7,)),
+            pltpu.SemaphoreType.REGULAR,
+        ],
+        compiler_params=pltpu.CompilerParams(collective_id=2, has_side_effects=True, vmem_limit_bytes=VMEM_MAX),
+        name="head_stage",
+    )(product, gain, residual, score_id, w_down, head_t)
 
 
 def rope_tables(positions, head_dim):
@@ -215,26 +633,11 @@
         k_out = jnp.transpose(k_out, (0, 2, 1, 3))
         v_out = jnp.transpose(v_out, (0, 2, 1, 3))
 
-        attn_sum = lax.psum(jnp.dot(attended, w_o, preferred_element_type=jnp.float32).astype(jnp.bfloat16), "tp")
-        residual = (flat.astype(jnp.float32) + attn_sum.astype(jnp.float32)).astype(jnp.bfloat16)
-        normed_mlp = rms_norm(residual, mlp_norm)
-        gate = jnp.dot(normed_mlp, w_gate, preferred_element_type=jnp.float32)
-        upper = jnp.dot(normed_mlp, w_up, preferred_element_type=jnp.float32)
-        product = (jax.nn.silu(gate) * upper).astype(jnp.bfloat16)
-        mlp_sum = lax.psum(jnp.dot(product, w_down, preferred_element_type=jnp.float32).astype(jnp.bfloat16), "tp")
-        layer_out = (residual.astype(jnp.float32) + mlp_sum.astype(jnp.float32)).astype(jnp.bfloat16)
-        logits = jnp.dot(rms_norm(layer_out, final_norm), w_lm, preferred_element_type=jnp.float32)
-        vocab_local = logits.shape[-1]
-        local_id = score_id.reshape(rows, 1) - lax.axis_index("tp") * vocab_local
-        top = jnp.max(logits, axis=-1)
-        part = jnp.sum(jnp.exp(logits - top[:, None]), axis=-1)
-        hit = lax.broadcasted_iota(jnp.int32, logits.shape, 1) == local_id
-        picked = jnp.sum(jnp.where(hit, logits, 0.0), axis=-1)
-        stats = lax.all_gather(jnp.stack([top, part, picked]), "tp")
-        global_top = jnp.max(stats[:, 0], axis=0)
-        total = jnp.sum(stats[:, 1] * jnp.exp(stats[:, 0] - global_top), axis=0)
-        log_norm = global_top + jnp.log(total)
-        log_prob = jnp.sum(stats[:, 2], axis=0) - log_norm
+        tiles = dim // TILE
+        product, residual = mlp_stage(attended, mlp_norm.reshape(tiles, 1, TILE), flat, w_o, w_gate.T, w_up.T)
+        scores = head_stage(product, final_norm.reshape(tiles, 1, TILE), residual, score_id.reshape(1, rows), w_down, w_lm.T)
+        log_norm = scores[0]
+        log_prob = scores[1]
         return log_norm.reshape(requests, nodes), log_prob.reshape(requests, nodes), k_out, v_out
 
     request_spec = P("dp", None, None)

time: 568 us -> 357 us (0.63); the launches traced: 559 us -> 356 us
  Pallas kernels: 77.1 us -> 345 us
  waiting for transfers between devices: 267 us -> 0 us
  matrix products: 145 us -> 0 us
  other arithmetic: 31.3 us -> 4 us
  between operations: 14.5 us -> 0.68 us
  blocking collectives: 11.2 us -> 0 us
  starting transfers between devices: 10.8 us -> 0 us
    pallas_call x0 -> x2, Pallas kernels: none -> 267 us  [the longest x1 138 us: head_stage(): pl.pallas_call(head_kernel, in_specs=[vmem, vmem, vmem, vmem, anywhere, a...]
    psum x2 -> x0, waiting for transfers between devices: 267 us -> none  [the longest x1 137 us: group_step(): lax.psum(jnp.dot(product, w_down, preferred_element_type=jnp.float32).ast...]
    dot_general x5 -> x0, matrix products: 145 us -> none  [the longest x1 55.2 us: group_step(): jnp.dot(rms_norm(layer_out, final_norm), w_lm, preferred_element_type=jnp...]
    reduce_sum x4 -> x0, other arithmetic: 26.6 us -> none  [the longest x2 18.6 us: rms_norm(): jnp.mean(widened * widened, axis=-1, keepdims=True) + RMS_EPS]
    all_gather x1 -> x0, blocking collectives: 11.2 us -> none  [group_step(): stats = lax.all_gather(jnp.stack([top, part, picked]), 'tp')]
    psum x2 -> x0, starting transfers between devices: 10.8 us -> none  [the longest x1 10.7 us: group_step(): lax.psum(jnp.dot(product, w_down, preferred_element_type=jnp.float32).ast...]
  transfers between devices with their start and end apart: 2 -> 0, of which waited for: 2 -> 0; matrix products, arithmetic and copies ran while one was open for 0% -> 0% of each run, Pallas kernels for 0% -> 0%
where the time goes in v2:
time: 357 us; the launch traced here: 356 us
  Pallas kernels  345 us (97%)
  local copies, waits for them, and re-layouts  6.71 us (2%)
  other arithmetic  4 us (1%)
    pallas_call x1, Pallas kernels, head_stage(): pl.pallas_call(head_kernel, in_specs=[vmem, vmem, vmem, vmem, anywhere, a...  138 us
    pallas_call x1, Pallas kernels, mlp_stage(): pl.pallas_call(mlp_kernel, in_specs=[vmem, vmem, anywhere, anywhere, anyw...  130 us
    pallas_call x1, Pallas kernels, attend(): pl.pallas_call(attend_kernel, grid_spec=pltpu.PrefetchScalarGridSpec(num_...  41.7 us
    pallas_call x1, Pallas kernels, project(): pl.pallas_call(qkv_kernel, grid=(rows // block,), in_specs=[pl.BlockSpec(...  35.6 us

profile of v2, /device:TPU:0, one launch (start us, length us, event | category | flops | bytes accessed | tf_op | source)
XLA Modules:
  0.0 356.1 jit_solution(14050562779768465084)
XLA Ops:
  0.6 0.8 add_convert_fusion
  1.4 0.1 convert_element_type.11
  1.5 1.9 fusion
  3.4 1.3 pad_maximum_fusion
  4.7 1.3 reshape.38.gain_ref
  6.0 35.6 %project.1 = (bf16[16,5,64,128]{3,2,1,0:T(8,128)(2,1)}, bf16[16,5,64,128]{3,2,1,0:T(8,128)(2,1)}, bf16[16,5,64,128]{3,2,1,0:T(8,128)(2,1)}) custom-call(bf16[1024,5120]{1,0:T(8,128)(2,1)} %bitcast.8, bf16[1,5120]{1,0:T(2,128)(2,1)} %reshape.38.gain_ref, f32[1024,128]{1,0:T(8,128)} %get-tuple-element.25.cos_ref, f32[1024,128]{1,0:T(8,128)} %get-tuple-element.26.sin_ref, ...), custom_call_target="tpu_custom_call" | custom-call | tf_op jit(solution)/shard_map/project/pallas_call | solution.py:50
  41.6 0.0 copy-start
  41.6 41.7 %attend.1 = (bf16[1024,640]{1,0:T(8,128)(2,1)}, bf16[512,5,16,128]{3,2,1,0:T(8,128)(2,1)}, bf16[512,5,16,128]{3,2,1,0:T(8,128)(2,1)}) custom-call(s32[16,32]{1,0:T(8,128)} %table_ref.1, s32[16]{0:T(128)} %ctx_ref.1, bf16[16,5,64,128]{3,2,1,0:T(8,128)(2,1)} %get-tuple-element.12.q_ref, bf16[16,5,64,128]{3,2,1,0:T(8,128)(2,1)} %get-tuple-element.13.kn_ref, ...), custom_call_target="tpu_custom_call" | custom-call | tf_op jit(solution)/shard_map/attend/pallas_call | solution.py:159
  83.3 0.0 copy-done
  83.3 0.6 reshape.42.gain_ref
  83.9 129.9 %mlp_stage.1 = (bf16[1024,1792]{1,0:T(8,128)(2,1)}, bf16[10,128,512]{2,1,0:T(8,128)(2,1)}) custom-call(bf16[1024,640]{1,0:T(8,128)(2,1)} %get-tuple-element.15.att_ref, bf16[10,1,512]{2,1,0:T(2,128)(2,1)} %reshape.42.gain_ref, bf16[1024,5120]{1,0:T(8,128)(2,1)} %bitcast.9, bf16[640,5120]{1,0:T(8,128)(2,1)} %wo_hbm.1, bf16[1728,5120]{1,0:T(8,128)(2,1)} %bitcast.11, ...), custom_call_target="tpu_custom_call" | custom-call | tf_op jit(solution)/shard_map/mlp_stage/pallas_call | solution.py:555
  213.9 1.3 reshape.43.gain_ref
  215.2 1.4 reshape.41.id_ref
  216.5 137.5 %head_stage.1 = f32[2,8,128]{2,1,0:T(8,128)} custom-call(bf16[1024,1792]{1,0:T(8,128)(2,1)} %get-tuple-element.16.prod_ref, bf16[10,1,512]{2,1,0:T(2,128)(2,1)} %reshape.43.gain_ref, bf16[10,128,512]{2,1,0:T(8,128)(2,1)} %get-tuple-element.17.res_ref, s32[1,1024]{1,0:T(1,128)} %reshape.41.id_ref, bf16[1728,5120]{1,0:T(8,128)(2,1)} %wd_hbm.1, ...), custom_call_target="tpu_custom_call" | custom-call | tf_op jit(solution)/shard_map/head_stage/pallas_call | solution.py:588
  354.1 0.7 fusion.1
  354.8 0.7 reshape_squeeze.6
  355.5 0.7 reshape_squeeze.7
  (1 shorter events, 0.0 us)
Async XLA Ops:
  41.6 41.7 %copy-start = (bf16[5120]{0:T(1024)(128)(2,1)S(1)}, bf16[5120]{0:T(1024)(128)(2,1)}, u32[]{:S(2)}) copy-start(bf16[5120]{0:T(1024)(128)(2,1)} %param.32) | copy-start | bytes 30724

commit v3 on v2

--- a/solution.py
+++ b/solution.py
@@ -22,7 +22,8 @@
     requests, heads, nodes, head_dim = q_ref.shape
     widened = hid_ref[...].astype(jnp.float32)
     scale = lax.rsqrt(jnp.mean(widened * widened, axis=-1, keepdims=True) + RMS_EPS)
-    normed = (widened * scale * gain_ref[...].astype(jnp.float32)).astype(jnp.bfloat16)
+    gain = gain_ref[...].reshape(1, widened.shape[1]).astype(jnp.float32)
+    normed = (widened * scale * gain).astype(jnp.bfloat16)
     cosine = cos_ref[...]
     sine = sin_ref[...]
 
@@ -52,7 +53,7 @@
         grid=(rows // block,),
         in_specs=[
             pl.BlockSpec((block, dim), lambda i: (i, 0)),
-            pl.BlockSpec((1, dim), lambda i: (0, 0)),
+            pl.BlockSpec((dim,), lambda i: (0,)),
             pl.BlockSpec((block, head_dim), lambda i: (i, 0)),
             pl.BlockSpec((block, head_dim), lambda i: (i, 0)),
             full,
@@ -69,31 +70,22 @@
 def attend_kernel(table_ref, ctx_ref, q_ref, kn_ref, vn_ref, mask_ref, kc_ref, vc_ref, out_ref, ko_ref, vo_ref, kbuf, vbuf, rsem, wsem):
     b = pl.program_id(0)
     count = pl.num_programs(0)
-    heads, span, head_dim = kbuf.shape[1:]
+    pages, heads, page, head_dim = kbuf.shape[1:]
+    span = pages * page
     nodes = q_ref.shape[2]
-    page = kc_ref.shape[2]
-    pages = span // page
     window = nodes + page
 
     def load(i, slot):
-        def one(s, _):
+        for s in range(pages):
             block = table_ref[i, s]
-            rows = pl.ds(pl.multiple_of(s * page, page), page)
-            pltpu.make_async_copy(kc_ref.at[block], kbuf.at[slot, :, rows], rsem.at[0, slot]).start()
-            pltpu.make_async_copy(vc_ref.at[block], vbuf.at[slot, :, rows], rsem.at[1, slot]).start()
-            return 0
-
-        lax.fori_loop(0, pages, one, 0)
+            pltpu.make_async_copy(kc_ref.at[block], kbuf.at[slot, s], rsem.at[0, slot]).start()
+            pltpu.make_async_copy(vc_ref.at[block], vbuf.at[slot, s], rsem.at[1, slot]).start()
 
     def save(i, slot):
-        def one(s, _):
+        for s in range(pages):
             block = table_ref[i, s]
-            rows = pl.ds(pl.multiple_of(s * page, page), page)
-            pltpu.make_async_copy(kbuf.at[slot, :, rows], ko_ref.at[block], wsem.at[0, slot]).start()
-            pltpu.make_async_copy(vbuf.at[slot, :, rows], vo_ref.at[block], wsem.at[1, slot]).start()
-            return 0
-
-        lax.fori_loop(0, pages, one, 0)
+            pltpu.make_async_copy(kbuf.at[slot, s], ko_ref.at[block], wsem.at[0, slot]).start()
+            pltpu.make_async_copy(vbuf.at[slot, s], vo_ref.at[block], wsem.at[1, slot]).start()
 
     def whole(slot, sem):
         pltpu.make_async_copy(kbuf.at[slot], kbuf.at[slot], sem.at[0, slot]).wait()
@@ -110,23 +102,23 @@
     def _():
         whole(after, wsem)
 
-    @pl.when(b + 1 < count)
-    def _():
-        load(b + 1, after)
-
     whole(slot, rsem)
+    load(jnp.minimum(b + 1, count - 1), after)
     ctx = ctx_ref[b]
-    base = pl.multiple_of(jnp.minimum((ctx // page) * page, span - window), page)
+    first = jnp.minimum(ctx // page, pages - window // page)
+    base = first * page
     row = base + lax.broadcasted_iota(jnp.int32, (window, nodes), 0)
     node = ctx + lax.broadcasted_iota(jnp.int32, (window, nodes), 1)
     place = jnp.where(row == node, 1.0, 0.0).astype(jnp.bfloat16)
     slot_id = base + lax.broadcasted_iota(jnp.int32, (window, head_dim), 0)
     fresh = (slot_id >= ctx) & (slot_id < ctx + nodes)
-    for h in range(heads):
-        for buf, new_ref in ((kbuf, kn_ref), (vbuf, vn_ref)):
-            moved = jnp.dot(place, new_ref[0, h], preferred_element_type=jnp.float32)
-            old = buf[slot, h, pl.ds(base, window), :]
-            buf[slot, h, pl.ds(base, window), :] = jnp.where(fresh, moved, old.astype(jnp.float32)).astype(jnp.bfloat16)
+    for buf, new_ref in ((kbuf, kn_ref), (vbuf, vn_ref)):
+        moved = [jnp.dot(place, new_ref[0, h], preferred_element_type=jnp.float32) for h in range(heads)]
+        for h in range(heads):
+            for i in range(window // page):
+                rows = slice(i * page, (i + 1) * page)
+                old = buf[slot, first + i, h].astype(jnp.float32)
+                buf[slot, first + i, h] = jnp.where(fresh[rows], moved[h][rows], old).astype(jnp.bfloat16)
     save(b, slot)
     spread = jnp.where(
         ctx + lax.broadcasted_iota(jnp.int32, (nodes, span), 0) == lax.broadcasted_iota(jnp.int32, (nodes, span), 1), 1.0, 0.0
@@ -135,25 +127,29 @@
     seen_new = jnp.dot(linked, spread, preferred_element_type=jnp.float32) > 0.5
     seen = seen_new | (lax.broadcasted_iota(jnp.int32, (nodes, span), 1) < ctx)
     scale = head_dim**-0.5
+    scores = [dot_nt(q_ref[0, h], kbuf[slot, :, h].reshape(span, head_dim)) for h in range(heads)]
+    scores = [jnp.where(seen, score * scale, -jnp.inf) for score in scores]
+    tops = [jnp.max(score, axis=-1, keepdims=True) for score in scores]
+    probs = [jnp.exp(score - top) for score, top in zip(scores, tops)]
+    totals = [jnp.sum(prob, axis=-1, keepdims=True) for prob in probs]
+    mixed = [
+        jnp.dot(prob.astype(jnp.bfloat16), vbuf[slot, :, h].reshape(span, head_dim), preferred_element_type=jnp.float32)
+        for h, prob in enumerate(probs)
+    ]
     for h in range(heads):
-        score = dot_nt(q_ref[0, h], kbuf[slot, h]) * scale
-        score = jnp.where(seen, score, -jnp.inf)
-        top = jnp.max(score, axis=-1, keepdims=True)
-        prob = jnp.exp(score - top)
-        total = jnp.sum(prob, axis=-1, keepdims=True)
-        mixed = jnp.dot(prob.astype(jnp.bfloat16), vbuf[slot, h], preferred_element_type=jnp.float32)
-        out_ref[:, h * head_dim : (h + 1) * head_dim] = (mixed / total).astype(jnp.bfloat16)
+        out_ref[:, h * head_dim : (h + 1) * head_dim] = (mixed[h] / totals[h]).astype(jnp.bfloat16)
 
     @pl.when(b == count - 1)
     def _():
         whole(lax.rem(b + 2, 3), wsem)
         whole(slot, wsem)
+        whole(after, rsem)
 
 
 def attend(table, ctx_len, query, key_new, val_new, tree_mask, k_cache, v_cache):
     requests, heads, nodes, head_dim = query.shape
     page = k_cache.shape[2]
-    span = table.shape[1] * page
+    pages = table.shape[1]
     node_spec = pl.BlockSpec((1, heads, nodes, head_dim), lambda b, *_: (b, 0, 0, 0))
     anywhere = pl.BlockSpec(memory_space=pl.ANY)
     return pl.pallas_call(
@@ -171,8 +167,8 @@
             ],
             out_specs=[pl.BlockSpec((nodes, heads * head_dim), lambda b, *_: (b, 0)), anywhere, anywhere],
             scratch_shapes=[
-                pltpu.VMEM((3, heads, span, head_dim), jnp.bfloat16),
-                pltpu.VMEM((3, heads, span, head_dim), jnp.bfloat16),
+                pltpu.VMEM((3, pages, heads, page, head_dim), jnp.bfloat16),
+                pltpu.VMEM((3, pages, heads, page, head_dim), jnp.bfloat16),
                 pltpu.SemaphoreType.DMA((2, 3)),
                 pltpu.SemaphoreType.DMA((2, 3)),
             ],
@@ -299,11 +295,10 @@
         pl.semaphore_signal(free, inc=1, device_id={"tp": target}, device_id_type=MESH)
     scale = lax.rsqrt(jnp.sum(ssq[...], axis=-1, keepdims=True) * (1.0 / (tiles * TILE)) + RMS_EPS)
 
-    def norm_step(t, _):
-        mbuf[t, y, x, core] = (h_ref[t].astype(jnp.float32) * scale * gain_ref[t].astype(jnp.float32)).astype(jnp.bfloat16)
-        return 0
-
-    lax.fori_loop(0, tiles, norm_step, 0)
+    for t in range(tiles):
+        gain = gain_ref[pl.ds(t * TILE, TILE)].reshape(1, TILE).astype(jnp.float32)
+        mbuf[t, y, x, core] = (h_ref[t].astype(jnp.float32) * scale * gain).astype(jnp.bfloat16)
+
     pl.semaphore_wait(free, 3)
 
     def own(t):
@@ -371,8 +366,8 @@
     tiles = mbuf.shape[0]
     rows = mbuf.shape[4]
     width = wg_hbm.shape[0]
-    blocks = acc_g.shape[0]
     padded = wg_buf.shape[1]
+    blocks = padded // 256
 
     def fetch(t):
         cols = pl.ds(pl.multiple_of(t * TILE, TILE), TILE)
@@ -404,22 +399,18 @@
     def idle_work(j):
         @pl.when(j < blocks)
         def _():
-            acc_g[j] = jnp.zeros(acc_g.shape[1:], jnp.float32)
-            acc_u[j] = jnp.zeros(acc_u.shape[1:], jnp.float32)
+            cols = pl.ds(pl.multiple_of(j * 256, 256), 256)
+            acc_g[:, cols] = jnp.zeros((8 * rows, 256), jnp.float32)
+            acc_u[:, cols] = jnp.zeros((8 * rows, 256), jnp.float32)
 
     def compute(t):
         slot = t % 2
         for copy in fetch(t):
             copy.wait()
 
-        def one(n, _):
-            cols = pl.ds(pl.multiple_of(n * 256, 256), 256)
-            left = mbuf[t].reshape(8 * rows, TILE)
-            acc_g[n] += dot_nt(left, wg_buf[slot, cols])
-            acc_u[n] += dot_nt(left, wu_buf[slot, cols])
-            return 0
-
-        lax.fori_loop(0, blocks, one, 0)
+        left = mbuf[t].reshape(8 * rows, TILE)
+        acc_g[...] += dot_nt(left, wg_buf[slot])
+        acc_u[...] += dot_nt(left, wu_buf[slot])
 
         @pl.when(t + 2 < tiles)
         def _():
@@ -430,13 +421,13 @@
 
     def finish(n, _):
         cols = pl.ds(pl.multiple_of(n * 256, 256), 256)
-        prod_ref[:, cols] = (jax.nn.silu(acc_g[n]) * acc_u[n]).astype(jnp.bfloat16)
+        prod_ref[:, cols] = (jax.nn.silu(acc_g[:, cols]) * acc_u[:, cols]).astype(jnp.bfloat16)
         return 0
 
     lax.fori_loop(0, blocks, finish, 0)
 
 
-def head_kernel(prod_ref, gain_ref, res_ref, id_ref, wd_hbm, wl_hbm, out_ref, h_ref, mbuf, r1, rx, ry, r2x, r2y, ssq, wd_buf, wl_buf, acc, stats, ssem, rsem, wsem, lsem, tsem, usem, free):
+def head_kernel(prod_ref, gain_ref, res_ref, id_ref, wd_hbm, wl_hbm, norm_ref, prob_ref, h_ref, mbuf, r1, rx, ry, r2x, r2y, ssq, wd_buf, wl_buf, acc, stats, ssem, rsem, wsem, lsem, tsem, usem, free):
     me, core, x, y, to_x, to_y, to_pair = seat()
     tiles = mbuf.shape[0]
     rows = mbuf.shape[4]
@@ -488,7 +479,7 @@
 
     best = lax.fori_loop(0, blocks, top_step, jnp.full((8, count), -jnp.inf, jnp.float32))
     best = jnp.max(best, axis=0, keepdims=True)
-    local_id = id_ref[...] - me * vocab
+    local_id = jnp.concatenate([id_ref[i : i + 1] for i in range(id_ref.shape[0])], axis=1) - me * vocab
 
     def sum_step(n, carry):
         total, picked = carry
@@ -525,8 +516,11 @@
         whole = whole + stats[d, 1] * jnp.exp(stats[d, 0] - top)
         score = score + stats[d, 2]
     norm = top + jnp.log(whole)
-    out_ref[0] = norm
-    out_ref[1] = score - norm
+    for ref, values in ((norm_ref, norm), (prob_ref, score - norm)):
+        nodes = ref.shape[1]
+        for i in range(ref.shape[0]):
+            start = i * nodes
+            ref[i : i + 1] = values[start // 128 : start // 128 + 1, start % 128 : start % 128 + nodes]
 
 
 def exchange_scratch(tiles, rows):
@@ -563,8 +557,8 @@
             pltpu.VMEM((tiles, rows, TILE), bf16),
             pltpu.VMEM((2, padded, TILE), bf16),
             pltpu.VMEM((2, padded, TILE), bf16),
-            pltpu.VMEM((blocks, count, 256), jnp.float32),
-            pltpu.VMEM((blocks, count, 256), jnp.float32),
+            pltpu.VMEM((count, padded), jnp.float32),
+            pltpu.VMEM((count, padded), jnp.float32),
             pltpu.SemaphoreType.DMA((13,)),
             pltpu.SemaphoreType.DMA((13, tiles)),
             pltpu.SemaphoreType.DMA((2,)),
@@ -581,21 +575,21 @@
     count, padded = product.shape
     tiles, rows, _ = residual.shape
     vocab = head_t.shape[0]
-    block = vocab // 5
+    block = vocab // 2
     vmem = pl.BlockSpec(memory_space=pltpu.VMEM)
     anywhere = pl.BlockSpec(memory_space=pl.ANY)
     bf16 = jnp.bfloat16
     return pl.pallas_call(
         head_kernel,
         in_specs=[vmem, vmem, vmem, vmem, anywhere, anywhere],
-        out_specs=vmem,
-        out_shape=jax.ShapeDtypeStruct((2, 8, count // 8), jnp.float32),
+        out_specs=[vmem, vmem],
+        out_shape=[jax.ShapeDtypeStruct(score_id.shape, jnp.float32)] * 2,
         scratch_shapes=[pltpu.VMEM((tiles, rows, TILE), bf16)]
         + exchange_scratch(tiles, rows)
         + [
             pltpu.VMEM((2, padded, TILE), bf16),
             pltpu.VMEM((2, vocab, TILE), bf16),
-            pltpu.VMEM((5, block, count), jnp.float32),
+            pltpu.VMEM((2, block, count), jnp.float32),
             pltpu.VMEM((8, 3, 8, count // 8), jnp.float32),
             pltpu.SemaphoreType.DMA((13,)),
             pltpu.SemaphoreType.DMA((13, tiles)),
@@ -612,11 +606,10 @@
 
 def rope_tables(positions, head_dim):
     half = head_dim // 2
-    inv_freq = 1.0 / (ROPE_THETA ** (jnp.arange(half, dtype=jnp.float32) * (2.0 / head_dim)))
+    lane = jnp.arange(head_dim, dtype=jnp.int32)
+    inv_freq = 1.0 / (ROPE_THETA ** ((lane % half).astype(jnp.float32) * (2.0 / head_dim)))
     angles = positions.astype(jnp.float32)[:, None] * inv_freq
-    cosine = jnp.cos(angles)
-    sine = jnp.sin(angles)
-    return jnp.concatenate([cosine, cosine], axis=-1), jnp.concatenate([-sine, sine], axis=-1)
+    return jnp.cos(angles), jnp.sin(angles) * jnp.where(lane < half, -1.0, 1.0)
 
 
 def solution(mesh):
@@ -626,18 +619,15 @@
         rows = requests * nodes
         flat = hidden.reshape(rows, dim)
         cosine, sine = rope_tables((ctx_len[:, None] + depth).reshape(rows), head_dim)
-        query, key_new, val_new = project(flat, attn_norm.reshape(1, dim), cosine, sine, w_q, w_k, w_v, requests, nodes, head_dim, 4)
+        query, key_new, val_new = project(flat, attn_norm, cosine, sine, w_q, w_k, w_v, requests, nodes, head_dim, 4)
         attended, k_out, v_out = attend(
             block_table, ctx_len, query, key_new, val_new, tree_mask, jnp.transpose(k_cache, (0, 2, 1, 3)), jnp.transpose(v_cache, (0, 2, 1, 3))
         )
         k_out = jnp.transpose(k_out, (0, 2, 1, 3))
         v_out = jnp.transpose(v_out, (0, 2, 1, 3))
 
-        tiles = dim // TILE
-        product, residual = mlp_stage(attended, mlp_norm.reshape(tiles, 1, TILE), flat, w_o, w_gate.T, w_up.T)
-        scores = head_stage(product, final_norm.reshape(tiles, 1, TILE), residual, score_id.reshape(1, rows), w_down, w_lm.T)
-        log_norm = scores[0]
-        log_prob = scores[1]
+        product, residual = mlp_stage(attended, mlp_norm, flat, w_o, w_gate.T, w_up.T)
+        log_norm, log_prob = head_stage(product, final_norm, residual, score_id, w_down, w_lm.T)
         return log_norm.reshape(requests, nodes), log_prob.reshape(requests, nodes), k_out, v_out
 
     request_spec = P("dp", None, None)

time: 357 us -> 327 us (0.916)
  Pallas kernels: 345 us -> 319 us
  local copies, waits for them, and re-layouts: 6.71 us -> 2.66 us
    pallas_call x1, Pallas kernels: 41.7 us -> 24.6 us  [attend(): pl.pallas_call(attend_kernel, grid_spec=pltpu.PrefetchScalarGridSpec(num_...]
    pallas_call x1, Pallas kernels: 130 us -> 124 us  [mlp_stage(): pl.pallas_call(mlp_kernel, in_specs=[vmem, vmem, anywhere, anywhere, anyw...]
    reshape x4 -> x0, local copies, waits for them, and re-layouts: 4.62 us -> none  [the longest x1 1.36 us: group_step(): score_id.reshape(1, rows)]
where the time goes in v3:
time: 327 us; the launch traced here: 326 us
  Pallas kernels  319 us (98%)
  other arithmetic  3.83 us (1%)
    pallas_call x1, Pallas kernels, head_stage(): pl.pallas_call(head_kernel, in_specs=[vmem, vmem, vmem, vmem, anywhere, a...  135 us
    pallas_call x1, Pallas kernels, mlp_stage(): pl.pallas_call(mlp_kernel, in_specs=[vmem, vmem, anywhere, anywhere, anyw...  124 us
    pallas_call x1, Pallas kernels, project(): pl.pallas_call(qkv_kernel, grid=(rows // block,), in_specs=[pl.BlockSpec(...  35.6 us
    pallas_call x1, Pallas kernels, attend(): pl.pallas_call(attend_kernel, grid_spec=pltpu.PrefetchScalarGridSpec(num_...  24.6 us

profile of v3, /device:TPU:0, one launch (start us, length us, event | category | flops | bytes accessed | tf_op | source)
XLA Modules:
  0.0 325.7 jit_solution(14147191270261551007)
XLA Ops:
  0.6 0.8 add_convert_fusion
  1.4 0.1 convert_element_type.18
  1.5 3.0 fusion
  4.5 35.6 %project.1 = (bf16[16,5,64,128]{3,2,1,0:T(8,128)(2,1)}, bf16[16,5,64,128]{3,2,1,0:T(8,128)(2,1)}, bf16[16,5,64,128]{3,2,1,0:T(8,128)(2,1)}) custom-call(bf16[1024,5120]{1,0:T(8,128)(2,1)} %bitcast.8, bf16[5120]{0:T(1024)(128)(2,1)} %gain_ref.3, f32[1024,128]{1,0:T(8,128)} %get-tuple-element.25.cos_ref, f32[1024,128]{1,0:T(8,128)} %get-tuple-element.24.sin_ref, ...), custom_call_target="tpu_custom_call" | custom-call | tf_op jit(solution)/shard_map/project/pallas_call | solution.py:51
  40.1 24.6 %attend.1 = (bf16[1024,640]{1,0:T(8,128)(2,1)}, bf16[512,5,16,128]{3,2,1,0:T(8,128)(2,1)}, bf16[512,5,16,128]{3,2,1,0:T(8,128)(2,1)}) custom-call(s32[16,32]{1,0:T(8,128)} %table_ref.1, s32[16]{0:T(128)} %ctx_ref.1, bf16[16,5,64,128]{3,2,1,0:T(8,128)(2,1)} %get-tuple-element.14.q_ref, bf16[16,5,64,128]{3,2,1,0:T(8,128)(2,1)} %get-tuple-element.15.kn_ref, ...), custom_call_target="tpu_custom_call" | custom-call | tf_op jit(solution)/shard_map/attend/pallas_call | solution.py:155
  64.8 123.6 %mlp_stage.1 = (bf16[1024,1792]{1,0:T(8,128)(2,1)}, bf16[10,128,512]{2,1,0:T(8,128)(2,1)}) custom-call(bf16[1024,640]{1,0:T(8,128)(2,1)} %get-tuple-element.17.att_ref, bf16[5120]{0:T(1024)(128)(2,1)} %gain_ref.4, bf16[1024,5120]{1,0:T(8,128)(2,1)} %bitcast.9, bf16[640,5120]{1,0:T(8,128)(2,1)} %wo_hbm.1, bf16[1728,5120]{1,0:T(8,128)(2,1)} %bitcast.11, ...), custom_call_target="tpu_custom_call" | custom-call | tf_op jit(solution)/shard_map/mlp_stage/pallas_call | solution.py:549
  188.4 134.7 %head_stage.1 = (f32[16,64]{1,0:T(8,128)}, f32[16,64]{1,0:T(8,128)}) custom-call(bf16[1024,1792]{1,0:T(8,128)(2,1)} %get-tuple-element.18.prod_ref, bf16[5120]{0:T(1024)(128)(2,1)} %gain_ref.5, bf16[10,128,512]{2,1,0:T(8,128)(2,1)} %get-tuple-element.19.res_ref, s32[16,64]{1,0:T(8,128)} %id_ref.1, bf16[1728,5120]{1,0:T(8,128)(2,1)} %wd_hbm.1, ...), custom_call_target="tpu_custom_call" | custom-call | tf_op jit(solution)/shard_map/head_stage/pallas_call | solution.py:582
  323.1 1.3 copy.25
  324.4 1.3 copy.26
  (1 shorter events, 0.0 us)

commit v4 on v3

v4 whole, which is shorter than its diff:
```python
import jax
import jax.numpy as jnp
from jax import lax
from jax.experimental import pallas as pl
from jax.experimental.pallas import tpu as pltpu
from jax.sharding import PartitionSpec as P

RMS_EPS = 1e-5
ROPE_THETA = 500000
MESH = pl.DeviceIdType.MESH
NT_DIMS = (((1,), (1,)), ((), ()))
VMEM_MAX = 67043328


def dot_nt(left, right):
    return lax.dot_general(left, right, NT_DIMS, preferred_element_type=jnp.float32)


def qkv_kernel(hid_ref, gain_ref, cos_ref, sin_ref, wq_ref, wk_ref, wv_ref, q_ref, k_ref, v_ref):
    requests, heads, nodes, head_dim = q_ref.shape
    widened = hid_ref[...].astype(jnp.float32)
    scale = lax.rsqrt(jnp.mean(widened * widened, axis=-1, keepdims=True) + RMS_EPS)
    gain = gain_ref[...].reshape(1, widened.shape[1]).astype(jnp.float32)
    normed = (widened * scale * gain).astype(jnp.bfloat16)
    cosine = cos_ref[...]
    sine = sin_ref[...]

    def put(out_ref, weight_ref, turned):
        product = jnp.dot(normed, weight_ref[...], preferred_element_type=jnp.float32)
        for h in range(heads):
            part = product[:, h * head_dim : (h + 1) * head_dim]
            if turned:
                part = part * cosine + pltpu.roll(part, head_dim // 2, 1) * sine
            out_ref[:, h] = part.astype(jnp.bfloat16).reshape(requests, nodes, head_dim)

    put(q_ref, wq_ref, True)
    put(k_ref, wk_ref, True)
    put(v_ref, wv_ref, False)


def project(hidden, gain, cosine, sine, w_q, w_k, w_v, requests, nodes, head_dim, group):
    rows, dim = hidden.shape
    cols = w_q.shape[1]
    heads = cols // head_dim
    block = group * nodes
    full = pl.BlockSpec((dim, cols), lambda i: (0, 0), pipeline_mode=pl.Buffered(1))
    out = pl.BlockSpec((group, heads, nodes, head_dim), lambda i: (i, 0, 0, 0))
    shape = jax.ShapeDtypeStruct((requests, heads, nodes, head_dim), jnp.bfloat16)
    return pl.pallas_call(
        qkv_kernel,
        grid=(rows // block,),
        in_specs=[
            pl.BlockSpec((block, dim), lambda i: (i, 0)),
            pl.BlockSpec((dim,), lambda i: (0,)),
            pl.BlockSpec((block, head_dim), lambda i: (i, 0)),
            pl.BlockSpec((block, head_dim), lambda i: (i, 0)),
            full,
            full,
            full,
        ],
        out_specs=[out, out, out],
        out_shape=[shape, shape, shape],
        compiler_params=pltpu.CompilerParams(vmem_limit_bytes=VMEM_MAX),
        name="project",
    )(hidden, gain, cosine, sine, w_q, w_k, w_v)


def attend_kernel(table_ref, ctx_ref, q_ref, kn_ref, vn_ref, mask_ref, kc_ref, vc_ref, out_ref, ko_ref, vo_ref, kbuf, vbuf, rsem, wsem):
    b = pl.program_id(0)
    count = pl.num_programs(0)
    pages, heads, page, head_dim = kbuf.shape[1:]
    span = pages * page
    nodes = q_ref.shape[2]
    window = nodes + page

    def load(i, slot):
        for s in range(pages):
            block = table_ref[i, s]
            pltpu.make_async_copy(kc_ref.at[block], kbuf.at[slot, s], rsem.at[0, slot]).start()
            pltpu.make_async_copy(vc_ref.at[block], vbuf.at[slot, s], rsem.at[1, slot]).start()

    def save(i, slot):
        for s in range(pages):
            block = table_ref[i, s]
            pltpu.make_async_copy(kbuf.at[slot, s], ko_ref.at[block], wsem.at[0, slot]).start()
            pltpu.make_async_copy(vbuf.at[slot, s], vo_ref.at[block], wsem.at[1, slot]).start()

    def whole(slot, sem):
        pltpu.make_async_copy(kbuf.at[slot], kbuf.at[slot], sem.at[0, slot]).wait()
        pltpu.make_async_copy(vbuf.at[slot], vbuf.at[slot], sem.at[1, slot]).wait()

    slot = lax.rem(b, 3)
    after = lax.rem(b + 1, 3)

    @pl.when(b == 0)
    def _():
        load(0, 0)

    @pl.when(b >= 2)
    def _():
        whole(after, wsem)

    whole(slot, rsem)
    load(jnp.minimum(b + 1, count - 1), after)
    ctx = ctx_ref[b]
    first = jnp.minimum(ctx // page, pages - window // page)
    base = first * page
    row = base + lax.broadcasted_iota(jnp.int32, (window, nodes), 0)
    node = ctx + lax.broadcasted_iota(jnp.int32, (window, nodes), 1)
    place = jnp.where(row == node, 1.0, 0.0).astype(jnp.bfloat16)
    slot_id = base + lax.broadcasted_iota(jnp.int32, (window, head_dim), 0)
    fresh = (slot_id >= ctx) & (slot_id < ctx + nodes)
    for buf, new_ref in ((kbuf, kn_ref), (vbuf, vn_ref)):
        moved = [jnp.dot(place, new_ref[0, h], preferred_element_type=jnp.float32) for h in range(heads)]
        for h in range(heads):
            for i in range(window // page):
                rows = slice(i * page, (i + 1) * page)
                old = buf[slot, first + i, h].astype(jnp.float32)
                buf[slot, first + i, h] = jnp.where(fresh[rows], moved[h][rows], old).astype(jnp.bfloat16)
    save(b, slot)
    spread = jnp.where(
        ctx + lax.broadcasted_iota(jnp.int32, (nodes, span), 0) == lax.broadcasted_iota(jnp.int32, (nodes, span), 1), 1.0, 0.0
    ).astype(jnp.bfloat16)
    linked = jnp.where(mask_ref[0] > 0, 1.0, 0.0).astype(jnp.bfloat16)
    seen_new = jnp.dot(linked, spread, preferred_element_type=jnp.float32) > 0.5
    seen = seen_new | (lax.broadcasted_iota(jnp.int32, (nodes, span), 1) < ctx)
    scale = head_dim**-0.5
    scores = [dot_nt(q_ref[0, h], kbuf[slot, :, h].reshape(span, head_dim)) for h in range(heads)]
    scores = [jnp.where(seen, score * scale, -jnp.inf) for score in scores]
    tops = [jnp.max(score, axis=-1, keepdims=True) for score in scores]
    probs = [jnp.exp(score - top) for score, top in zip(scores, tops)]
    totals = [jnp.sum(prob, axis=-1, keepdims=True) for prob in probs]
    mixed = [
        jnp.dot(prob.astype(jnp.bfloat16), vbuf[slot, :, h].reshape(span, head_dim), preferred_element_type=jnp.float32)
        for h, prob in enumerate(probs)
    ]
    for h in range(heads):
        out_ref[:, h * head_dim : (h + 1) * head_dim] = (mixed[h] / totals[h]).astype(jnp.bfloat16)

    @pl.when(b == count - 1)
    def _():
        whole(lax.rem(b + 2, 3), wsem)
        whole(slot, wsem)
        whole(after, rsem)


def attend(table, ctx_len, query, key_new, val_new, tree_mask, k_cache, v_cache):
    requests, heads, nodes, head_dim = query.shape
    page = k_cache.shape[2]
    pages = table.shape[1]
    node_spec = pl.BlockSpec((1, heads, nodes, head_dim), lambda b, *_: (b, 0, 0, 0))
    anywhere = pl.BlockSpec(memory_space=pl.ANY)
    return pl.pallas_call(
        attend_kernel,
        grid_spec=pltpu.PrefetchScalarGridSpec(
            num_scalar_prefetch=2,
            grid=(requests,),
            in_specs=[
                node_spec,
                node_spec,
                node_spec,
                pl.BlockSpec((1, nodes, nodes), lambda b, *_: (b, 0, 0)),
                anywhere,
                anywhere,
            ],
            out_specs=[pl.BlockSpec((nodes, heads * head_dim), lambda b, *_: (b, 0)), anywhere, anywhere],
            scratch_shapes=[
                pltpu.VMEM((3, pages, heads, page, head_dim), jnp.bfloat16),
                pltpu.VMEM((3, pages, heads, page, head_dim), jnp.bfloat16),
                pltpu.SemaphoreType.DMA((2, 3)),
                pltpu.SemaphoreType.DMA((2, 3)),
            ],
        ),
        out_shape=[
            jax.ShapeDtypeStruct((requests * nodes, heads * head_dim), jnp.bfloat16),
            jax.ShapeDtypeStruct(k_cache.shape, k_cache.dtype),
            jax.ShapeDtypeStruct(v_cache.shape, v_cache.dtype),
        ],
        name="attend",
    )(table, ctx_len, query, key_new, val_new, tree_mask, k_cache, v_cache)


TILE = 512
HALF = TILE // 2
PAIR, X1, Y1, X2, Y2, GX, GY, GP, FX, FY, PX, PY, PD = range(13)


def seat():
    me = lax.axis_index("tp")
    core = me % 2
    x = (me // 2) % 2
    y = me // 4
    blocks = []
    for dy in range(2):
        for dx in range(2):
            for dc in range(2):
                blocks.append((1 - y if dy else y) * 4 + (1 - x if dx else x) * 2 + (1 - core if dc else core))
    return me, blocks


def landed(ref, rsem, kind, t):
    pltpu.make_async_copy(ref, ref, rsem.at[kind, t]).wait()


def sent(ref, ssem, kind):
    pltpu.make_async_copy(ref, ref, ssem.at[kind]).wait()


def reduce_norm_gather(left_ref, fetch, wbuf, depth, resid_ref, resid_ready, gain_ref, h_ref, mbuf, bufs, ssem, rsem, free, idle_work, gather_work, pre, rest):
    r1, rx, ry, r2x, r2y, ssq = bufs
    _, blocks = seat()
    to_pair, to_x, to_y = blocks[1], blocks[2], blocks[4]
    tiles = mbuf.shape[0]
    rows = mbuf.shape[4]
    low = pl.ds(0, HALF)
    high = pl.ds(HALF, HALF)

    def send(src, dst, kind, t, target):
        pltpu.make_async_remote_copy(
            src_ref=src, dst_ref=dst, send_sem=ssem.at[kind], recv_sem=rsem.at[kind, t], device_id={"tp": target}, device_id_type=MESH
        ).start()

    def scatter_step(j, _):
        @pl.when(j < tiles)
        def _():
            fetch(j).wait()
            for half in range(2):
                cols = pl.ds(half * HALF, HALF)
                part = jnp.dot(left_ref[...].reshape(8 * rows, depth), wbuf[j % 2, pl.ds(0, depth), cols], preferred_element_type=jnp.float32)
                mbuf[j, :, :, :, :, cols] = part.astype(jnp.bfloat16).reshape(2, 2, 2, rows, HALF)

            @pl.when(j + 2 < tiles)
            def _():
                fetch(j + 2).start()

            send(mbuf.at[j, :, :, 1], r1.at[j], PAIR, j, to_pair)
            idle_work(j)

        @pl.when((j >= 1) & (j < tiles + 1))
        def _():
            t = j - 1
            landed(r1.at[t], rsem, PAIR, t)
            mbuf[t, :, :, 0] = mbuf[t, :, :, 0] + r1[t]
            send(mbuf.at[t, :, 1, 0, :, low], rx.at[t], X1, t, to_x)
            send(mbuf.at[t, 1, :, 0, :, high], ry.at[t], Y1, t, to_y)

        @pl.when((j >= 2) & (j < tiles + 2))
        def _():
            t = j - 2
            landed(rx.at[t], rsem, X1, t)
            mbuf[t, :, 0, 0, :, low] = mbuf[t, :, 0, 0, :, low] + rx[t]
            send(mbuf.at[t, 1, 0, 0, :, low], r2y.at[t], Y2, t, to_y)
            landed(ry.at[t], rsem, Y1, t)
            mbuf[t, 0, :, 0, :, high] = mbuf[t, 0, :, 0, :, high] + ry[t]
            send(mbuf.at[t, 0, 1, 0, :, high], r2x.at[t], X2, t, to_x)

        @pl.when(j == 3)
        def _():
            resid_ready()
            ssq[...] = jnp.zeros_like(ssq)

        @pl.when(j >= 3)
        def _():
            t = j - 3
            landed(r2y.at[t], rsem, Y2, t)
            landed(r2x.at[t], rsem, X2, t)
            for cols, other in ((low, r2y), (high, r2x)):
                total = (mbuf[t, 0, 0, 0, :, cols] + other[t]).astype(jnp.float32)
                new = (resid_ref[t, :, cols].astype(jnp.float32) + total).astype(jnp.bfloat16)
                h_ref[t, :, cols] = new
                wide = new.astype(jnp.float32)
                wide = wide * wide
                ssq[...] += sum(wide[:, lane : lane + 128] for lane in range(0, HALF, 128))

        return 0

    lax.fori_loop(0, tiles + 3, scatter_step, 0)
    sent(r1, ssem, PAIR)
    sent(rx, ssem, X1)
    sent(ry, ssem, Y1)
    sent(r2x, ssem, X2)
    sent(r2y, ssem, Y2)
    for target in (to_x, to_y, to_pair):
        pl.semaphore_signal(free, inc=1, device_id={"tp": target}, device_id_type=MESH)
    scale = lax.rsqrt(jnp.sum(ssq[...], axis=-1, keepdims=True) * (1.0 / (tiles * TILE)) + RMS_EPS)
    for t in range(tiles):
        gain = gain_ref[pl.ds(t * TILE, TILE)].reshape(1, TILE).astype(jnp.float32)
        mbuf[t, 0, 0, 0] = (h_ref[t].astype(jnp.float32) * scale * gain).astype(jnp.bfloat16)
    pl.semaphore_wait(free, 3)

    def own(t):
        mine = mbuf.at[t, 0, 0, 0]
        send(mine, mbuf.at[t, 0, 1, 0], GX, t, to_x)
        send(mine, mbuf.at[t, 1, 0, 0], GY, t, to_y)

    own(0)
    own(1)

    def own_pair(t, _):
        send(mbuf.at[t, 0, 0, 0], mbuf.at[t, 0, 0, 1], GP, t, to_pair)
        return 0

    lax.fori_loop(0, tiles, own_pair, 0)
    gather_work()

    def pre_step(t, _):
        landed(mbuf.at[t, 0, 0, 1], rsem, GP, t)
        pre(t)
        return 0

    def gather_step(j, _):
        @pl.when(j < 3)
        def _():
            lax.fori_loop(j * 3 + (j + 2) // 3, j * 3 + 4, pre_step, 0)

        @pl.when(j + 2 < tiles)
        def _():
            own(j + 2)

        @pl.when(j < tiles)
        def _():
            upper = pl.ds(0, rows // 2)
            lower = pl.ds(rows // 2, rows // 2)
            landed(mbuf.at[j, 0, 1, 0], rsem, GX, j)
            send(mbuf.at[j, 0, 1, 0, upper], mbuf.at[j, 1, 1, 0, upper], FY, j, to_y)
            send(mbuf.at[j, 0, 1, 0], mbuf.at[j, 0, 1, 1], PX, j, to_pair)
            landed(mbuf.at[j, 1, 0, 0], rsem, GY, j)
            send(mbuf.at[j, 1, 0, 0, lower], mbuf.at[j, 1, 1, 0, lower], FX, j, to_x)
            send(mbuf.at[j, 1, 0, 0], mbuf.at[j, 1, 0, 1], PY, j, to_pair)

        @pl.when((j >= 1) & (j < tiles + 1))
        def _():
            t = j - 1
            landed(mbuf.at[t, 1, 1, 0, pl.ds(0, rows // 2)], rsem, FY, t)
            landed(mbuf.at[t, 1, 1, 0, pl.ds(rows // 2, rows // 2)], rsem, FX, t)
            send(mbuf.at[t, 1, 1, 0], mbuf.at[t, 1, 1, 1], PD, t, to_pair)

        @pl.when(j >= 2)
        def _():
            t = j - 2
            landed(mbuf.at[t, 0, 1, 1], rsem, PX, t)
            landed(mbuf.at[t, 1, 0, 1], rsem, PY, t)
            landed(mbuf.at[t, 1, 1, 1], rsem, PD, t)
            rest(t)

        return 0

    lax.fori_loop(0, tiles + 2, gather_step, 0)
    for kind in (GX, GY, GP, PX, PY, PD):
        sent(h_ref, ssem, kind)
    for kind in (FX, FY):
        sent(h_ref.at[pl.ds(0, tiles // 2)], ssem, kind)


def tail_kernel(mlp_gain, final_gain, id_ref, att_hbm, hid_hbm, wo_hbm, wg_hbm, wu_hbm, wd_hbm, wl_hbm, norm_ref, prob_ref, mbuf, r1, rx, ry, r2x, r2y, ssq, left, prod, resid, h_buf, wbuf, nbuf, acc, stats, ssem, rsem, wsem, nsem, isem, tsem, usem, free):
    me, blocks = seat()
    tiles = mbuf.shape[0]
    rows = mbuf.shape[4]
    count = 8 * rows
    heads_width = left.shape[2]
    width = wg_hbm.shape[0]
    padded = wbuf.shape[1]
    vocab = wl_hbm.shape[0]
    parts = acc.shape[0]
    side = acc.shape[1]
    piece = pl.cdiv(vocab, parts * 16) * 16
    pieces = [(n * piece, min(piece, vocab - n * piece)) for n in range(parts)]
    others = [(me + i) % 8 for i in range(1, 8)]

    def columns(t):
        return pl.ds(pl.multiple_of(t * TILE, TILE), TILE)

    def fetch_o(t):
        return pltpu.make_async_copy(wo_hbm.at[:, columns(t)], wbuf.at[t % 2, pl.ds(0, heads_width)], wsem.at[t % 2])

    def fetch_d(t):
        return pltpu.make_async_copy(wd_hbm.at[:, columns(t)], wbuf.at[t % 2, pl.ds(0, width)], wsem.at[t % 2])

    def fetch_in(i):
        t = i % tiles
        slot = i % 2
        return (
            pltpu.make_async_copy(wg_hbm.at[:, columns(t)], nbuf.at[slot, pl.ds(0, width)], nsem.at[0, slot]),
            pltpu.make_async_copy(wu_hbm.at[:, columns(t)], nbuf.at[slot, pl.ds(padded, width)], nsem.at[1, slot]),
        )

    def fetch_l(i):
        slot = i % 2
        return (pltpu.make_async_copy(wl_hbm.at[:, columns(i % tiles)], nbuf.at[slot, pl.ds(0, vocab)], nsem.at[0, slot]),)

    fetch_o(0).start()
    for k, block in enumerate(blocks):
        pltpu.make_async_copy(att_hbm.at[pl.ds(pl.multiple_of(block * rows, rows), rows)], left.at[k], isem.at[0]).start()
    fetch_o(1).start()
    barrier = pltpu.get_barrier_semaphore()
    for other in others:
        pl.semaphore_signal(barrier, inc=1, device_id={"tp": other}, device_id_type=MESH)
    pl.semaphore_wait(barrier, 7)
    for t in range(tiles):
        pltpu.make_async_copy(hid_hbm.at[pl.ds(pl.multiple_of(me * rows, rows), rows), pl.ds(t * TILE, TILE)], resid.at[t], isem.at[1]).start()
    pltpu.make_async_copy(left, left, isem.at[0]).wait()

    def resid_ready():
        pltpu.make_async_copy(resid, resid, isem.at[1]).wait()

    def clear(j):
        @pl.when(j < parts)
        def _():
            acc[j] = jnp.zeros(acc.shape[1:], jnp.float32)

    def idle_in(j):
        clear(j)

        @pl.when(j == 4)
        def _():
            for slot in range(2):
                gap = jnp.zeros((padded - width, TILE), jnp.bfloat16)
                wbuf[slot, pl.ds(width, padded - width)] = gap
                nbuf[slot, pl.ds(width, padded - width)] = gap
                nbuf[slot, pl.ds(padded + width, padded - width)] = gap
                for copy in fetch_in(slot):
                    copy.start()

    def gather_in():
        fetch_d(0).start()
        fetch_d(1).start()

    def streamed(fetch, i, work):
        for copy in fetch(i):
            copy.wait()
        work(i % 2)

        @pl.when(i + 2 < 2 * tiles)
        def _():
            for copy in fetch(i + 2):
                copy.start()

    def in_part(slot, left_rows, some):
        for half in range(2):
            for n in range(2):
                wide = min(side, padded - n * side)
                weights = nbuf[slot, pl.ds(half * padded + n * side, wide)]
                acc[half * 2 + n, some, pl.ds(0, wide)] += dot_nt(left_rows, weights)

    def pre_in(t):
        streamed(fetch_in, t, lambda slot: in_part(slot, mbuf[t, 0, 0].reshape(2 * rows, TILE), pl.ds(0, 2 * rows)))

    def rest_in(t):
        def work(slot):
            far = mbuf[t].reshape(8 * rows, TILE)[2 * rows :]
            in_part(slot, far, pl.ds(2 * rows, 6 * rows))

        streamed(fetch_in, t + tiles, work)

    bufs = (r1, rx, ry, r2x, r2y, ssq)
    reduce_norm_gather(left, fetch_o, wbuf, heads_width, resid, resid_ready, mlp_gain, h_buf, mbuf, bufs, ssem.at[0], rsem.at[0], free.at[0], idle_in, gather_in, pre_in, rest_in)

    def finish(n, _):
        cols = pl.ds(pl.multiple_of(n % 4 * 256, 256), 256)
        value = jax.nn.silu(acc[n // 4, :, cols]) * acc[2 + n // 4, :, cols]
        prod[:, pl.ds(pl.multiple_of(n * 256, 256), 256)] = value.astype(jnp.bfloat16)
        return 0

    lax.fori_loop(0, padded // 256, finish, 0)

    def idle_head(j):
        clear(j)

        @pl.when(j == 1)
        def _():
            for slot in range(2):
                for copy in fetch_l(slot):
                    copy.start()

    def head_part(slot, right_rows, some):
        for n, (start, size) in enumerate(pieces):
            acc[n, pl.ds(0, size), some] += dot_nt(nbuf[slot, pl.ds(start, size)], right_rows)

    def pre_head(t):
        streamed(fetch_l, t, lambda slot: head_part(slot, mbuf[t, 0, 0].reshape(2 * rows, TILE), pl.ds(0, 2 * rows)))

    def rest_head(t):
        def work(slot):
            far = mbuf[t].reshape(8 * rows, TILE)[2 * rows :]
            head_part(slot, far, pl.ds(2 * rows, 6 * rows))

        streamed(fetch_l, t + tiles, work)

    reduce_norm_gather(prod, fetch_d, wbuf, padded, h_buf, lambda: None, final_gain, h_buf, mbuf, bufs, ssem.at[1], rsem.at[1], free.at[1], idle_head, lambda: None, pre_head, rest_head)

    best = jnp.full((8, count), -jnp.inf, jnp.float32)
    for n, (start, size) in enumerate(pieces):
        best = jnp.maximum(best, jnp.max(acc[n, pl.ds(0, size)].reshape(size // 8, 8, count), axis=0))
    best = jnp.max(best, axis=0, keepdims=True)
    ids = []
    for block in blocks:
        ids += [id_ref[pl.ds(2 * block, 1)], id_ref[pl.ds(2 * block + 1, 1)]]
    local_id = jnp.concatenate(ids, axis=1) - me * vocab

    total = jnp.zeros((8, count), jnp.float32)
    picked = jnp.zeros((8, count), jnp.float32)
    for n, (start, size) in enumerate(pieces):
        value = acc[n, pl.ds(0, size)]
        hit = lax.broadcasted_iota(jnp.int32, (size, count), 0) + start == local_id
        total = total + jnp.sum(jnp.exp(value - best).reshape(size // 8, 8, count), axis=0)
        picked = picked + jnp.sum(jnp.where(hit, value, 0.0).reshape(size // 8, 8, count), axis=0)
    for i, values in enumerate((best, jnp.sum(total, axis=0, keepdims=True), jnp.sum(picked, axis=0, keepdims=True))):
        for k, block in enumerate(blocks):
            stats[me, i, pl.ds(block, 1)] = values[:, k * rows : (k + 1) * rows]
    copies = []
    for i, other in enumerate(others):
        copy = pltpu.make_async_remote_copy(
            src_ref=stats.at[me], dst_ref=stats.at[me], send_sem=tsem.at[i], recv_sem=usem.at[i], device_id={"tp": other}, device_id_type=MESH
        )
        copy.start()
        copies.append(copy)
    for copy in copies:
        copy.wait()
    top = stats[0, 0]
    for d in range(1, 8):
        top = jnp.maximum(top, stats[d, 0])
    whole = jnp.zeros_like(top)
    score = jnp.zeros_like(top)
    for d in range(8):
        whole = whole + stats[d, 1] * jnp.exp(stats[d, 0] - top)
        score = score + stats[d, 2]
    norm = top + jnp.log(whole)
    for ref, values in ((norm_ref, norm), (prob_ref, score - norm)):
        nodes = ref.shape[1]
        for i in range(ref.shape[0]):
            start = i * nodes
            ref[i : i + 1] = values[start // 128 : start // 128 + 1, start % 128 : start % 128 + nodes]


def tail_stage(mlp_gain, final_gain, score_id, attended, hidden, w_o, gate_t, up_t, w_down, head_t):
    count, dim = hidden.shape
    tiles = dim // TILE
    rows = count // 8
    padded = pl.cdiv(gate_t.shape[0], 256) * 256
    vocab = head_t.shape[0]
    vmem = pl.BlockSpec(memory_space=pltpu.VMEM)
    anywhere = pl.BlockSpec(memory_space=pl.ANY)
    bf16 = jnp.bfloat16
    return pl.pallas_call(
        tail_kernel,
        in_specs=[vmem] * 3 + [anywhere] * 7,
        out_specs=[vmem, vmem],
        out_shape=[jax.ShapeDtypeStruct(score_id.shape, jnp.float32)] * 2,
        scratch_shapes=[
            pltpu.VMEM((tiles, 2, 2, 2, rows, TILE), bf16),
            pltpu.VMEM((tiles, 2, 2, rows, TILE), bf16),
            pltpu.VMEM((tiles, 2, rows, HALF), bf16),
            pltpu.VMEM((tiles, 2, rows, HALF), bf16),
            pltpu.VMEM((tiles, rows, HALF), bf16),
            pltpu.VMEM((tiles, rows, HALF), bf16),
            pltpu.VMEM((rows, 128), jnp.float32),
            pltpu.VMEM((8, rows, w_o.shape[0]), bf16),
            pltpu.VMEM((count, padded), bf16),
            pltpu.VMEM((tiles, rows, TILE), bf16),
            pltpu.VMEM((tiles, rows, TILE), bf16),
            pltpu.VMEM((2, padded, TILE), bf16),
            pltpu.VMEM((2, max(2 * padded, vocab), TILE), bf16),
            pltpu.VMEM((4, 1024, count), jnp.float32),
            pltpu.VMEM((8, 3, 8, count // 8), jnp.float32),
            pltpu.SemaphoreType.DMA((2, 13)),
            pltpu.SemaphoreType.DMA((2, 13, tiles)),
            pltpu.SemaphoreType.DMA((2,)),
            pltpu.SemaphoreType.DMA((2, 2)),
            pltpu.SemaphoreType.DMA((2,)),
            pltpu.SemaphoreType.DMA((7,)),
            pltpu.SemaphoreType.DMA((7,)),
            pltpu.SemaphoreType.REGULAR((2,)),
        ],
        compiler_params=pltpu.CompilerParams(collective_id=1, has_side_effects=True, vmem_limit_bytes=VMEM_MAX),
        name="tail_stage",
    )(mlp_gain, final_gain, score_id, attended, hidden, w_o, gate_t, up_t, w_down, head_t)


def rope_tables(positions, head_dim):
    half = head_dim // 2
    lane = jnp.arange(head_dim, dtype=jnp.int32)
    inv_freq = 1.0 / (ROPE_THETA ** ((lane % half).astype(jnp.float32) * (2.0 / head_dim)))
    angles = positions.astype(jnp.float32)[:, None] * inv_freq
    return jnp.cos(angles), jnp.sin(angles) * jnp.where(lane < half, -1.0, 1.0)


def solution(mesh):
    def group_step(hidden, tree_mask, depth, ctx_len, block_table, score_id, k_cache, v_cache, attn_norm, w_q, w_k, w_v, w_o, mlp_norm, w_gate, w_up, w_down, final_norm, w_lm):
        requests, nodes, dim = hidden.shape
        head_dim = k_cache.shape[3]
        rows = requests * nodes
        flat = hidden.reshape(rows, dim)
        cosine, sine = rope_tables((ctx_len[:, None] + depth).reshape(rows), head_dim)
        query, key_new, val_new = project(flat, attn_norm, cosine, sine, w_q, w_k, w_v, requests, nodes, head_dim, 4)
        attended, k_out, v_out = attend(
            block_table, ctx_len, query, key_new, val_new, tree_mask, jnp.transpose(k_cache, (0, 2, 1, 3)), jnp.transpose(v_cache, (0, 2, 1, 3))
        )
        k_out = jnp.transpose(k_out, (0, 2, 1, 3))
        v_out = jnp.transpose(v_out, (0, 2, 1, 3))

        log_norm, log_prob = tail_stage(mlp_norm, final_norm, score_id, attended, flat, w_o, w_gate.T, w_up.T, w_down, w_lm.T)
        return log_norm.reshape(requests, nodes), log_prob.reshape(requests, nodes), k_out, v_out

    request_spec = P("dp", None, None)
    node_spec = P("dp", None)
    cache_spec = P("dp", None, "tp", None)
    shared_spec = P(None)
    column_spec = P(None, "tp")
    row_spec = P("tp", None)
    in_specs = (request_spec, request_spec, node_spec, P("dp"), node_spec, node_spec, cache_spec, cache_spec, shared_spec, column_spec, column_spec, column_spec, row_spec, shared_spec, column_spec, column_spec, row_spec, shared_spec, column_spec)
    out_specs = (node_spec, node_spec, cache_spec, cache_spec)
    return jax.shard_map(group_step, mesh=mesh, in_specs=in_specs, out_specs=out_specs, check_vma=False)
```

time: 327 us -> 306 us (0.936)
  Pallas kernels: 319 us -> 297 us
    pallas_call x2 -> x1, Pallas kernels: 258 us -> 236 us  [tail_stage(): pl.pallas_call(tail_kernel, in_specs=[vmem] * 3 + [anywhere] * 7, out_spe...]
where the time goes in v4:
time: 306 us; the launch traced here: 304 us
  Pallas kernels  297 us (97%)
  other arithmetic  3.83 us (1%)
    pallas_call x1, Pallas kernels, tail_stage(): pl.pallas_call(tail_kernel, in_specs=[vmem] * 3 + [anywhere] * 7, out_spe...  236 us
    pallas_call x1, Pallas kernels, project(): pl.pallas_call(qkv_kernel, grid=(rows // block,), in_specs=[pl.BlockSpec(...  35.6 us
    pallas_call x1, Pallas kernels, attend(): pl.pallas_call(attend_kernel, grid_spec=pltpu.PrefetchScalarGridSpec(num_...  24.6 us

profile of v4, /device:TPU:0, one launch (start us, length us, event | category | flops | bytes accessed | tf_op | source)
XLA Modules:
  0.0 303.9 jit_solution(6434754975783329505)
XLA Ops:
  0.6 0.8 add_convert_fusion
  1.4 0.1 convert_element_type.18
  1.5 3.0 %fusion = (f32[1024,128]{1,0:T(8,128)}, f32[1024,128]{1,0:T(8,128)}) fusion(f32[128]{0:T(128)S(1)} %get-tuple-element.22, f32[128]{0:T(128)S(1)} %get-tuple-element.23, f32[1024]{0:T(1024)S(1)} %convert_element_type.18), kind=kLoop, calls=%fused_computation.2 | loop fusion | flops 262144 | bytes 1053696 | tf_op jit(solution)/shard_map/mul | solution.py:584
  4.5 35.6 %project.1 = (bf16[16,5,64,128]{3,2,1,0:T(8,128)(2,1)}, bf16[16,5,64,128]{3,2,1,0:T(8,128)(2,1)}, bf16[16,5,64,128]{3,2,1,0:T(8,128)(2,1)}) custom-call(bf16[1024,5120]{1,0:T(8,128)(2,1)} %bitcast.8, bf16[5120]{0:T(1024)(128)(2,1)} %gain_ref.1, f32[1024,128]{1,0:T(8,128)} %get-tuple-element.21.cos_ref, f32[1024,128]{1,0:T(8,128)} %get-tuple-element.20.sin_ref, ...), custom_call_target="tpu_custom_call" | custom-call | tf_op jit(solution)/shard_map/project/pallas_call | solution.py:49
  40.1 24.6 %attend.1 = (bf16[1024,640]{1,0:T(8,128)(2,1)}, bf16[512,5,16,128]{3,2,1,0:T(8,128)(2,1)}, bf16[512,5,16,128]{3,2,1,0:T(8,128)(2,1)}) custom-call(s32[16,32]{1,0:T(8,128)} %table_ref.1, s32[16]{0:T(128)} %ctx_ref.1, bf16[16,5,64,128]{3,2,1,0:T(8,128)(2,1)} %get-tuple-element.12.q_ref, bf16[16,5,64,128]{3,2,1,0:T(8,128)(2,1)} %get-tuple-element.13.kn_ref, ...), custom_call_target="tpu_custom_call" | custom-call | tf_op jit(solution)/shard_map/attend/pallas_call | solution.py:153
  64.8 236.5 %tail_stage.1 = (f32[16,64]{1,0:T(8,128)}, f32[16,64]{1,0:T(8,128)}) custom-call(bf16[5120]{0:T(1024)(128)(2,1)} %mlp_gain.1, bf16[5120]{0:T(1024)(128)(2,1)} %final_gain.1, s32[16,64]{1,0:T(8,128)} %id_ref.1, bf16[1024,640]{1,0:T(8,128)(2,1)} %get-tuple-element.15.att_hbm, bf16[1024,5120]{1,0:T(8,128)(2,1)} %bitcast.9, bf16[640,5120]{1,0:T(8,128)(2,1)} %wo_hbm.1, ...), custom_call_target="tpu_custom_call" | custom-call | tf_op jit(solution)/shard_map/tail_stage/pallas_call | solution.py:544
  301.3 1.3 copy.25
  302.6 1.3 copy.26
  (1 shorter events, 0.0 us)

commit v5 on v1

v5 whole, which is shorter than its diff:
```python
import jax
import jax.numpy as jnp
from jax import lax
from jax.experimental import pallas as pl
from jax.experimental.pallas import tpu as pltpu
from jax.sharding import PartitionSpec as P

RMS_EPS = 1e-5
ROPE_THETA = 500000
MESH = pl.DeviceIdType.MESH
NT_DIMS = (((1,), (1,)), ((), ()))
VMEM_MAX = 67043328


def dot_nt(left, right):
    return lax.dot_general(left, right, NT_DIMS, preferred_element_type=jnp.float32)


def qkv_kernel(hid_ref, gain_ref, cos_ref, sin_ref, wq_ref, wk_ref, wv_ref, q_ref, k_ref, v_ref):
    requests, heads, nodes, head_dim = q_ref.shape
    widened = hid_ref[...].astype(jnp.float32)
    scale = lax.rsqrt(jnp.mean(widened * widened, axis=-1, keepdims=True) + RMS_EPS)
    gain = gain_ref[...].reshape(1, widened.shape[1]).astype(jnp.float32)
    normed = (widened * scale * gain).astype(jnp.bfloat16)
    cosine = cos_ref[...]
    sine = sin_ref[...]

    def put(out_ref, weight_ref, turned):
        product = jnp.dot(normed, weight_ref[...], preferred_element_type=jnp.float32)
        for h in range(heads):
            part = product[:, h * head_dim : (h + 1) * head_dim]
            if turned:
                part = part * cosine + pltpu.roll(part, head_dim // 2, 1) * sine
            out_ref[:, h] = part.astype(jnp.bfloat16).reshape(requests, nodes, head_dim)

    put(q_ref, wq_ref, True)
    put(k_ref, wk_ref, True)
    put(v_ref, wv_ref, False)


def project(hidden, gain, cosine, sine, w_q, w_k, w_v, requests, nodes, head_dim, group):
    rows, dim = hidden.shape
    cols = w_q.shape[1]
    heads = cols // head_dim
    block = group * nodes
    full = pl.BlockSpec((dim, cols), lambda i: (0, 0), pipeline_mode=pl.Buffered(1))
    out = pl.BlockSpec((group, heads, nodes, head_dim), lambda i: (i, 0, 0, 0))
    shape = jax.ShapeDtypeStruct((requests, heads, nodes, head_dim), jnp.bfloat16)
    return pl.pallas_call(
        qkv_kernel,
        grid=(rows // block,),
        in_specs=[
            pl.BlockSpec((block, dim), lambda i: (i, 0)),
            pl.BlockSpec((dim,), lambda i: (0,)),
            pl.BlockSpec((block, head_dim), lambda i: (i, 0)),
            pl.BlockSpec((block, head_dim), lambda i: (i, 0)),
            full,
            full,
            full,
        ],
        out_specs=[out, out, out],
        out_shape=[shape, shape, shape],
        compiler_params=pltpu.CompilerParams(vmem_limit_bytes=VMEM_MAX),
        name="project",
    )(hidden, gain, cosine, sine, w_q, w_k, w_v)


def attend_kernel(table_ref, ctx_ref, q_ref, kn_ref, vn_ref, mask_ref, kc_ref, vc_ref, out_ref, ko_ref, vo_ref, kbuf, vbuf, rsem, wsem):
    b = pl.program_id(0)
    count = pl.num_programs(0)
    pages, heads, page, head_dim = kbuf.shape[1:]
    span = pages * page
    nodes = q_ref.shape[2]
    window = nodes + page

    def load(i, slot):
        for s in range(pages):
            block = table_ref[i, s]
            pltpu.make_async_copy(kc_ref.at[block], kbuf.at[slot, s], rsem.at[0, slot]).start()
            pltpu.make_async_copy(vc_ref.at[block], vbuf.at[slot, s], rsem.at[1, slot]).start()

    def save(i, slot):
        for s in range(pages):
            block = table_ref[i, s]
            pltpu.make_async_copy(kbuf.at[slot, s], ko_ref.at[block], wsem.at[0, slot]).start()
            pltpu.make_async_copy(vbuf.at[slot, s], vo_ref.at[block], wsem.at[1, slot]).start()

    def whole(slot, sem):
        pltpu.make_async_copy(kbuf.at[slot], kbuf.at[slot], sem.at[0, slot]).wait()
        pltpu.make_async_copy(vbuf.at[slot], vbuf.at[slot], sem.at[1, slot]).wait()

    slot = lax.rem(b, 3)
    after = lax.rem(b + 1, 3)

    @pl.when(b == 0)
    def _():
        load(0, 0)

    @pl.when(b >= 2)
    def _():
        whole(after, wsem)

    whole(slot, rsem)
    load(jnp.minimum(b + 1, count - 1), after)
    ctx = ctx_ref[b]
    first = jnp.minimum(ctx // page, pages - window // page)
    base = first * page
    row = base + lax.broadcasted_iota(jnp.int32, (window, nodes), 0)
    node = ctx + lax.broadcasted_iota(jnp.int32, (window, nodes), 1)
    place = jnp.where(row == node, 1.0, 0.0).astype(jnp.bfloat16)
    slot_id = base + lax.broadcasted_iota(jnp.int32, (window, head_dim), 0)
    fresh = (slot_id >= ctx) & (slot_id < ctx + nodes)
    for buf, new_ref in ((kbuf, kn_ref), (vbuf, vn_ref)):
        moved = [jnp.dot(place, new_ref[0, h], preferred_element_type=jnp.float32) for h in range(heads)]
        for h in range(heads):
            for i in range(window // page):
                rows = slice(i * page, (i + 1) * page)
                old = buf[slot, first + i, h].astype(jnp.float32)
                buf[slot, first + i, h] = jnp.where(fresh[rows], moved[h][rows], old).astype(jnp.bfloat16)
    save(b, slot)
    spread = jnp.where(
        ctx + lax.broadcasted_iota(jnp.int32, (nodes, span), 0) == lax.broadcasted_iota(jnp.int32, (nodes, span), 1), 1.0, 0.0
    ).astype(jnp.bfloat16)
    linked = jnp.where(mask_ref[0] > 0, 1.0, 0.0).astype(jnp.bfloat16)
    seen_new = jnp.dot(linked, spread, preferred_element_type=jnp.float32) > 0.5
    seen = seen_new | (lax.broadcasted_iota(jnp.int32, (nodes, span), 1) < ctx)
    scale = head_dim**-0.5
    scores = [dot_nt(q_ref[0, h], kbuf[slot, :, h].reshape(span, head_dim)) for h in range(heads)]
    scores = [jnp.where(seen, score * scale, -jnp.inf) for score in scores]
    tops = [jnp.max(score, axis=-1, keepdims=True) for score in scores]
    probs = [jnp.exp(score - top) for score, top in zip(scores, tops)]
    totals = [jnp.sum(prob, axis=-1, keepdims=True) for prob in probs]
    mixed = [
        jnp.dot(prob.astype(jnp.bfloat16), vbuf[slot, :, h].reshape(span, head_dim), preferred_element_type=jnp.float32)
        for h, prob in enumerate(probs)
    ]
    for h in range(heads):
        out_ref[:, h * head_dim : (h + 1) * head_dim] = (mixed[h] / totals[h]).astype(jnp.bfloat16)

    @pl.when(b == count - 1)
    def _():
        whole(lax.rem(b + 2, 3), wsem)
        whole(slot, wsem)
        whole(after, rsem)


def attend(table, ctx_len, query, key_new, val_new, tree_mask, k_cache, v_cache):
    requests, heads, nodes, head_dim = query.shape
    page = k_cache.shape[2]
    pages = table.shape[1]
    node_spec = pl.BlockSpec((1, heads, nodes, head_dim), lambda b, *_: (b, 0, 0, 0))
    anywhere = pl.BlockSpec(memory_space=pl.ANY)
    return pl.pallas_call(
        attend_kernel,
        grid_spec=pltpu.PrefetchScalarGridSpec(
            num_scalar_prefetch=2,
            grid=(requests,),
            in_specs=[
                node_spec,
                node_spec,
                node_spec,
                pl.BlockSpec((1, nodes, nodes), lambda b, *_: (b, 0, 0)),
                anywhere,
                anywhere,
            ],
            out_specs=[pl.BlockSpec((nodes, heads * head_dim), lambda b, *_: (b, 0)), anywhere, anywhere],
            scratch_shapes=[
                pltpu.VMEM((3, pages, heads, page, head_dim), jnp.bfloat16),
                pltpu.VMEM((3, pages, heads, page, head_dim), jnp.bfloat16),
                pltpu.SemaphoreType.DMA((2, 3)),
                pltpu.SemaphoreType.DMA((2, 3)),
            ],
        ),
        out_shape=[
            jax.ShapeDtypeStruct((requests * nodes, heads * head_dim), jnp.bfloat16),
            jax.ShapeDtypeStruct(k_cache.shape, k_cache.dtype),
            jax.ShapeDtypeStruct(v_cache.shape, v_cache.dtype),
        ],
        name="attend",
    )(table, ctx_len, query, key_new, val_new, tree_mask, k_cache, v_cache)


TILE = 512
HALF = TILE // 2
PAIR, X1, Y1, X2, Y2, GX, GY, GP, FX, FY, PX, PY, PD = range(13)


def seat():
    me = lax.axis_index("tp")
    core = me % 2
    x = (me // 2) % 2
    y = me // 4
    blocks = []
    for dy in range(2):
        for dx in range(2):
            for dc in range(2):
                blocks.append((1 - y if dy else y) * 4 + (1 - x if dx else x) * 2 + (1 - core if dc else core))
    return me, blocks


class Exchange:
    def __init__(self, left, fetch, wbuf, depth, resid, gain, h_buf, mbuf, bufs, ssem, rsem, free, scatter_work, gather_work, compute):
        self.left, self.fetch, self.wbuf, self.depth = left, fetch, wbuf, depth
        self.resid, self.gain, self.h_buf, self.mbuf = resid, gain, h_buf, mbuf
        self.r1, self.rx, self.ry, self.r2x, self.r2y, self.ssq = bufs
        self.ssem, self.rsem, self.free = ssem, rsem, free
        self.scatter_work, self.gather_work, self.compute = scatter_work, gather_work, compute
        _, blocks = seat()
        self.to_pair, self.to_x, self.to_y = blocks[1], blocks[2], blocks[4]
        self.steps = mbuf.shape[0]
        self.tiles = self.steps // 2
        self.rows = mbuf.shape[4]

    def send(self, src, dst, kind, i, target):
        pltpu.make_async_remote_copy(
            src_ref=src,
            dst_ref=dst,
            send_sem=self.ssem.at[i // self.tiles, kind],
            recv_sem=self.rsem.at[kind, i],
            device_id={"tp": target},
            device_id_type=MESH,
        ).start()

    def landed(self, ref, kind, i):
        pltpu.make_async_copy(ref, ref, self.rsem.at[kind, i]).wait()

    def sent(self, ref, kind, h):
        pltpu.make_async_copy(ref, ref, self.ssem.at[h, kind]).wait()

    def scatter_step(self, i):
        mbuf, steps, rows = self.mbuf, self.steps, self.rows
        low = pl.ds(0, HALF)
        high = pl.ds(HALF, HALF)

        @pl.when(i < steps)
        def _():
            self.fetch(i).wait()
            left = self.left[i // self.tiles].reshape(8 * rows, self.depth)
            part = jnp.dot(left, self.wbuf[i % 2, pl.ds(0, self.depth)], preferred_element_type=jnp.float32)
            mbuf[i] = part.astype(jnp.bfloat16).reshape(2, 2, 2, rows, TILE)

            @pl.when(i + 2 < steps)
            def _():
                self.fetch(i + 2).start()

            self.send(mbuf.at[i, :, :, 1], self.r1.at[i], PAIR, i, self.to_pair)

        @pl.when((i >= 1) & (i < steps + 1))
        def _():
            t = i - 1
            self.landed(self.r1.at[t], PAIR, t)
            mbuf[t, :, :, 0] = mbuf[t, :, :, 0] + self.r1[t]
            self.send(mbuf.at[t, :, 1, 0, :, low], self.rx.at[t], X1, t, self.to_x)
            self.send(mbuf.at[t, 1, :, 0, :, high], self.ry.at[t], Y1, t, self.to_y)

        @pl.when((i >= 3) & (i < steps + 3))
        def _():
            t = i - 3
            self.landed(self.rx.at[t], X1, t)
            mbuf[t, :, 0, 0, :, low] = mbuf[t, :, 0, 0, :, low] + self.rx[t]
            self.send(mbuf.at[t, 1, 0, 0, :, low], self.r2y.at[t], Y2, t, self.to_y)
            self.landed(self.ry.at[t], Y1, t)
            mbuf[t, 0, :, 0, :, high] = mbuf[t, 0, :, 0, :, high] + self.ry[t]
            self.send(mbuf.at[t, 0, 1, 0, :, high], self.r2x.at[t], X2, t, self.to_x)

        @pl.when(i >= 5)
        def _():
            t = i - 5
            h = t // self.tiles
            self.landed(self.r2y.at[t], Y2, t)
            self.landed(self.r2x.at[t], X2, t)
            for cols, other in ((low, self.r2y), (high, self.r2x)):
                total = (mbuf[t, 0, 0, 0, :, cols] + other[t]).astype(jnp.float32)
                new = (self.resid[t, :, cols].astype(jnp.float32) + total).astype(jnp.bfloat16)
                self.h_buf[t, :, cols] = new
                wide = new.astype(jnp.float32)
                wide = wide * wide
                self.ssq[h] += sum(wide[:, lane : lane + 128] for lane in range(0, HALF, 128))

        @pl.when(i == self.tiles + 5)
        def _():
            self.norm(0)

        @pl.when(i == steps + 1)
        def _():
            self.open(0)

        self.scatter_work(i)

    def norm(self, h):
        tiles = self.tiles
        part = pl.ds(h * tiles, tiles)
        self.sent(self.r1.at[part], PAIR, h)
        self.sent(self.rx.at[part], X1, h)
        self.sent(self.ry.at[part], Y1, h)
        self.sent(self.r2x.at[part], X2, h)
        self.sent(self.r2y.at[part], Y2, h)
        for target in (self.to_x, self.to_y, self.to_pair):
            pl.semaphore_signal(self.free.at[h], inc=1, device_id={"tp": target}, device_id_type=MESH)
        scale = lax.rsqrt(jnp.sum(self.ssq[h], axis=-1, keepdims=True) * (1.0 / (tiles * TILE)) + RMS_EPS)
        for t in range(tiles):
            gain = self.gain[pl.ds(t * TILE, TILE)].reshape(1, TILE).astype(jnp.float32)
            i = h * tiles + t
            self.mbuf[i, 0, 0, 0] = (self.h_buf[i].astype(jnp.float32) * scale * gain).astype(jnp.bfloat16)

    def own(self, i):
        mine = self.mbuf.at[i, 0, 0, 0]
        self.send(mine, self.mbuf.at[i, 0, 1, 0], GX, i, self.to_x)
        self.send(mine, self.mbuf.at[i, 1, 0, 0], GY, i, self.to_y)
        self.send(mine, self.mbuf.at[i, 0, 0, 1], GP, i, self.to_pair)

    def open(self, h):
        pl.semaphore_wait(self.free.at[h], 3)
        if h == 0:
            for i in range(2):
                self.own(i)

    def gather_step(self, i):
        mbuf, steps, rows = self.mbuf, self.steps, self.rows
        upper = pl.ds(0, rows // 2)
        lower = pl.ds(rows // 2, rows // 2)

        @pl.when(i == 6)
        def _():
            self.open(1)

        @pl.when(i < steps)
        def _():
            self.landed(mbuf.at[i, 0, 1, 0], GX, i)
            self.send(mbuf.at[i, 0, 1, 0, upper], mbuf.at[i, 1, 1, 0, upper], FY, i, self.to_y)
            self.send(mbuf.at[i, 0, 1, 0], mbuf.at[i, 0, 1, 1], PX, i, self.to_pair)
            self.landed(mbuf.at[i, 1, 0, 0], GY, i)
            self.send(mbuf.at[i, 1, 0, 0, lower], mbuf.at[i, 1, 1, 0, lower], FX, i, self.to_x)
            self.send(mbuf.at[i, 1, 0, 0], mbuf.at[i, 1, 0, 1], PY, i, self.to_pair)

        @pl.when(i + 2 < steps)
        def _():
            self.own(i + 2)

        @pl.when((i >= 2) & (i < steps + 2))
        def _():
            t = i - 2
            self.landed(mbuf.at[t, 1, 1, 0, upper], FY, t)
            self.landed(mbuf.at[t, 1, 1, 0, lower], FX, t)
            self.send(mbuf.at[t, 1, 1, 0], mbuf.at[t, 1, 1, 1], PD, t, self.to_pair)

        self.gather_work(i)

        @pl.when(i >= 3)
        def _():
            t = i - 3
            self.landed(mbuf.at[t, 0, 0, 1], GP, t)
            self.landed(mbuf.at[t, 0, 1, 1], PX, t)
            self.landed(mbuf.at[t, 1, 0, 1], PY, t)
            self.landed(mbuf.at[t, 1, 1, 1], PD, t)
            self.compute(t)

    def close(self, h):
        part = pl.ds(h * self.tiles, self.tiles)
        for kind in (GX, GY, GP, PX, PY, PD):
            self.sent(self.h_buf.at[part], kind, h)
        half = pl.ds(h * self.tiles, self.tiles // 2)
        for kind in (FX, FY):
            self.sent(self.h_buf.at[half], kind, h)


def loop(start, stop, step):
    def body(i, _):
        step(i)
        return 0

    lax.fori_loop(start, stop, body, 0)


def tail_kernel(mlp_gain, final_gain, id_ref, att_hbm, hid_hbm, wo_hbm, wg_hbm, wu_hbm, wd_hbm, wl_hbm, norm_ref, prob_ref, mbuf, r1, rx, ry, r2x, r2y, ssq, left, prod, resid, h_buf, wbuf, nbuf, acc, stats, ssem, rsem, wsem, nsem, isem, tsem, usem, free):
    me, blocks = seat()
    steps = mbuf.shape[0]
    tiles = steps // 2
    rows = mbuf.shape[4]
    half = 8 * rows
    count = 2 * half
    heads_width = left.shape[3]
    width = wg_hbm.shape[0]
    padded = wbuf.shape[1]
    vocab = wl_hbm.shape[0]
    parts = acc.shape[0]
    side = acc.shape[1]
    piece = pl.cdiv(vocab, parts * 16) * 16
    pieces = [(n * piece, min(piece, vocab - n * piece)) for n in range(parts)]
    others = [(me + i) % 8 for i in range(1, 8)]

    def columns(i):
        return pl.ds(pl.multiple_of(i % tiles * TILE, TILE), TILE)

    def fetch_o(i):
        return pltpu.make_async_copy(wo_hbm.at[:, columns(i)], wbuf.at[i % 2, pl.ds(0, heads_width)], wsem.at[i % 2])

    def fetch_d(i):
        return pltpu.make_async_copy(wd_hbm.at[:, columns(i)], wbuf.at[i % 2, pl.ds(0, width)], wsem.at[i % 2])

    def fetch_in(i):
        slot = i % 2
        return (
            pltpu.make_async_copy(wg_hbm.at[:, columns(i)], nbuf.at[slot, pl.ds(0, width)], nsem.at[0, slot]),
            pltpu.make_async_copy(wu_hbm.at[:, columns(i)], nbuf.at[slot, pl.ds(padded, width)], nsem.at[1, slot]),
        )

    def fetch_l(i):
        slot = i % 2
        return (pltpu.make_async_copy(wl_hbm.at[:, columns(i)], nbuf.at[slot, pl.ds(0, vocab)], nsem.at[0, slot]),)

    fetch_o(0).start()
    for h in range(2):
        for k, block in enumerate(blocks):
            source = pl.ds(pl.multiple_of(block * 2 * rows + h * rows, rows), rows)
            pltpu.make_async_copy(att_hbm.at[source], left.at[h, k], isem.at[0]).start()
    fetch_o(1).start()
    barrier = pltpu.get_barrier_semaphore()
    for other in others:
        pl.semaphore_signal(barrier, inc=1, device_id={"tp": other}, device_id_type=MESH)
    pl.semaphore_wait(barrier, 7)
    for i in range(steps):
        source = pl.ds(pl.multiple_of(me * 2 * rows + i // tiles * rows, rows), rows)
        pltpu.make_async_copy(hid_hbm.at[source, pl.ds(i % tiles * TILE, TILE)], resid.at[i], isem.at[1]).start()
    pltpu.make_async_copy(left, left, isem.at[0]).wait()
    ssq[...] = jnp.zeros_like(ssq)

    def clear(n):
        acc[n] = jnp.zeros(acc.shape[1:], jnp.float32)

    def finish(h):
        some = pl.ds(h * half, half)

        def one(n):
            cols = pl.ds(pl.multiple_of(n % 4 * 256, 256), 256)
            value = jax.nn.silu(acc[n // 4, some, cols]) * acc[2 + n // 4, some, cols]
            prod[h, :, pl.ds(pl.multiple_of(n * 256, 256), 256)] = value.astype(jnp.bfloat16)

        loop(0, padded // 256, one)

    def streamed(fetch, i, work):
        for copy in fetch(i):
            copy.wait()
        work(i % 2, pl.ds(pl.multiple_of(i // tiles * half, half), half))

        @pl.when(i + 2 < steps)
        def _():
            for copy in fetch(i + 2):
                copy.start()

    def work_one(i):
        @pl.when(i < parts)
        def _():
            clear(i)

        @pl.when(i == 4)
        def _():
            pltpu.make_async_copy(resid, resid, isem.at[1]).wait()
            for slot in range(2):
                gap = jnp.zeros((padded - width, TILE), jnp.bfloat16)
                wbuf[slot, pl.ds(width, padded - width)] = gap
                nbuf[slot, pl.ds(width, padded - width)] = gap
                nbuf[slot, pl.ds(padded + width, padded - width)] = gap
                for copy in fetch_in(slot):
                    copy.start()

    def compute_in(i):
        def work(slot, some):
            left_rows = mbuf[i].reshape(half, TILE)
            for which in range(2):
                for n in range(2):
                    wide = min(side, padded - n * side)
                    weights = nbuf[slot, pl.ds(which * padded + n * side, wide)]
                    acc[which * 2 + n, some, pl.ds(0, wide)] += dot_nt(left_rows, weights)

        streamed(fetch_in, i, work)

    def between(i):
        @pl.when(i == 0)
        def _():
            first.norm(1)
            fetch_d(0).start()
            fetch_d(1).start()
            ssq[...] = jnp.zeros_like(ssq)

        @pl.when(i == 13)
        def _():
            finish(0)

        @pl.when(i == 15)
        def _():
            first.close(0)

        @pl.when(i >= steps)
        def _():
            second.scatter_step(i - steps)

    def work_two(i):
        @pl.when(i == 3)
        def _():
            finish(1)
            first.close(1)
            for slot in range(2):
                for copy in fetch_l(slot):
                    copy.start()

        @pl.when((i >= 4) & (i < 4 + parts))
        def _():
            clear(i - 4)

    def compute_head(i):
        def work(slot, some):
            right_rows = mbuf[i].reshape(half, TILE)
            for n, (start, size) in enumerate(pieces):
                acc[n, pl.ds(0, size), some] += dot_nt(nbuf[slot, pl.ds(start, size)], right_rows)

        streamed(fetch_l, i, work)

    def last(i):
        @pl.when(i == 0)
        def _():
            second.norm(1)

    bufs = (r1, rx, ry, r2x, r2y, ssq)
    first = Exchange(left, fetch_o, wbuf, heads_width, resid, mlp_gain, h_buf, mbuf, bufs, ssem, rsem, free.at[0], work_one, between, compute_in)
    second = Exchange(prod, fetch_d, wbuf, padded, h_buf, final_gain, h_buf, mbuf, bufs, ssem, rsem, free.at[1], work_two, last, compute_head)
    loop(0, steps + 5, first.scatter_step)
    loop(0, steps + 3, first.gather_step)
    loop(3, steps + 5, second.scatter_step)
    loop(0, steps + 3, second.gather_step)
    second.close(0)
    second.close(1)

    best = jnp.full((8, count), -jnp.inf, jnp.float32)
    for n, (start, size) in enumerate(pieces):
        best = jnp.maximum(best, jnp.max(acc[n, pl.ds(0, size)].reshape(size // 8, 8, count), axis=0))
    best = jnp.max(best, axis=0, keepdims=True)
    ids = [id_ref[pl.ds(2 * block + h, 1)] for h in range(2) for block in blocks]
    local_id = jnp.concatenate(ids, axis=1) - me * vocab
    total = jnp.zeros((8, count), jnp.float32)
    picked = jnp.zeros((8, count), jnp.float32)
    for n, (start, size) in enumerate(pieces):
        value = acc[n, pl.ds(0, size)]
        hit = lax.broadcasted_iota(jnp.int32, (size, count), 0) + start == local_id
        total = total + jnp.sum(jnp.exp(value - best).reshape(size // 8, 8, count), axis=0)
        picked = picked + jnp.sum(jnp.where(hit, value, 0.0).reshape(size // 8, 8, count), axis=0)
    for n, values in enumerate((best, jnp.sum(total, axis=0, keepdims=True), jnp.sum(picked, axis=0, keepdims=True))):
        for h in range(2):
            for k, block in enumerate(blocks):
                start = h * half + k * rows
                stats[me, n, pl.ds(2 * block + h, 1)] = values[:, start : start + rows]
    copies = []
    for i, other in enumerate(others):
        copy = pltpu.make_async_remote_copy(
            src_ref=stats.at[me], dst_ref=stats.at[me], send_sem=tsem.at[i], recv_sem=usem.at[i], device_id={"tp": other}, device_id_type=MESH
        )
        copy.start()
        copies.append(copy)
    for copy in copies:
        copy.wait()
    top = stats[0, 0]
    for d in range(1, 8):
        top = jnp.maximum(top, stats[d, 0])
    whole = jnp.zeros_like(top)
    score = jnp.zeros_like(top)
    for d in range(8):
        whole = whole + stats[d, 1] * jnp.exp(stats[d, 0] - top)
        score = score + stats[d, 2]
    norm = top + jnp.log(whole)
    norm_ref[...] = norm
    prob_ref[...] = score - norm


def tail_stage(mlp_gain, final_gain, score_id, attended, hidden, w_o, gate_t, up_t, w_down, head_t):
    count, dim = hidden.shape
    steps = 2 * dim // TILE
    rows = count // 16
    padded = pl.cdiv(gate_t.shape[0], 256) * 256
    vocab = head_t.shape[0]
    vmem = pl.BlockSpec(memory_space=pltpu.VMEM)
    anywhere = pl.BlockSpec(memory_space=pl.ANY)
    bf16 = jnp.bfloat16
    return pl.pallas_call(
        tail_kernel,
        in_specs=[vmem] * 3 + [anywhere] * 7,
        out_specs=[vmem, vmem],
        out_shape=[jax.ShapeDtypeStruct(score_id.shape, jnp.float32)] * 2,
        scratch_shapes=[
            pltpu.VMEM((steps, 2, 2, 2, rows, TILE), bf16),
            pltpu.VMEM((steps, 2, 2, rows, TILE), bf16),
            pltpu.VMEM((steps, 2, rows, HALF), bf16),
            pltpu.VMEM((steps, 2, rows, HALF), bf16),
            pltpu.VMEM((steps, rows, HALF), bf16),
            pltpu.VMEM((steps, rows, HALF), bf16),
            pltpu.VMEM((2, rows, 128), jnp.float32),
            pltpu.VMEM((2, 8, rows, w_o.shape[0]), bf16),
            pltpu.VMEM((2, 8 * rows, padded), bf16),
            pltpu.VMEM((steps, rows, TILE), bf16),
            pltpu.VMEM((steps, rows, TILE), bf16),
            pltpu.VMEM((2, padded, TILE), bf16),
            pltpu.VMEM((2, max(2 * padded, vocab), TILE), bf16),
            pltpu.VMEM((4, 1024, count), jnp.float32),
            pltpu.VMEM((8, 3) + score_id.shape, jnp.float32),
            pltpu.SemaphoreType.DMA((2, 13)),
            pltpu.SemaphoreType.DMA((13, steps)),
            pltpu.SemaphoreType.DMA((2,)),
            pltpu.SemaphoreType.DMA((2, 2)),
            pltpu.SemaphoreType.DMA((2,)),
            pltpu.SemaphoreType.DMA((7,)),
            pltpu.SemaphoreType.DMA((7,)),
            pltpu.SemaphoreType.REGULAR((2, 2)),
        ],
        compiler_params=pltpu.CompilerParams(collective_id=1, has_side_effects=True, vmem_limit_bytes=VMEM_MAX),
        name="tail_stage",
    )(mlp_gain, final_gain, score_id, attended, hidden, w_o, gate_t, up_t, w_down, head_t)


def rope_tables(positions, head_dim):
    half = head_dim // 2
    lane = jnp.arange(head_dim, dtype=jnp.int32)
    inv_freq = 1.0 / (ROPE_THETA ** ((lane % half).astype(jnp.float32) * (2.0 / head_dim)))
    angles = positions.astype(jnp.float32)[:, None] * inv_freq
    return jnp.cos(angles), jnp.sin(angles) * jnp.where(lane < half, -1.0, 1.0)


def solution(mesh):
    def group_step(hidden, tree_mask, depth, ctx_len, block_table, score_id, k_cache, v_cache, attn_norm, w_q, w_k, w_v, w_o, mlp_norm, w_gate, w_up, w_down, final_norm, w_lm):
        requests, nodes, dim = hidden.shape
        head_dim = k_cache.shape[3]
        rows = requests * nodes
        flat = hidden.reshape(rows, dim)
        cosine, sine = rope_tables((ctx_len[:, None] + depth).reshape(rows), head_dim)
        query, key_new, val_new = project(flat, attn_norm, cosine, sine, w_q, w_k, w_v, requests, nodes, head_dim, 4)
        attended, k_out, v_out = attend(
            block_table, ctx_len, query, key_new, val_new, tree_mask, jnp.transpose(k_cache, (0, 2, 1, 3)), jnp.transpose(v_cache, (0, 2, 1, 3))
        )
        k_out = jnp.transpose(k_out, (0, 2, 1, 3))
        v_out = jnp.transpose(v_out, (0, 2, 1, 3))

        log_norm, log_prob = tail_stage(mlp_norm, final_norm, score_id, attended, flat, w_o, w_gate.T, w_up.T, w_down, w_lm.T)
        return log_norm.reshape(requests, nodes), log_prob.reshape(requests, nodes), k_out, v_out

    request_spec = P("dp", None, None)
    node_spec = P("dp", None)
    cache_spec = P("dp", None, "tp", None)
    shared_spec = P(None)
    column_spec = P(None, "tp")
    row_spec = P("tp", None)
    in_specs = (request_spec, request_spec, node_spec, P("dp"), node_spec, node_spec, cache_spec, cache_spec, shared_spec, column_spec, column_spec, column_spec, row_spec, shared_spec, column_spec, column_spec, row_spec, shared_spec, column_spec)
    out_specs = (node_spec, node_spec, cache_spec, cache_spec)
    return jax.shard_map(group_step, mesh=mesh, in_specs=in_specs, out_specs=out_specs, check_vma=False)
```

time: 568 us -> 291 us (0.51); the launches traced: 559 us -> 289 us
  waiting for transfers between devices: 267 us -> 0 us
  Pallas kernels: 77.1 us -> 282 us
  matrix products: 145 us -> 0 us
  other arithmetic: 31.3 us -> 3.83 us
  between operations: 14.5 us -> 0.65 us
  blocking collectives: 11.2 us -> 0 us
  starting transfers between devices: 10.8 us -> 0 us
    psum x2 -> x0, waiting for transfers between devices: 267 us -> none  [the longest x1 137 us: group_step(): lax.psum(jnp.dot(product, w_down, preferred_element_type=jnp.float32).ast...]
    pallas_call x0 -> x1, Pallas kernels: none -> 221 us  [tail_stage(): pl.pallas_call(tail_kernel, in_specs=[vmem] * 3 + [anywhere] * 7, out_spe...]
    dot_general x5 -> x0, matrix products: 145 us -> none  [the longest x1 55.2 us: group_step(): jnp.dot(rms_norm(layer_out, final_norm), w_lm, preferred_element_type=jnp...]
    reduce_sum x4 -> x0, other arithmetic: 26.6 us -> none  [the longest x2 18.6 us: rms_norm(): jnp.mean(widened * widened, axis=-1, keepdims=True) + RMS_EPS]
    pallas_call x1, Pallas kernels: 41.5 us -> 24.6 us  [attend(): pl.pallas_call(attend_kernel, grid_spec=pltpu.PrefetchScalarGridSpec(num_...]
    all_gather x1 -> x0, blocking collectives: 11.2 us -> none  [group_step(): stats = lax.all_gather(jnp.stack([top, part, picked]), 'tp')]
    psum x2 -> x0, starting transfers between devices: 10.8 us -> none  [the longest x1 10.7 us: group_step(): lax.psum(jnp.dot(product, w_down, preferred_element_type=jnp.float32).ast...]
  transfers between devices with their start and end apart: 2 -> 0, of which waited for: 2 -> 0; matrix products, arithmetic and copies ran while one was open for 0% -> 0% of each run, Pallas kernels for 0% -> 0%
where the time goes in v5:
time: 291 us; the launch traced here: 289 us
  Pallas kernels  282 us (97%)
  other arithmetic  3.83 us (1%)
    pallas_call x1, Pallas kernels, tail_stage(): pl.pallas_call(tail_kernel, in_specs=[vmem] * 3 + [anywhere] * 7, out_spe...  221 us
    pallas_call x1, Pallas kernels, project(): pl.pallas_call(qkv_kernel, grid=(rows // block,), in_specs=[pl.BlockSpec(...  35.6 us
    pallas_call x1, Pallas kernels, attend(): pl.pallas_call(attend_kernel, grid_spec=pltpu.PrefetchScalarGridSpec(num_...  24.6 us

profile of v5, /device:TPU:0, one launch (start us, length us, event | category | flops | bytes accessed | tf_op | source)
XLA Modules:
  0.0 288.9 jit_solution(9023358720375845494)
XLA Ops:
  0.6 0.8 add_convert_fusion
  1.4 0.1 convert_element_type.18
  1.5 3.0 %fusion = (f32[1024,128]{1,0:T(8,128)}, f32[1024,128]{1,0:T(8,128)}) fusion(f32[128]{0:T(128)S(1)} %get-tuple-element.22, f32[128]{0:T(128)S(1)} %get-tuple-element.23, f32[1024]{0:T(1024)S(1)} %convert_element_type.18), kind=kLoop, calls=%fused_computation.2 | loop fusion | flops 262144 | bytes 1053696 | tf_op jit(solution)/shard_map/mul | solution.py:623
  4.5 35.6 %project.1 = (bf16[16,5,64,128]{3,2,1,0:T(8,128)(2,1)}, bf16[16,5,64,128]{3,2,1,0:T(8,128)(2,1)}, bf16[16,5,64,128]{3,2,1,0:T(8,128)(2,1)}) custom-call(bf16[1024,5120]{1,0:T(8,128)(2,1)} %bitcast.8, bf16[5120]{0:T(1024)(128)(2,1)} %gain_ref.1, f32[1024,128]{1,0:T(8,128)} %get-tuple-element.21.cos_ref, f32[1024,128]{1,0:T(8,128)} %get-tuple-element.20.sin_ref, ...), custom_call_target="tpu_custom_call" | custom-call | tf_op jit(solution)/shard_map/project/pallas_call | solution.py:49
  40.1 24.6 %attend.1 = (bf16[1024,640]{1,0:T(8,128)(2,1)}, bf16[512,5,16,128]{3,2,1,0:T(8,128)(2,1)}, bf16[512,5,16,128]{3,2,1,0:T(8,128)(2,1)}) custom-call(s32[16,32]{1,0:T(8,128)} %table_ref.1, s32[16]{0:T(128)} %ctx_ref.1, bf16[16,5,64,128]{3,2,1,0:T(8,128)(2,1)} %get-tuple-element.12.q_ref, bf16[16,5,64,128]{3,2,1,0:T(8,128)(2,1)} %get-tuple-element.13.kn_ref, ...), custom_call_target="tpu_custom_call" | custom-call | tf_op jit(solution)/shard_map/attend/pallas_call | solution.py:153
  64.8 221.5 %tail_stage.1 = (f32[16,64]{1,0:T(8,128)}, f32[16,64]{1,0:T(8,128)}) custom-call(bf16[5120]{0:T(1024)(128)(2,1)} %mlp_gain.1, bf16[5120]{0:T(1024)(128)(2,1)} %final_gain.1, s32[16,64]{1,0:T(8,128)} %id_ref.1, bf16[1024,640]{1,0:T(8,128)(2,1)} %get-tuple-element.15.att_hbm, bf16[1024,5120]{1,0:T(8,128)(2,1)} %bitcast.9, bf16[640,5120]{1,0:T(8,128)(2,1)} %wo_hbm.1, ...), custom_call_target="tpu_custom_call" | custom-call | tf_op jit(solution)/shard_map/tail_stage/pallas_call | solution.py:583
  286.3 1.3 copy.25
  287.6 1.3 copy.26
  (1 shorter events, 0.0 us)

commit v6 on v5

--- a/solution.py
+++ b/solution.py
@@ -16,168 +16,166 @@
     return lax.dot_general(left, right, NT_DIMS, preferred_element_type=jnp.float32)
 
 
-def qkv_kernel(hid_ref, gain_ref, cos_ref, sin_ref, wq_ref, wk_ref, wv_ref, q_ref, k_ref, v_ref):
-    requests, heads, nodes, head_dim = q_ref.shape
-    widened = hid_ref[...].astype(jnp.float32)
-    scale = lax.rsqrt(jnp.mean(widened * widened, axis=-1, keepdims=True) + RMS_EPS)
-    gain = gain_ref[...].reshape(1, widened.shape[1]).astype(jnp.float32)
-    normed = (widened * scale * gain).astype(jnp.bfloat16)
-    cosine = cos_ref[...]
-    sine = sin_ref[...]
-
-    def put(out_ref, weight_ref, turned):
-        product = jnp.dot(normed, weight_ref[...], preferred_element_type=jnp.float32)
+def front_kernel(table_ref, ctx_ref, hid_ref, gain_ref, cos_ref, sin_ref, mask_ref, wq_hbm, wk_hbm, wv_hbm, kc_ref, vc_ref, out_ref, ko_ref, vo_ref, w_buf, n_buf, new, kbuf, vbuf, fixed, wsem, rsem, ssem, psem):
+    g = pl.program_id(0)
+    count = pl.num_programs(0) - 1
+    _, heads, page, head_dim = kbuf.shape
+    _, _, group, _, nodes, _ = new.shape
+    pages = table_ref.shape[1]
+    window = nodes // page + 1
+
+    def weight(n):
+        source = (wq_hbm, wk_hbm, wv_hbm)[n]
+        return pltpu.make_async_copy(source, w_buf.at[n], wsem.at[n])
+
+    spans = [pl.ds(i * (kbuf.shape[0] // 8), kbuf.shape[0] // 8) for i in range(8)]
+    caches = ((kc_ref, kbuf, ko_ref), (vc_ref, vbuf, vo_ref))
+    cache_in = [pltpu.make_async_copy(src.at[span], buf.at[span], rsem.at[n, i]) for n, (src, buf, _) in enumerate(caches) for i, span in enumerate(spans)]
+    cache_out = [pltpu.make_async_copy(buf.at[span], dst.at[span], ssem.at[n, i]) for n, (_, buf, dst) in enumerate(caches) for i, span in enumerate(spans)]
+
+    @pl.when(g == 0)
+    def _():
+        weight(0).start()
+        weight(1).start()
+
+    @pl.when(g < count)
+    def _():
+        widened = hid_ref[...].astype(jnp.float32)
+        rms = lax.rsqrt(jnp.mean(widened * widened, axis=-1, keepdims=True) + RMS_EPS)
+        gain = gain_ref[...].reshape(1, widened.shape[1]).astype(jnp.float32)
+        n_buf[...] = (widened * rms * gain).astype(jnp.bfloat16)
+        for n in range(3):
+
+            @pl.when(g == 0)
+            def _():
+                weight(n).wait()
+                if n == 0:
+                    weight(2).start()
+                if n == 2:
+                    for copy in cache_in:
+                        copy.start()
+
+            product = jnp.dot(n_buf[...], w_buf[n], preferred_element_type=jnp.float32)
+            for h in range(heads):
+                part = product[:, h * head_dim : (h + 1) * head_dim]
+                if n < 2:
+                    part = part * cos_ref[...] + pltpu.roll(part, head_dim // 2, 1) * sin_ref[...]
+                new[g % 2, n, :, h] = part.astype(jnp.bfloat16).reshape(group, nodes, head_dim)
+
+    @pl.when(g == 1)
+    def _():
+        for copy in cache_in:
+            copy.wait()
+        for copy in cache_out:
+            copy.start()
+
+    turn = (g + 1) % 2
+
+    def first_page(b):
+        return jnp.minimum(ctx_ref[b] // page, pages - window)
+
+    def attend(r, _):
+        b = (g - 1) * group + r
+        ctx = ctx_ref[b]
+        first = first_page(b)
+        base = first * page
+        row = base + lax.broadcasted_iota(jnp.int32, (window * page, nodes), 0)
+        node = ctx + lax.broadcasted_iota(jnp.int32, (window * page, nodes), 1)
+        place = jnp.where(row == node, 1.0, 0.0).astype(jnp.bfloat16)
+        slot_id = base + lax.broadcasted_iota(jnp.int32, (window * page, head_dim), 0)
+        fresh = (slot_id >= ctx) & (slot_id < ctx + nodes)
+        edge = [table_ref[b, first + i] for i in range(window)]
+        for which, buf in ((0, kbuf), (1, vbuf)):
+            moved = [jnp.dot(place, new[turn, 1 + which, r, h], preferred_element_type=jnp.float32) for h in range(heads)]
+            for i, block in enumerate(edge):
+                rows = slice(i * page, (i + 1) * page)
+                for h in range(heads):
+                    old = buf[block, h].astype(jnp.float32)
+                    fixed[which, b, i, h] = jnp.where(fresh[rows], moved[h][rows], old).astype(jnp.bfloat16)
+        table = [table_ref[b, s] for s in range(pages)]
+        seen = lax.broadcasted_iota(jnp.int32, (nodes, pages * page), 1) < ctx
+        linked = mask_ref[r] > 0
+        scale = head_dim**-0.5
+        old_k = [jnp.concatenate([kbuf[block, h] for block in table], axis=0) for h in range(heads)]
+        scores = [jnp.where(seen, dot_nt(new[turn, 0, r, h], old_k[h]) * scale, -jnp.inf) for h in range(heads)]
+        fresh_scores = [jnp.where(linked, dot_nt(new[turn, 0, r, h], new[turn, 1, r, h]) * scale, -jnp.inf) for h in range(heads)]
+        tops = [
+            jnp.maximum(jnp.max(old, axis=-1, keepdims=True), jnp.max(fresh, axis=-1, keepdims=True))
+            for old, fresh in zip(scores, fresh_scores)
+        ]
+        probs = [jnp.exp(score - top) for score, top in zip(scores, tops)]
+        fresh_probs = [jnp.exp(score - top) for score, top in zip(fresh_scores, tops)]
+        totals = [jnp.sum(old, axis=-1, keepdims=True) + jnp.sum(fresh, axis=-1, keepdims=True) for old, fresh in zip(probs, fresh_probs)]
+        old_v = [jnp.concatenate([vbuf[block, h] for block in table], axis=0) for h in range(heads)]
         for h in range(heads):
-            part = product[:, h * head_dim : (h + 1) * head_dim]
-            if turned:
-                part = part * cosine + pltpu.roll(part, head_dim // 2, 1) * sine
-            out_ref[:, h] = part.astype(jnp.bfloat16).reshape(requests, nodes, head_dim)
-
-    put(q_ref, wq_ref, True)
-    put(k_ref, wk_ref, True)
-    put(v_ref, wv_ref, False)
-
-
-def project(hidden, gain, cosine, sine, w_q, w_k, w_v, requests, nodes, head_dim, group):
+            mixed = jnp.dot(probs[h].astype(jnp.bfloat16), old_v[h], preferred_element_type=jnp.float32)
+            mixed = mixed + jnp.dot(fresh_probs[h].astype(jnp.bfloat16), new[turn, 2, r, h], preferred_element_type=jnp.float32)
+            out_ref[r, :, h * head_dim : (h + 1) * head_dim] = (mixed / totals[h]).astype(jnp.bfloat16)
+        return 0
+
+    @pl.when(g > 0)
+    def _():
+        lax.fori_loop(0, group, attend, 0, unroll=2)
+
+    @pl.when(g == count)
+    def _():
+        for copy in cache_out:
+            copy.wait()
+
+        def put(b, _):
+            for i in range(window):
+                block = table_ref[b, first_page(b) + i]
+                pltpu.make_async_copy(fixed.at[0, b, i], ko_ref.at[block], psem).start()
+                pltpu.make_async_copy(fixed.at[1, b, i], vo_ref.at[block], psem).start()
+            return 0
+
+        lax.fori_loop(0, group * count, put, 0)
+        pltpu.make_async_copy(fixed, fixed, psem).wait()
+
+
+def front_stage(table, ctx_len, hidden, gain, cosine, sine, tree_mask, w_q, w_k, w_v, k_cache, v_cache, group):
+    requests, nodes, _ = tree_mask.shape
     rows, dim = hidden.shape
+    _, heads, page, head_dim = k_cache.shape
     cols = w_q.shape[1]
-    heads = cols // head_dim
     block = group * nodes
-    full = pl.BlockSpec((dim, cols), lambda i: (0, 0), pipeline_mode=pl.Buffered(1))
-    out = pl.BlockSpec((group, heads, nodes, head_dim), lambda i: (i, 0, 0, 0))
-    shape = jax.ShapeDtypeStruct((requests, heads, nodes, head_dim), jnp.bfloat16)
-    return pl.pallas_call(
-        qkv_kernel,
-        grid=(rows // block,),
-        in_specs=[
-            pl.BlockSpec((block, dim), lambda i: (i, 0)),
-            pl.BlockSpec((dim,), lambda i: (0,)),
-            pl.BlockSpec((block, head_dim), lambda i: (i, 0)),
-            pl.BlockSpec((block, head_dim), lambda i: (i, 0)),
-            full,
-            full,
-            full,
-        ],
-        out_specs=[out, out, out],
-        out_shape=[shape, shape, shape],
-        compiler_params=pltpu.CompilerParams(vmem_limit_bytes=VMEM_MAX),
-        name="project",
-    )(hidden, gain, cosine, sine, w_q, w_k, w_v)
-
-
-def attend_kernel(table_ref, ctx_ref, q_ref, kn_ref, vn_ref, mask_ref, kc_ref, vc_ref, out_ref, ko_ref, vo_ref, kbuf, vbuf, rsem, wsem):
-    b = pl.program_id(0)
-    count = pl.num_programs(0)
-    pages, heads, page, head_dim = kbuf.shape[1:]
-    span = pages * page
-    nodes = q_ref.shape[2]
-    window = nodes + page
-
-    def load(i, slot):
-        for s in range(pages):
-            block = table_ref[i, s]
-            pltpu.make_async_copy(kc_ref.at[block], kbuf.at[slot, s], rsem.at[0, slot]).start()
-            pltpu.make_async_copy(vc_ref.at[block], vbuf.at[slot, s], rsem.at[1, slot]).start()
-
-    def save(i, slot):
-        for s in range(pages):
-            block = table_ref[i, s]
-            pltpu.make_async_copy(kbuf.at[slot, s], ko_ref.at[block], wsem.at[0, slot]).start()
-            pltpu.make_async_copy(vbuf.at[slot, s], vo_ref.at[block], wsem.at[1, slot]).start()
-
-    def whole(slot, sem):
-        pltpu.make_async_copy(kbuf.at[slot], kbuf.at[slot], sem.at[0, slot]).wait()
-        pltpu.make_async_copy(vbuf.at[slot], vbuf.at[slot], sem.at[1, slot]).wait()
-
-    slot = lax.rem(b, 3)
-    after = lax.rem(b + 1, 3)
-
-    @pl.when(b == 0)
-    def _():
-        load(0, 0)
-
-    @pl.when(b >= 2)
-    def _():
-        whole(after, wsem)
-
-    whole(slot, rsem)
-    load(jnp.minimum(b + 1, count - 1), after)
-    ctx = ctx_ref[b]
-    first = jnp.minimum(ctx // page, pages - window // page)
-    base = first * page
-    row = base + lax.broadcasted_iota(jnp.int32, (window, nodes), 0)
-    node = ctx + lax.broadcasted_iota(jnp.int32, (window, nodes), 1)
-    place = jnp.where(row == node, 1.0, 0.0).astype(jnp.bfloat16)
-    slot_id = base + lax.broadcasted_iota(jnp.int32, (window, head_dim), 0)
-    fresh = (slot_id >= ctx) & (slot_id < ctx + nodes)
-    for buf, new_ref in ((kbuf, kn_ref), (vbuf, vn_ref)):
-        moved = [jnp.dot(place, new_ref[0, h], preferred_element_type=jnp.float32) for h in range(heads)]
-        for h in range(heads):
-            for i in range(window // page):
-                rows = slice(i * page, (i + 1) * page)
-                old = buf[slot, first + i, h].astype(jnp.float32)
-                buf[slot, first + i, h] = jnp.where(fresh[rows], moved[h][rows], old).astype(jnp.bfloat16)
-    save(b, slot)
-    spread = jnp.where(
-        ctx + lax.broadcasted_iota(jnp.int32, (nodes, span), 0) == lax.broadcasted_iota(jnp.int32, (nodes, span), 1), 1.0, 0.0
-    ).astype(jnp.bfloat16)
-    linked = jnp.where(mask_ref[0] > 0, 1.0, 0.0).astype(jnp.bfloat16)
-    seen_new = jnp.dot(linked, spread, preferred_element_type=jnp.float32) > 0.5
-    seen = seen_new | (lax.broadcasted_iota(jnp.int32, (nodes, span), 1) < ctx)
-    scale = head_dim**-0.5
-    scores = [dot_nt(q_ref[0, h], kbuf[slot, :, h].reshape(span, head_dim)) for h in range(heads)]
-    scores = [jnp.where(seen, score * scale, -jnp.inf) for score in scores]
-    tops = [jnp.max(score, axis=-1, keepdims=True) for score in scores]
-    probs = [jnp.exp(score - top) for score, top in zip(scores, tops)]
-    totals = [jnp.sum(prob, axis=-1, keepdims=True) for prob in probs]
-    mixed = [
-        jnp.dot(prob.astype(jnp.bfloat16), vbuf[slot, :, h].reshape(span, head_dim), preferred_element_type=jnp.float32)
-        for h, prob in enumerate(probs)
-    ]
-    for h in range(heads):
-        out_ref[:, h * head_dim : (h + 1) * head_dim] = (mixed[h] / totals[h]).astype(jnp.bfloat16)
-
-    @pl.when(b == count - 1)
-    def _():
-        whole(lax.rem(b + 2, 3), wsem)
-        whole(slot, wsem)
-        whole(after, rsem)
-
-
-def attend(table, ctx_len, query, key_new, val_new, tree_mask, k_cache, v_cache):
-    requests, heads, nodes, head_dim = query.shape
-    page = k_cache.shape[2]
-    pages = table.shape[1]
-    node_spec = pl.BlockSpec((1, heads, nodes, head_dim), lambda b, *_: (b, 0, 0, 0))
+    last = requests // group - 1
     anywhere = pl.BlockSpec(memory_space=pl.ANY)
     return pl.pallas_call(
-        attend_kernel,
+        front_kernel,
         grid_spec=pltpu.PrefetchScalarGridSpec(
             num_scalar_prefetch=2,
-            grid=(requests,),
+            grid=(requests // group + 1,),
             in_specs=[
-                node_spec,
-                node_spec,
-                node_spec,
-                pl.BlockSpec((1, nodes, nodes), lambda b, *_: (b, 0, 0)),
-                anywhere,
-                anywhere,
-            ],
-            out_specs=[pl.BlockSpec((nodes, heads * head_dim), lambda b, *_: (b, 0)), anywhere, anywhere],
+                pl.BlockSpec((block, dim), lambda i, *_: (jnp.minimum(i, last), 0)),
+                pl.BlockSpec((dim,), lambda i, *_: (0,)),
+                pl.BlockSpec((block, head_dim), lambda i, *_: (jnp.minimum(i, last), 0)),
+                pl.BlockSpec((block, head_dim), lambda i, *_: (jnp.minimum(i, last), 0)),
+                pl.BlockSpec((group, nodes, nodes), lambda i, *_: (jnp.maximum(i - 1, 0), 0, 0)),
+            ]
+            + [anywhere] * 5,
+            out_specs=[pl.BlockSpec((group, nodes, cols), lambda i, *_: (jnp.maximum(i - 1, 0), 0, 0)), anywhere, anywhere],
             scratch_shapes=[
-                pltpu.VMEM((3, pages, heads, page, head_dim), jnp.bfloat16),
-                pltpu.VMEM((3, pages, heads, page, head_dim), jnp.bfloat16),
-                pltpu.SemaphoreType.DMA((2, 3)),
-                pltpu.SemaphoreType.DMA((2, 3)),
+                pltpu.VMEM((3, dim, cols), jnp.bfloat16),
+                pltpu.VMEM((block, dim), jnp.bfloat16),
+                pltpu.VMEM((2, 3, group, heads, nodes, head_dim), jnp.bfloat16),
+                pltpu.VMEM(k_cache.shape, jnp.bfloat16),
+                pltpu.VMEM(v_cache.shape, jnp.bfloat16),
+                pltpu.VMEM((2, requests, nodes // page + 1, heads, page, head_dim), jnp.bfloat16),
+                pltpu.SemaphoreType.DMA((3,)),
+                pltpu.SemaphoreType.DMA((2, 8)),
+                pltpu.SemaphoreType.DMA((2, 8)),
+                pltpu.SemaphoreType.DMA,
             ],
         ),
         out_shape=[
-            jax.ShapeDtypeStruct((requests * nodes, heads * head_dim), jnp.bfloat16),
+            jax.ShapeDtypeStruct((requests, nodes, cols), jnp.bfloat16),
             jax.ShapeDtypeStruct(k_cache.shape, k_cache.dtype),
             jax.ShapeDtypeStruct(v_cache.shape, v_cache.dtype),
         ],
-        name="attend",
-    )(table, ctx_len, query, key_new, val_new, tree_mask, k_cache, v_cache)
+        compiler_params=pltpu.CompilerParams(vmem_limit_bytes=VMEM_MAX),
+        name="front_stage",
+    )(table, ctx_len, hidden, gain, cosine, sine, tree_mask, w_q, w_k, w_v, k_cache, v_cache)
 
 
 TILE = 512
@@ -630,10 +628,10 @@
         rows = requests * nodes
         flat = hidden.reshape(rows, dim)
         cosine, sine = rope_tables((ctx_len[:, None] + depth).reshape(rows), head_dim)
-        query, key_new, val_new = project(flat, attn_norm, cosine, sine, w_q, w_k, w_v, requests, nodes, head_dim, 4)
-        attended, k_out, v_out = attend(
-            block_table, ctx_len, query, key_new, val_new, tree_mask, jnp.transpose(k_cache, (0, 2, 1, 3)), jnp.transpose(v_cache, (0, 2, 1, 3))
-        )
+        old_k = jnp.transpose(k_cache, (0, 2, 1, 3))
+        old_v = jnp.transpose(v_cache, (0, 2, 1, 3))
+        attended, k_out, v_out = front_stage(block_table, ctx_len, flat, attn_norm, cosine, sine, tree_mask, w_q, w_k, w_v, old_k, old_v, 4)
+        attended = attended.reshape(rows, w_q.shape[1])
         k_out = jnp.transpose(k_out, (0, 2, 1, 3))
         v_out = jnp.transpose(v_out, (0, 2, 1, 3))
 

time: 291 us -> 283 us (0.973)
  Pallas kernels: 282 us -> 275 us
    pallas_call x2 -> x1, Pallas kernels: 60.2 us -> 53.3 us  [front_stage(): pl.pallas_call(front_kernel, grid_spec=pltpu.PrefetchScalarGridSpec(num_s...]
where the time goes in v6:
time: 283 us; the launch traced here: 282 us
  Pallas kernels  275 us (97%)
  other arithmetic  3.86 us (1%)
    pallas_call x1, Pallas kernels, tail_stage(): pl.pallas_call(tail_kernel, in_specs=[vmem] * 3 + [anywhere] * 7, out_spe...  222 us
    pallas_call x1, Pallas kernels, front_stage(): pl.pallas_call(front_kernel, grid_spec=pltpu.PrefetchScalarGridSpec(num_s...  53.3 us

profile of v6, /device:TPU:0, one launch (start us, length us, event | category | flops | bytes accessed | tf_op | source)
XLA Modules:
  0.0 282.2 jit_solution(8292373496350268615)
XLA Ops:
  0.6 0.8 add_convert_fusion
  1.4 0.1 convert_element_type.18
  1.5 3.1 %fusion = (f32[1024,128]{1,0:T(8,128)}, f32[1024,128]{1,0:T(8,128)}) fusion(f32[128]{0:T(128)S(1)} %get-tuple-element.16, f32[128]{0:T(128)S(1)} %get-tuple-element.17, f32[1024]{0:T(1024)S(1)} %convert_element_type.18), kind=kLoop, calls=%fused_computation.2 | loop fusion | flops 262144 | bytes 1053696 | tf_op jit(solution)/shard_map/mul | solution.py:621
  4.6 53.3 %front_stage.1 = (bf16[16,64,640]{2,1,0:T(8,128)(2,1)}, bf16[512,5,16,128]{3,2,1,0:T(8,128)(2,1)}, bf16[512,5,16,128]{3,2,1,0:T(8,128)(2,1)}) custom-call(s32[16,32]{1,0:T(8,128)} %table_ref.1, s32[16]{0:T(128)} %ctx_ref.1, bf16[1024,5120]{1,0:T(8,128)(2,1)} %bitcast.9, bf16[5120]{0:T(1024)(128)(2,1)} %gain_ref.1, f32[1024,128]{1,0:T(8,128)} %get-tuple-element.15.cos_ref, ...), custom_call_target="tpu_custom_call" | custom-call | tf_op jit(solution)/shard_map/front_stage/pallas_call | solution.py:144
  57.9 221.7 %tail_stage.1 = (f32[16,64]{1,0:T(8,128)}, f32[16,64]{1,0:T(8,128)}) custom-call(bf16[5120]{0:T(1024)(128)(2,1)} %mlp_gain.1, bf16[5120]{0:T(1024)(128)(2,1)} %final_gain.1, s32[16,64]{1,0:T(8,128)} %id_ref.1, bf16[1024,640]{1,0:T(8,128)(2,1)} %bitcast.16, bf16[1024,5120]{1,0:T(8,128)(2,1)} %bitcast.10, bf16[640,5120]{1,0:T(8,128)(2,1)} %wo_hbm.1, ...), custom_call_target="tpu_custom_call" | custom-call | tf_op jit(solution)/shard_map/tail_stage/pallas_call | solution.py:581
  279.6 1.3 copy.25
  280.9 1.3 copy.26
  (1 shorter events, 0.0 us)

commit v7 on v6

--- a/solution.py
+++ b/solution.py
@@ -37,6 +37,7 @@
     def _():
         weight(0).start()
         weight(1).start()
+        weight(2).start()
 
     @pl.when(g < count)
     def _():
@@ -49,8 +50,6 @@
             @pl.when(g == 0)
             def _():
                 weight(n).wait()
-                if n == 0:
-                    weight(2).start()
                 if n == 2:
                     for copy in cache_in:
                         copy.start()
@@ -115,7 +114,7 @@
 
     @pl.when(g > 0)
     def _():
-        lax.fori_loop(0, group, attend, 0, unroll=2)
+        lax.fori_loop(0, group, attend, 0, unroll=4)
 
     @pl.when(g == count)
     def _():
@@ -370,7 +369,7 @@
     lax.fori_loop(start, stop, body, 0)
 
 
-def tail_kernel(mlp_gain, final_gain, id_ref, att_hbm, hid_hbm, wo_hbm, wg_hbm, wu_hbm, wd_hbm, wl_hbm, norm_ref, prob_ref, mbuf, r1, rx, ry, r2x, r2y, ssq, left, prod, resid, h_buf, wbuf, nbuf, acc, stats, ssem, rsem, wsem, nsem, isem, tsem, usem, free):
+def tail_kernel(mlp_gain, final_gain, id_ref, att_hbm, hid_hbm, wo_hbm, wg_hbm, wu_hbm, wd_hbm, wl_hbm, out_ref, mbuf, r1, rx, ry, r2x, r2y, ssq, left, prod, resid, h_buf, wbuf, nbuf, acc, stats, ssem, rsem, wsem, nsem, isem, tsem, usem, free):
     me, blocks = seat()
     steps = mbuf.shape[0]
     tiles = steps // 2
@@ -565,8 +564,8 @@
         whole = whole + stats[d, 1] * jnp.exp(stats[d, 0] - top)
         score = score + stats[d, 2]
     norm = top + jnp.log(whole)
-    norm_ref[...] = norm
-    prob_ref[...] = score - norm
+    out_ref[0] = norm
+    out_ref[1] = score - norm
 
 
 def tail_stage(mlp_gain, final_gain, score_id, attended, hidden, w_o, gate_t, up_t, w_down, head_t):
@@ -581,8 +580,8 @@
     return pl.pallas_call(
         tail_kernel,
         in_specs=[vmem] * 3 + [anywhere] * 7,
-        out_specs=[vmem, vmem],
-        out_shape=[jax.ShapeDtypeStruct(score_id.shape, jnp.float32)] * 2,
+        out_specs=vmem,
+        out_shape=jax.ShapeDtypeStruct((2,) + score_id.shape, jnp.float32),
         scratch_shapes=[
             pltpu.VMEM((steps, 2, 2, 2, rows, TILE), bf16),
             pltpu.VMEM((steps, 2, 2, rows, TILE), bf16),
@@ -635,8 +634,8 @@
         k_out = jnp.transpose(k_out, (0, 2, 1, 3))
         v_out = jnp.transpose(v_out, (0, 2, 1, 3))
 
-        log_norm, log_prob = tail_stage(mlp_norm, final_norm, score_id, attended, flat, w_o, w_gate.T, w_up.T, w_down, w_lm.T)
-        return log_norm.reshape(requests, nodes), log_prob.reshape(requests, nodes), k_out, v_out
+        scores = tail_stage(mlp_norm, final_norm, score_id, attended, flat, w_o, w_gate.T, w_up.T, w_down, w_lm.T)
+        return scores[0], scores[1], k_out, v_out
 
     request_spec = P("dp", None, None)
     node_spec = P("dp", None)

time: 283 us -> 281 us (level)
  no operation moved by 1% of the time
where the time goes in v7:
time: 281 us; the launch traced here: 280 us
  Pallas kernels  274 us (98%)
  other arithmetic  3.86 us (1%)
    pallas_call x1, Pallas kernels, tail_stage(): pl.pallas_call(tail_kernel, in_specs=[vmem] * 3 + [anywhere] * 7, out_spe...  222 us
    pallas_call x1, Pallas kernels, front_stage(): pl.pallas_call(front_kernel, grid_spec=pltpu.PrefetchScalarGridSpec(num_s...  52.8 us

profile of v7, /device:TPU:0, one launch (start us, length us, event | category | flops | bytes accessed | tf_op | source)
XLA Modules:
  0.0 280.4 jit_solution(4367237970017719324)
XLA Ops:
  0.6 0.8 add_convert_fusion
  1.4 0.1 convert_element_type.18
  1.5 3.1 %fusion = (f32[1024,128]{1,0:T(8,128)}, f32[1024,128]{1,0:T(8,128)}) fusion(f32[128]{0:T(128)S(1)} %get-tuple-element.14, f32[128]{0:T(128)S(1)} %get-tuple-element.15, f32[1024]{0:T(1024)S(1)} %convert_element_type.18), kind=kLoop, calls=%fused_computation.2 | loop fusion | flops 262144 | bytes 1053696 | tf_op jit(solution)/shard_map/mul | solution.py:620
  4.6 52.8 %front_stage.1 = (bf16[16,64,640]{2,1,0:T(8,128)(2,1)}, bf16[512,5,16,128]{3,2,1,0:T(8,128)(2,1)}, bf16[512,5,16,128]{3,2,1,0:T(8,128)(2,1)}) custom-call(s32[16,32]{1,0:T(8,128)} %table_ref.1, s32[16]{0:T(128)} %ctx_ref.1, bf16[1024,5120]{1,0:T(8,128)(2,1)} %bitcast.13, bf16[5120]{0:T(1024)(128)(2,1)} %gain_ref.1, f32[1024,128]{1,0:T(8,128)} %get-tuple-element.13.cos_ref, ...), custom_call_target="tpu_custom_call" | custom-call | tf_op jit(solution)/shard_map/front_stage/pallas_call | solution.py:143
  57.4 221.7 %tail_stage.1 = f32[2,16,64]{2,1,0:T(8,128)} custom-call(bf16[5120]{0:T(1024)(128)(2,1)} %mlp_gain.1, bf16[5120]{0:T(1024)(128)(2,1)} %final_gain.1, s32[16,64]{1,0:T(8,128)} %id_ref.1, bf16[1024,640]{1,0:T(8,128)(2,1)} %bitcast.20, bf16[1024,5120]{1,0:T(8,128)(2,1)} %bitcast.14, bf16[640,5120]{1,0:T(8,128)(2,1)} %wo_hbm.1, bf16[1728,5120]{1,0:T(8,128)(2,1)} %bitcast.16, ...), custom_call_target="tpu_custom_call" | custom-call | tf_op jit(solution)/shard_map/tail_stage/pallas_call | solution.py:580
  279.0 1.3 slice_bitcast_fusion
  (1 shorter events, 0.0 us)
